TPU v7x, 32 devices: a whole 2x2x4 slice. The times are simulated.
32 devices in a mesh: dp: 2 (over x), tp: 4 (over z), cp: 4 (over y, core).
Axes of the slice: x: 2, y: 2, z: 4, core: 2. Of those that a mesh axis runs over, the one named last changes fastest.
Arguments:
- hidden_in: bfloat16 [8, 1024, 2048], P('dp'), parts along dimension 0
- lengths: int32 [8], P('dp'), parts along dimension 0
- k_cache: bfloat16 [8, 16, 4096, 128], P('dp', 'tp', 'cp'), parts along dimension 0
- v_cache: bfloat16 [8, 16, 4096, 128], P('dp', 'tp', 'cp'), parts along dimension 0
- ln1_gain: float32 [2048], replicated
- ln1_bias: float32 [2048], replicated
- ln2_gain: float32 [2048], replicated
- ln2_bias: float32 [2048], replicated
- w_qkv: bfloat16 [2048, 6144], P(None, 'tp')
- b_qkv: bfloat16 [6144], P('tp')
- w_out: bfloat16 [2048, 2048], P('tp')
- b_out: bfloat16 [2048], replicated
- w_up: bfloat16 [2048, 8192], P(None, 'tp')
- b_up: bfloat16 [8192], P('tp')
- w_down: bfloat16 [8192, 2048], P('tp')
- b_down: bfloat16 [2048], replicated
Outputs:
- output 1: bfloat16 [8, 1024, 2048], P('dp'), parts along dimension 0
- output 2: bfloat16 [8, 16, 1024, 128], P('dp', 'tp'), parts along dimension 0
- output 3: bfloat16 [8, 16, 1024, 128], P('dp', 'tp'), parts along dimension 0
There are 2 independent parts. A program takes and returns all parts, laid end to end along the dimension named above; an argument that names none is the same for every part.
All inputs are finite; a program needn't handle non-finite values.
Results may differ from a plain program's by a relative error of at most 0.00418695.
Values sent between devices are 32-bit elements.
A program may use at most 1 GiB of HBM per device.

v0:
```python
import jax
import jax.numpy as jnp
from jax import lax
from jax.sharding import PartitionSpec as P

EPSILON = 1e-5
NEG_BIG = -1e30
ROTARY_SHARE = 4
ROPE_BASE = 10000.0


def layer_norm(values_in, gain_vec, bias_vec):
    x_f32 = values_in.astype(jnp.float32)
    row_mean = jnp.mean(x_f32, axis=-1, keepdims=True)
    centered = x_f32 - row_mean
    variance = jnp.mean(centered * centered, axis=-1, keepdims=True)
    return (centered * lax.rsqrt(variance + EPSILON) * gain_vec + bias_vec).astype(jnp.bfloat16)


def rotary(values_in, positions):
    head_dim = values_in.shape[-1]
    rot_dim = head_dim // ROTARY_SHARE
    half_rot = rot_dim // 2
    inv_freq = ROPE_BASE ** (-2.0 * jnp.arange(half_rot, dtype=jnp.float32) / rot_dim)
    angles = positions.astype(jnp.float32)[..., None] * inv_freq
    cos_tab = jnp.cos(angles)[..., None, :]
    sin_tab = jnp.sin(angles)[..., None, :]
    rot_first = values_in[..., :half_rot].astype(jnp.float32)
    rot_second = values_in[..., half_rot:rot_dim].astype(jnp.float32)
    new_first = rot_first * cos_tab - rot_second * sin_tab
    new_second = rot_second * cos_tab + rot_first * sin_tab
    return jnp.concatenate([new_first.astype(jnp.bfloat16), new_second.astype(jnp.bfloat16), values_in[..., rot_dim:]], axis=-1)


def cache_piece(q_rot, k_slots, v_slots, slot_ids, lengths):
    head_dim = q_rot.shape[3]
    slot_valid = (slot_ids[None, :] < lengths[:, None])[:, None, None, :]
    scores = jnp.einsum("bchd,bhsd->bhcs", q_rot, k_slots, preferred_element_type=jnp.float32) * head_dim ** -0.5
    scores = jnp.where(slot_valid, scores, NEG_BIG)
    piece_max = scores.max(axis=-1)
    probs = jnp.where(slot_valid, jnp.exp(scores - piece_max[..., None]), 0.0)
    piece_out = jnp.einsum("bhcs,bhsd->bhcd", probs.astype(jnp.bfloat16), v_slots, preferred_element_type=jnp.float32)
    return piece_max, probs.sum(axis=-1), piece_out


def self_piece(q_chunk, k_chunk, v_chunk):
    chunk_len = q_chunk.shape[1]
    head_dim = q_chunk.shape[3]
    causal = jnp.arange(chunk_len)[:, None] >= jnp.arange(chunk_len)[None, :]
    scores = jnp.einsum("bchd,bkhd->bhck", q_chunk, k_chunk, preferred_element_type=jnp.float32) * head_dim ** -0.5
    scores = jnp.where(causal, scores, NEG_BIG)
    piece_max = scores.max(axis=-1)
    probs = jnp.where(causal, jnp.exp(scores - piece_max[..., None]), 0.0)
    piece_out = jnp.einsum("bhck,bkhd->bhcd", probs.astype(jnp.bfloat16), v_chunk, preferred_element_type=jnp.float32)
    return piece_max, probs.sum(axis=-1), piece_out


def empty_piece(q_chunk, k_chunk, v_chunk):
    num_rows, chunk_len, heads_here, head_dim = q_chunk.shape
    stat_shape = (num_rows, heads_here, chunk_len)
    return (jnp.full(stat_shape, NEG_BIG, jnp.float32), jnp.zeros(stat_shape, jnp.float32), jnp.zeros(stat_shape + (head_dim,), jnp.float32))


def solution(mesh):
    in_specs = (P("dp", None, None), P("dp"), P("dp", "tp", "cp", None), P("dp", "tp", "cp", None), P(), P(), P(), P(), P(None, "tp"), P("tp"), P("tp", None), P(), P(None, "tp"), P("tp"), P("tp", None), P())
    out_specs = (P("dp", None, None), P("dp", "tp", None, None), P("dp", "tp", None, None))

    def local_layer(hidden_in, lengths, k_block, v_block, ln1_gain, ln1_bias, ln2_gain, ln2_bias, w_qkv, b_qkv, w_out, b_out, w_up, b_up, w_down, b_down):
        num_rows, chunk_len, d_model = hidden_in.shape
        heads_here = k_block.shape[1]
        block_len = k_block.shape[2]
        head_dim = k_block.shape[3]
        cp_index = lax.axis_index("cp")
        normed_attn = layer_norm(hidden_in, ln1_gain, ln1_bias)
        normed_mlp = layer_norm(hidden_in, ln2_gain, ln2_bias)
        qkv_all = (jnp.einsum("bcd,de->bce", normed_attn, w_qkv, preferred_element_type=jnp.float32) + b_qkv.astype(jnp.float32)).astype(jnp.bfloat16)
        qkv_all = qkv_all.reshape(num_rows, chunk_len, heads_here, 3, head_dim)
        positions = lengths[:, None] + jnp.arange(chunk_len, dtype=jnp.int32)[None, :]
        q_rot = rotary(qkv_all[:, :, :, 0], positions)
        k_rot = rotary(qkv_all[:, :, :, 1], positions)
        v_chunk = qkv_all[:, :, :, 2]
        slot_ids = cp_index * block_len + jnp.arange(block_len, dtype=jnp.int32)
        cache_max, cache_sum, cache_out = cache_piece(q_rot, k_block, v_block, slot_ids, lengths)
        own_max, own_sum, own_out = lax.cond(cp_index == 0, self_piece, empty_piece, q_rot, k_rot, v_chunk)
        global_max = lax.pmax(jnp.maximum(cache_max, own_max), "cp")
        cache_weight = jnp.exp(cache_max - global_max)
        own_weight = jnp.exp(own_max - global_max)
        out_part = cache_out * cache_weight[..., None] + own_out * own_weight[..., None]
        sum_part = cache_sum * cache_weight + own_sum * own_weight
        out_total, sum_total = lax.psum((out_part, sum_part), "cp")
        context = (out_total / sum_total[..., None]).astype(jnp.bfloat16)
        attn_part = jnp.einsum("bhcd,hde->bce", context, w_out.reshape(heads_here, head_dim, d_model), preferred_element_type=jnp.float32)
        hidden = jax.nn.gelu(jnp.einsum("bcd,df->bcf", normed_mlp, w_up, preferred_element_type=jnp.float32) + b_up.astype(jnp.float32), approximate=False).astype(jnp.bfloat16)
        mlp_part = jnp.einsum("bcf,fd->bcd", hidden, w_down, preferred_element_type=jnp.float32)
        branch_sum = lax.psum(attn_part + mlp_part, "tp")
        out_sum = hidden_in.astype(jnp.float32) + branch_sum + b_out.astype(jnp.float32) + b_down.astype(jnp.float32)
        return out_sum.astype(jnp.bfloat16), jnp.swapaxes(k_rot, 1, 2), jnp.swapaxes(v_chunk, 1, 2)

    return jax.shard_map(local_layer, mesh=mesh, in_specs=in_specs, out_specs=out_specs, check_vma=False)
```

profile of v0, /device:TPU:0, one launch (start us, length us, event | category | flops | bytes accessed | tf_op | source)
XLA Modules:
  0.0 1712.7 jit_solution(10404884710317990720)
XLA Ops:
  7.2 0.0 copy-start
  7.2 0.0 copy-start.8
  7.2 0.0 copy-start.14
  7.2 0.0 copy-start.13
  7.2 0.0 all-reduce.5.cloned.1.call-start
  7.3 0.0 slice-start
  7.3 0.0 slice-start.1
  7.3 8.9 convert_reduce_fusion
  16.2 0.0 copy-start.4
  16.2 0.0 slice-start.2
  16.2 0.0 slice-start.3
  16.3 9.4 fusion.20
  25.7 0.0 copy-done.8
  25.7 0.0 copy-start.6
  25.7 0.0 copy-done.4
  25.7 0.6 copy-done.6
  26.3 0.0 copy-done.14
  26.3 0.0 copy-done.13
  26.3 0.0 slice-done
  26.4 36.6 %add_convert_fusion = bf16[4,1024,1536]{2,1,0:T(8,128)(2,1)} fusion(bf16[4,1024,2048]{2,1,0:T(8,128)(2,1)S(1)} %bitcast.52, f32[2048]{0:T(1024)S(1)} %copy-done.13, f32[2048]{0:T(1024)S(1)} %copy-done.14, f32[4,1024]{1,0:T(4,128)S(1)} %add_rsqrt_fusion, f32[4,1024]{1,0:T(4,128)S(1)} %broadcast_multiply_fusion, f32[1536]{0:T(1024)S(1)} %convert_element_type.78, ...), kind=kOutput, calls=%fused_computation.56 | convolution fusion | flops 25832718336 | bytes 35706880 | tf_op jit(solution)/shard_map/bcd,de->bce/dot_general | solution.py:76
  63.0 16.6 copy.30
  79.6 22.6 %slice_bitcast_fusion.2 = (bf16[4,4,1024,128]{2,3,1,0:T(8,128)(2,1)}, bf16[4,1024,4,128]{1,3,2,0:T(8,128)(2,1)S(1)}, bf16[4,1024,4,128]{1,3,2,0:T(8,128)(2,1)}, bf16[4,1024,4,128]{1,3,2,0:T(8,128)(2,1)S(1)}) fusion(bf16[4,1024,4,3,128]{1,4,3,2,0:T(8,128)(2,1)} %bitcast.53), kind=kLoop, calls=%fused_computation.112 | loop fusion | bytes 29360128 | tf_op jit(solution)/shard_map/transpose | solution.py:97
  102.3 0.0 copy-start.2
  102.3 0.0 copy-start.3
  102.3 0.1 add_convert_fusion.1
  102.4 1.9 copy-done.2
  104.3 2.4 slice.39
  106.6 0.0 copy-done.3
  106.6 2.1 slice.43
  108.7 0.1 broadcast_compare_fusion
  108.8 1.0 multiply_cosine_fusion
  109.8 3.2 fusion.95
  113.0 27.7 %fusion.9 = (f32[4,4,1024]{2,1,0:T(4,128)S(1)}, f32[4,4,1024,1024]{2,3,1,0:T(8,128)}) fusion(pred[4,1024]{1,0:T(4,128)(4,1)S(1)} %broadcast_compare_fusion, bf16[4,4,1024,128]{3,2,1,0:T(8,128)(2,1)} %param.20, bf16[4,1024,4,96]{1,3,2,0:T(8,128)(2,1)} %slice.39, bf16[4,1024,4,16]{1,3,2,0:T(8,128)(2,1)} %get-tuple-element.49, ...), kind=kOutput, calls=%fused_computation.13 | convolution fusion | flops 4357865472 | bytes 75567104 | tf_op jit(solution)/shard_map/bchd,bhsd->bhcs/dot_general | solution.py:38
  140.7 7.0 fusion.132
  147.7 81.5 %conditional.1 = (f32[4,4,1024]{2,1,0:T(4,128)}, f32[4,4,1024]{2,1,0:T(4,128)S(1)}, f32[4,4,1024,128]{3,2,1,0:T(8,128)}) conditional(s32[]{:T(128)} %convert_element_type.86, () %tuple.16, (bf16[4,1024,4,128]{1,3,2,0:T(8,128)(2,1)}, bf16[4,1024,4,128]{1,3,2,0:T(8,128)(2,1)}, bf16[4,1024,4,128]{1,3,2,0:T(8,128)(2,1)}) %tuple.17), branch_computations={%region_3.0_spmd, %region_4.7_spmd} | conditional | flops 8809054208 | bytes 226754592 | solution.py:84
  147.7 0.3 iota_compare_fusion
  148.0 27.8 %fusion = (f32[4,4,1024]{2,1,0:T(4,128)}, f32[4,4,1024,1024]{2,3,1,0:T(8,128)}) fusion(pred[1024,1024]{0,1:T(8,128)(4,1)S(1)} %iota_compare_fusion, bf16[4,1024,4,128]{1,3,2,0:T(8,128)(2,1)} %get-tuple-element.24, bf16[4,1024,4,128]{1,3,2,0:T(8,128)(2,1)} %get-tuple-element.25), kind=kOutput, calls=%fused_computation.2 | convolution fusion | flops 4345282560 | bytes 76611584 | tf_op jit(solution)/shard_map/cond/branch_1_fun/bchd,bkhd->bhck/dot_general | solution.py:50
  175.8 31.6 %fusion.3 = f32[4,4,1024,128]{3,2,1,0:T(8,128)} fusion(bf16[4,1024,4,128]{1,3,2,0:T(8,128)(2,1)} %get-tuple-element.26, f32[4,4,1024,1024]{2,3,1,0:T(8,128)} %get-tuple-element.38, f32[4,4,1024]{2,1,0:T(4,128)} %get-tuple-element.63, pred[1024,1024]{0,1:T(8,128)(4,1)S(1)} %iota_compare_fusion), kind=kOutput, calls=%fused_computation.5 | convolution fusion | flops 4378853376 | bytes 80805888 | tf_op jit(solution)/shard_map/cond/branch_1_fun/bhck,bkhd->bhcd/dot_general | solution.py:54
  207.4 21.8 %fusion.2 = f32[4,4,1024]{2,1,0:T(4,128)S(1)} fusion(f32[4,4,1024,1024]{2,3,1,0:T(8,128)} %get-tuple-element.38, f32[4,4,1024]{2,1,0:T(4,128)} %get-tuple-element.63, pred[1024,1024]{0,1:T(8,128)(4,1)S(1)} %iota_compare_fusion), kind=kLoop, calls=%fused_computation.4 | loop fusion | flops 83869696 | bytes 68288512 | tf_op jit(solution)/shard_map/cond/branch_1_fun/reduce_sum | solution.py:55
  229.2 1.5 max.5
  230.7 0.0 all-reduce.5.cloned.1.call-update
  230.7 0.0 all-reduce.9.cloned.1.call-start
  230.8 0.0 copy-start.9
  230.8 21.6 %fusion.10 = f32[4,4,1024]{2,1,0:T(4,128)S(1)} fusion(f32[4,4,1024,1024]{2,3,1,0:T(8,128)} %get-tuple-element.54, f32[4,4,1024]{2,1,0:T(4,128)S(1)} %get-tuple-element.53, pred[4,1024]{1,0:T(4,128)(4,1)S(1)} %broadcast_compare_fusion), kind=kLoop, calls=%fused_computation.18 | loop fusion | flops 83869696 | bytes 67244032 | tf_op jit(solution)/shard_map/reduce_sum | solution.py:43
  252.4 0.0 copy-done.9
  252.4 11.8 all-reduce.5.cloned.1.call-done
  264.2 1.5 multiply_add_fusion.1
  265.7 33.8 %multiply_add_fusion = f32[4,4,1024,128]{3,2,1,0:T(8,128)} fusion(f32[4,4,1024,128]{3,2,1,0:T(8,128)} %get-tuple-element.16, f32[4,4,1024]{2,1,0:T(4,128)S(1)} %bitcast.60, f32[4,4,1024]{2,1,0:T(4,128)S(1)} %bitcast.59, bf16[4,4,1024,128]{3,2,1,0:T(8,128)(2,1)} %param.21, f32[4,4,1024,1024]{2,3,1,0:T(8,128)} %get-tuple-element.54, ...), kind=kOutput, calls=%fused_computation.100 | convolution fusion | flops 4385144832 | bytes 88281088 | tf_op jit(solution)/shard_map/bhcs,bhsd->bhcd/dot_general | solution.py:42
  299.5 0.0 all-reduce.9.cloned.1.call-update
  299.5 0.3 all-reduce.7.cloned.1.call-start
  299.9 54.4 %fusion.82 = (u8[1024,2048]{1,0:T(8,128)(4,1)}, u8[1024,2048]{1,0:T(8,128)(4,1)}, f32[4,1024,2048]{2,1,0:T(8,128)}) fusion(f32[2048]{0:T(1024)S(1)} %convert_element_type.93, bf16[2048,2048]{1,0:T(8,128)(2,1)} %param.30, bf16[4,1024,2048]{2,1,0:T(8,128)(2,1)} %param.18, f32[2048]{0:T(1024)S(1)} %copy-done.15, f32[2048]{0:T(1024)S(1)} %copy-done.16, ...), kind=kOutput, calls=%fused_computation.102 | convolution fusion | flops 34523316224 | bytes 62971904 | tf_op jit(solution)/shard_map/bcd,df->bcf/dot_general | solution.py:93
  354.3 99.2 %all-reduce.9.cloned.1.call-done = (f32[4,4,1024,128]{3,2,1,0:T(8,128)}, f32[4,4,1024]{2,1,0:T(4,128)}) async-done(((f32[4,4,1024,128]{3,2,1,0:T(8,128)}, f32[4,4,1024]{2,1,0:T(4,128)}), (f32[4,4,1024,128]{3,2,1,0:T(8,128)}, f32[4,4,1024]{2,1,0:T(4,128)})) %all-reduce.9.cloned.1.call-update) | async-done | bytes 8454160 | tf_op jit(solution)/shard_map/psum | solution.py:90
  453.4 0.0 slice-start.5
  453.4 17.3 %fusion.84 = f32[4,1024,2048,1]{2,1,3,0:T(8,128)} fusion(bf16[4,128,2048,1]{2,1,0,3:T(8,128)(2,1)S(1)} %bitcast.50, f32[4,4,1024,128]{3,2,1,0:T(8,128)} %get-tuple-element.32, f32[4,4,1024]{2,1,0:T(4,128)} %get-tuple-element.33), kind=kOutput, calls=%fused_computation.104 | convolution fusion | flops 8594128896 | bytes 44105728 | tf_op jit(solution)/shard_map/bhcd,hde->bce/dot_general | solution.py:92
  470.8 0.0 slice-done.5
  470.8 112.8 %bitcast_add_fusion = f32[4,1024,2048]{2,1,0:T(8,128)} fusion(f32[4,1024,2048,1]{2,1,3,0:T(8,128)} %fusion.84, f32[4,1024,2048]{2,1,0:T(8,128)} %get-tuple-element.55, f32[2048]{0:T(1024)S(1)} %convert_element_type.93, bf16[2048,2048]{1,0:T(8,128)(2,1)S(1)} %bitcast.62, u8[1024,2048]{1,0:T(8,128)(4,1)S(1)} %copy-done.18, u8[1024,2048]{1,0:T(8,128)(4,1)S(1)} %copy-done.17), kind=kOutput, calls=%fused_computation.40 | convolution fusion | flops 34963718144 | bytes 113254400 | tf_op jit(solution)/shard_map/bcf,fd->bcd/dot_general | solution.py:94
  583.6 0.0 copy-start.11
  583.6 0.0 all-reduce.7.cloned.1.call-update
  583.6 0.6 copy-done.10
  584.3 0.0 copy-done.11
  584.3 6.2 copy.38
  590.5 6.3 copy.39
  596.8 1086.8 %all-reduce.7.cloned.1.call-done = f32[4,1024,2048]{2,1,0:T(8,128)} async-done(((f32[4,1024,2048]{2,1,0:T(8,128)}), f32[4,1024,2048]{2,1,0:T(8,128)}) %all-reduce.7.cloned.1.call-update) | async-done | bytes 33554448 | tf_op jit(solution)/shard_map/psum | solution.py:95
  1683.5 22.4 %fusion.23 = bf16[4,1024,2048]{2,1,0:T(8,128)(2,1)} fusion(f32[4,1024,2048]{2,1,0:T(8,128)} %all-reduce.7.cloned.1.call-done, bf16[4,1024,2048]{2,1,0:T(8,128)(2,1)} %param.18, f32[2048]{0:T(1024)S(1)} %convert_element_type.96, f32[2048]{0:T(1024)S(1)} %convert_element_type.95), kind=kLoop, calls=%fused_computation.31 | loop fusion | flops 41943040 | bytes 67125248 | tf_op jit(solution)/shard_map/convert_element_type | solution.py:97
  (33 shorter events, 0.1 us)
Async XLA Ops:
  7.2 446.3 %copy-start = (bf16[512,2048]{1,0:T(8,128)(2,1)S(1)}, bf16[512,2048]{1,0:T(8,128)(2,1)}, u32[]{:S(2)}) copy-start(bf16[512,2048]{1,0:T(8,128)(2,1)} %param.28) | copy-start | bytes 6291460
  7.2 18.5 %copy-start.8 = (bf16[1536]{0:T(1024)(128)(2,1)S(1)}, bf16[1536]{0:T(1024)(128)(2,1)}, u32[]{:S(2)}) copy-start(bf16[1536]{0:T(1024)(128)(2,1)} %param.27) | copy-start | bytes 9220
  7.2 19.1 %copy-start.14 = (f32[2048]{0:T(1024)S(1)}, f32[2048]{0:T(1024)}, u32[]{:S(2)}) copy-start(f32[2048]{0:T(1024)} %param.22) | copy-start | bytes 24580
  7.2 19.1 %copy-start.13 = (f32[2048]{0:T(1024)S(1)}, f32[2048]{0:T(1024)}, u32[]{:S(2)}) copy-start(f32[2048]{0:T(1024)} %param.23) | copy-start | bytes 24580
  7.2 256.9 %all-reduce.5.cloned.1.call-start = ((), (), s32[]{:S(2)}) async-start(), calls=%async_computation | async-start | bytes 131072 | tf_op jit(solution)/shard_map/pmax | solution.py:85
  7.3 19.1 %slice-start = ((s8[16777216]{0:T(1024)(128)(4,1)}), s8[4194304]{0:T(1024)(128)(4,1)S(1)}, s32[]{:S(2)}) async-start(s8[16777216]{0:T(1024)(128)(4,1)} %bitcast.51), calls=%async_computation.3 | async-start | bytes 8388608
  7.3 19.0 %slice-start.1 = ((s8[16777216]{0:T(1024)(128)(4,1)}), s8[4194304]{0:T(1024)(128)(4,1)S(1)}, s32[]{:S(2)}) async-start(s8[16777216]{0:T(1024)(128)(4,1)} %bitcast.51), calls=%async_computation.4 | async-start | bytes 8388608
  16.2 9.5 copy-start.4
  16.2 10.1 slice-start.2
  16.2 10.1 slice-start.3
  25.7 0.6 copy-start.6
  63.0 39.2 %copy-start.12 = (s32[4]{0:T(128)S(1)}, s32[4]{0:T(128)}, u32[]{:S(2)}) copy-start(s32[4]{0:T(128)} %param.19) | copy-start | bytes 52
  102.3 2.0 copy-start.2
  102.3 4.4 copy-start.3
  230.7 222.7 %all-reduce.9.cloned.1.call-start = ((), (), s32[]{:S(2)}) async-start(), calls=%async_computation.2 | async-start | bytes 16908288 | tf_op jit(solution)/shard_map/psum | solution.py:90
  230.8 21.6 %copy-start.9 = (bf16[2048]{0:T(1024)(128)(2,1)S(1)}, bf16[2048]{0:T(1024)(128)(2,1)}, u32[]{:S(2)}) copy-start(bf16[2048]{0:T(1024)(128)(2,1)} %param.31) | copy-start | bytes 12292
  265.7 34.2 %copy-start.5 = (f32[4,1024]{1,0:T(4,128)S(1)}, f32[4,1024]{1,0:T(4,128)}, u32[]{:S(2)}) copy-start(f32[4,1024]{1,0:T(4,128)} %copy-done.4) | copy-start | bytes 49156
  265.7 34.2 %copy-start.7 = (f32[4,1024]{1,0:T(4,128)S(1)}, f32[4,1024]{1,0:T(4,128)}, u32[]{:S(2)}) copy-start(f32[4,1024]{1,0:T(4,128)} %copy-done.6) | copy-start | bytes 49156
  265.7 34.2 %copy-start.15 = (f32[2048]{0:T(1024)S(1)}, f32[2048]{0:T(1024)}, u32[]{:S(2)}) copy-start(f32[2048]{0:T(1024)} %param.25) | copy-start | bytes 24580
  265.7 34.2 %copy-start.16 = (f32[2048]{0:T(1024)S(1)}, f32[2048]{0:T(1024)}, u32[]{:S(2)}) copy-start(f32[2048]{0:T(1024)} %param.24) | copy-start | bytes 24580
  299.5 1384.0 %all-reduce.7.cloned.1.call-start = ((), (), s32[]{:S(2)}) async-start(), calls=%async_computation.1 | async-start | bytes 67108864 | tf_op jit(solution)/shard_map/psum | solution.py:95
  453.4 17.4 %slice-start.4 = ((s8[8388608]{0:T(1024)(128)(4,1)}), s8[4194304]{0:T(1024)(128)(4,1)S(1)}, s32[]{:S(2)}) async-start(s8[8388608]{0:T(1024)(128)(4,1)} %bitcast.61), calls=%async_computation.7 | async-start | bytes 8388608
  453.4 17.4 %copy-start.17 = (u8[1024,2048]{1,0:T(8,128)(4,1)S(1)}, u8[1024,2048]{1,0:T(8,128)(4,1)}, u32[]{:S(2)}) copy-start(u8[1024,2048]{1,0:T(8,128)(4,1)} %get-tuple-element.30) | copy-start | bytes 6291460
  453.4 17.4 %copy-start.18 = (u8[1024,2048]{1,0:T(8,128)(4,1)S(1)}, u8[1024,2048]{1,0:T(8,128)(4,1)}, u32[]{:S(2)}) copy-start(u8[1024,2048]{1,0:T(8,128)(4,1)} %get-tuple-element.31) | copy-start | bytes 6291460
  453.4 17.4 %slice-start.5 = ((s8[8388608]{0:T(1024)(128)(4,1)}), s8[4194304]{0:T(1024)(128)(4,1)S(1)}, s32[]{:S(2)}) async-start(s8[8388608]{0:T(1024)(128)(4,1)} %bitcast.61), calls=%async_computation.8 | async-start | bytes 8388608
  583.6 0.7 copy-start.10
  583.6 0.7 copy-start.11
  590.5 1115.5 %copy-start.1 = (bf16[512,2048]{1,0:T(8,128)(2,1)S(1)}, bf16[512,2048]{1,0:T(8,128)(2,1)}, u32[]{:S(2)}) copy-start(bf16[512,2048]{1,0:T(8,128)(2,1)} %param.28) | copy-start | bytes 6291460
Sparse Core Ops, SparseCore 0:
  230.8 33.2 all-reduce.4
  299.6 153.7 all-reduce.8
  583.7 1099.7 all-reduce.6
where the time goes:
time: 1720 us; the launch traced here: 1710 us
  waiting for transfers between devices  1200 us (70%)
  matrix products  342 us (20%)
  other arithmetic  98.8 us (6%)
  local copies, waits for them, and re-layouts  59.4 us (3%)
    psum x1, waiting for transfers between devices, local_layer(): branch_sum = lax.psum(attn_part + mlp_part, 'tp')  1090 us
    dot_general x1, matrix products, local_layer(): jnp.einsum('bcf,fd->bcd', hidden, w_down, preferred_element_type=jnp.floa...  113 us
    psum x1, waiting for transfers between devices, local_layer(): out_total, sum_total = lax.psum((out_part, sum_part), 'cp')  99.2 us
    dot_general x1, matrix products, local_layer(): jnp.einsum('bcd,df->bcf', normed_mlp, w_up, preferred_element_type=jnp.fl...  54.4 us
    dot_general x1, matrix products, local_layer(): jnp.einsum('bcd,de->bce', normed_attn, w_qkv, preferred_element_type=jnp....  36.6 us
  transfers between devices with their start and end apart: 3, of which 3 were waited for; matrix products, arithmetic and copies ran while one was open for 5% of the time, Pallas kernels for 0%

commit v1 on v0

v1 whole, which is shorter than its diff:
```python
import functools
import math

import jax
import jax.numpy as jnp
from jax import lax
from jax.experimental import pallas as pl
from jax.experimental.pallas import tpu as pltpu
from jax.sharding import PartitionSpec as P

EPSILON = 1e-5
NEG_BIG = -1e30
ROTARY_SHARE = 4
ROPE_BASE = 10000.0
LOG2E = math.log2(math.e)
MESH = pl.DeviceIdType.MESH
F32 = jnp.float32
BF16 = jnp.bfloat16
VMEM_LIMIT = 60 * 1024 * 1024
CHUNKS = 64
STAGES = 4
LAG_BACK = 2
LAG_CORE = 3
LAG_Y = 6
LAG_LAST = 7


def layer_norm(values_in, gain_vec, bias_vec):
    x_f32 = values_in.astype(F32)
    row_mean = jnp.mean(x_f32, axis=-1, keepdims=True)
    centered = x_f32 - row_mean
    variance = jnp.mean(centered * centered, axis=-1, keepdims=True)
    return (centered * lax.rsqrt(variance + EPSILON) * gain_vec + bias_vec).astype(BF16)


def rope_table(lengths, chunk_len, head_dim):
    rot_dim = head_dim // ROTARY_SHARE
    half_rot = rot_dim // 2
    positions = lengths[:, None] + jnp.arange(chunk_len, dtype=jnp.int32)[None, :]
    inv_freq = ROPE_BASE ** (-2.0 * jnp.arange(half_rot, dtype=F32) / rot_dim)
    angles = positions.astype(F32)[..., None] * inv_freq
    cos_tab = jnp.cos(angles)
    sin_tab = jnp.sin(angles)
    pad = jnp.zeros(angles.shape[:-1] + (head_dim - 2 * rot_dim,), F32)
    return jnp.concatenate([cos_tab, cos_tab, -sin_tab, sin_tab, pad], axis=-1)


def qkv_kernel(heads, head_dim, x_ref, gain_ref, bias_ref, w_ref, wb_ref, tab_ref, q_ref, k_ref, v_ref):
    rot_dim = head_dim // ROTARY_SHARE
    half_rot = rot_dim // 2
    normed = layer_norm(x_ref[0], gain_ref[...], bias_ref[...])
    tab = tab_ref[0]
    lane = lax.broadcasted_iota(jnp.int32, tab.shape, 1)
    cos_tab = jnp.where(lane < rot_dim, tab, 1.0)
    sin_tab = jnp.where(lane < rot_dim, pltpu.roll(tab, head_dim - rot_dim, 1), 0.0)

    def rotate(values):
        wide = values.astype(F32)
        other = jnp.where(lane < half_rot, pltpu.roll(wide, head_dim - half_rot, 1), pltpu.roll(wide, half_rot, 1))
        return (wide * cos_tab + other * sin_tab).astype(BF16)

    pair = 2 * 3 * head_dim
    for first in range(0, heads, 2):
        cols = slice(first // 2 * pair, first // 2 * pair + pair)
        both = (jnp.dot(normed, w_ref[:, cols], preferred_element_type=F32) + wb_ref[:, cols]).astype(BF16)
        for h in (first, first + 1):
            base = (h - first) * 3 * head_dim
            q_ref[0, h] = rotate(both[:, base:base + head_dim])
            k_ref[0, h] = rotate(both[:, base + head_dim:base + 2 * head_dim])
            v_ref[0, h] = both[:, base + 2 * head_dim:base + 3 * head_dim]


def project_qkv(hidden_in, gain, bias, w_qkv, b_qkv, table, heads, head_dim):
    rows, chunk_len, d_model = hidden_in.shape
    tile = chunk_len // 4
    width = w_qkv.shape[1]
    out = jax.ShapeDtypeStruct((rows, heads, chunk_len, head_dim), BF16)
    head_spec = pl.BlockSpec((1, heads, tile, head_dim), lambda b, t: (b, 0, t, 0))
    once = dict(pipeline_mode=pl.Buffered(1))
    return pl.pallas_call(
        functools.partial(qkv_kernel, heads, head_dim),
        grid=(rows, chunk_len // tile),
        in_specs=[
            pl.BlockSpec((1, tile, d_model), lambda b, t: (b, t, 0)),
            pl.BlockSpec((1, d_model), lambda b, t: (0, 0), **once),
            pl.BlockSpec((1, d_model), lambda b, t: (0, 0), **once),
            pl.BlockSpec((d_model, width), lambda b, t: (0, 0), **once),
            pl.BlockSpec((1, width), lambda b, t: (0, 0), **once),
            pl.BlockSpec((1, tile, head_dim), lambda b, t: (b, t, 0)),
        ],
        out_specs=[head_spec] * 3,
        out_shape=[out] * 3,
        compiler_params=pltpu.CompilerParams(vmem_limit_bytes=VMEM_LIMIT),
        cost_estimate=pl.CostEstimate(
            flops=2 * rows * chunk_len * d_model * width,
            bytes_accessed=2 * (rows * chunk_len * (d_model + width) + d_model * width),
            transcendentals=0,
        ),
        name="qkv_rope",
    )(hidden_in, gain[None], bias[None], w_qkv, b_qkv.astype(F32)[None], table)


def block_step(heads, scale, q_of, k_of, v_of, m_scr, l_scr, o_scr, mask):
    for h in range(heads):
        scores = lax.dot_general(q_of(h), k_of(h), (((1,), (1,)), ((), ())), preferred_element_type=F32) * scale
        if mask is not None:
            scores = jnp.where(mask, scores, NEG_BIG)
        m_old = m_scr[h]
        m_new = jnp.maximum(m_old, jnp.max(scores, axis=1, keepdims=True))
        probs = jnp.exp2(scores - m_new[:, :1])
        shrink = jnp.exp2(m_old - m_new)
        l_scr[h] = l_scr[h] * shrink + jnp.sum(probs, axis=1, keepdims=True)
        m_scr[h] = m_new
        o_scr[h] = o_scr[h] * shrink + jnp.dot(probs.astype(BF16), v_of(h), preferred_element_type=F32)


def attn_kernel(heads, head_dim, q_tile, key_block, with_self, meta, q_ref, k_ref, v_ref, *rest):
    if with_self:
        kn_ref, vn_ref, *rest = rest
    os_ref, ss_ref, ok_ref, sk_ref, m_scr, l_scr, o_scr = rest
    slot = pl.program_id(0)
    tile = pl.program_id(1)
    valid = meta[2 + slot]
    scale = head_dim ** -0.5 * LOG2E
    m_scr[...] = jnp.full(m_scr.shape, NEG_BIG, F32)
    l_scr[...] = jnp.zeros(l_scr.shape, F32)
    o_scr[...] = jnp.zeros(o_scr.shape, F32)

    def query(h):
        return q_ref[0, h]

    def cache_block(block, mask):
        start = pl.multiple_of(block * key_block, key_block)
        block_step(
            heads, scale, query,
            lambda h: k_ref[0, h, pl.ds(start, key_block), :],
            lambda h: v_ref[0, h, pl.ds(start, key_block), :],
            m_scr, l_scr, o_scr, mask,
        )

    whole = lax.div(valid, key_block)

    @pl.loop(0, whole)
    def _(block):
        cache_block(block, None)

    @pl.when(lax.rem(valid, key_block) > 0)
    def _():
        keys = whole * key_block + lax.broadcasted_iota(jnp.int32, (q_tile, key_block), 1)
        cache_block(whole, keys < valid)

    if with_self:
        def own_block(block, mask):
            start = pl.multiple_of(block * q_tile, q_tile)
            block_step(
                heads, scale, query,
                lambda h: kn_ref[0, h, pl.ds(start, q_tile), :],
                lambda h: vn_ref[0, h, pl.ds(start, q_tile), :],
                m_scr, l_scr, o_scr, mask,
            )

        @pl.when(slot == 1)
        def _():
            @pl.loop(0, tile)
            def _(block):
                own_block(block, None)

            shape = (q_tile, q_tile)
            own_block(tile, lax.broadcasted_iota(jnp.int32, shape, 0) >= lax.broadcasted_iota(jnp.int32, shape, 1))

    lane = lax.broadcasted_iota(jnp.int32, (q_tile, head_dim), 1)
    stats = jnp.zeros((q_tile, head_dim), F32)
    for h in range(heads):
        stats = jnp.where(lane == h, m_scr[h], stats)
        stats = jnp.where(lane == heads + h, l_scr[h], stats)
    stats = stats.T[:8]

    @pl.when(slot == 0)
    def _():
        os_ref[...] = o_scr[...]
        ss_ref[...] = stats

    @pl.when(slot == 1)
    def _():
        ok_ref[...] = o_scr[...]
        sk_ref[...] = stats


def attend(rows, lengths, block_start, q_all, k_block, v_block, k_new=None, v_new=None):
    heads, chunk_len, head_dim = q_all.shape[1:]
    block_len = k_block.shape[2]
    q_tile = chunk_len // 4
    key_block = block_len // 2
    tiles = chunk_len // q_tile
    valid = jnp.clip(lengths[rows] - block_start, 0, block_len)
    meta = jnp.concatenate([rows, valid]).astype(jnp.int32)
    with_self = k_new is not None
    keys = pl.BlockSpec((1, heads, block_len, head_dim), lambda s, t, meta: (meta[s], 0, 0, 0))
    own = pl.BlockSpec((1, heads, chunk_len, head_dim), lambda s, t, meta: (meta[1], 0, 0, 0))
    sent = lambda s, t: jnp.where(s == 0, t, tiles - 1)
    kept = lambda s, t: jnp.where(s == 0, 0, t)
    o_shape = jax.ShapeDtypeStruct((heads, chunk_len, head_dim), F32)
    s_shape = jax.ShapeDtypeStruct((8, chunk_len), F32)
    return pl.pallas_call(
        functools.partial(attn_kernel, heads, head_dim, q_tile, key_block, with_self),
        grid_spec=pltpu.PrefetchScalarGridSpec(
            num_scalar_prefetch=1,
            grid=(2, tiles),
            in_specs=[pl.BlockSpec((1, heads, q_tile, head_dim), lambda s, t, meta: (meta[s], 0, t, 0)), keys, keys]
            + ([own, own] if with_self else []),
            out_specs=[
                pl.BlockSpec((heads, q_tile, head_dim), lambda s, t, meta: (0, sent(s, t), 0)),
                pl.BlockSpec((8, q_tile), lambda s, t, meta: (0, sent(s, t))),
                pl.BlockSpec((heads, q_tile, head_dim), lambda s, t, meta: (0, kept(s, t), 0)),
                pl.BlockSpec((8, q_tile), lambda s, t, meta: (0, kept(s, t))),
            ],
            scratch_shapes=[pltpu.VMEM((heads, q_tile, head_dim), F32)] * 3,
        ),
        out_shape=[o_shape, s_shape, o_shape, s_shape],
        compiler_params=pltpu.CompilerParams(vmem_limit_bytes=VMEM_LIMIT),
        cost_estimate=pl.CostEstimate(
            flops=16 * heads * chunk_len * (block_len + (chunk_len // 4 if with_self else 0)) * head_dim,
            bytes_accessed=2 * heads * (block_len + 2 * chunk_len) * head_dim * 4,
            transcendentals=2 * heads * chunk_len * block_len,
        ),
        name="attend_own" if with_self else "attend",
    )(meta, q_all, k_block, v_block, *((k_new, v_new) if with_self else ()))


def merge(heads, pieces):
    peak = functools.reduce(jnp.maximum, [s[:heads] for _, s in pieces])
    weights = [jnp.exp2(s[:heads] - peak) for _, s in pieces]
    total = functools.reduce(jnp.add, [s[heads:2 * heads] * w for (_, s), w in zip(pieces, weights)])
    out = functools.reduce(jnp.add, [o * w[..., None] for (o, _), w in zip(pieces, weights)])
    return out, peak, total


def share_kernel(tp_size, part, out_ref, acc, from_left, from_right, from_y, from_core, from_last, stage,
                 in_sem, left_sem, right_sem, y_sem, core_sem, last_sem, send_sem, stage_sem):
    z = lax.axis_index("tp")
    j = lax.axis_index("cp")
    y, c = lax.div(j, 2), lax.rem(j, 2)
    across, mate, corner = (1 - y) * 2 + c, y * 2 + (1 - c), (1 - y) * 2 + (1 - c)
    tokens = part.shape[0] // CHUNKS
    pairs = CHUNKS // 2
    last = tp_size - 1
    root_a, root_b = (tp_size - 1) // 2, tp_size // 2

    barrier = pltpu.get_barrier_semaphore()
    pl.semaphore_signal(barrier, inc=1, device_id={"cp": across}, device_id_type=MESH)
    pl.semaphore_signal(barrier, inc=1, device_id={"cp": mate}, device_id_type=MESH)

    @pl.when(z > 0)
    def _():
        pl.semaphore_signal(barrier, inc=1, device_id={"tp": z - 1}, device_id_type=MESH)

    @pl.when(z < last)
    def _():
        pl.semaphore_signal(barrier, inc=1, device_id={"tp": z + 1}, device_id_type=MESH)

    inside = jnp.logical_and(z > 0, z < last)

    @pl.when(inside)
    def _():
        pl.semaphore_wait(barrier, 4)

    @pl.when(jnp.logical_not(inside))
    def _():
        pl.semaphore_wait(barrier, 3)

    def at(ref, k):
        return ref.at[pl.ds(pl.multiple_of(k * tokens, tokens), tokens), :]

    def load(k):
        return pltpu.make_async_copy(at(part, k), at(acc, k), in_sem.at[k])

    def remote(src, dst, k, which, arrive, device):
        return pltpu.make_async_remote_copy(
            src_ref=at(src, k), dst_ref=at(dst, k), send_sem=send_sem.at[which], recv_sem=arrive.at[k],
            device_id=device, device_id_type=MESH,
        )

    def send_right(src, k):
        remote(src, from_left, k, 0, left_sem, {"tp": z + 1}).start()

    def send_left(src, k):
        remote(src, from_right, k, 1, right_sem, {"tp": z - 1}).start()

    def arrived(ref, sem, k):
        remote(ref, ref, k, 0, sem, {"cp": j}).wait_recv()

    def drained(ref, which):
        pltpu.make_async_copy(ref, ref, send_sem.at[which]).wait()

    def emit(stream, src, k, row):
        slot = lax.rem(k, STAGES)

        def copy():
            return pltpu.make_async_copy(stage.at[stream, slot], at(out_ref.at[row], k), stage_sem.at[stream, slot])

        @pl.when(k >= STAGES)
        def _():
            copy().wait()

        rows = pl.ds(pl.multiple_of(k * tokens, tokens), tokens)
        stage[stream, slot] = src[rows, :].astype(BF16)
        copy().start()

    def finish(src, k):
        remote(src, from_y, k, 2, y_sem, {"cp": across}).start()
        remote(src, from_core, k, 3, core_sem, {"cp": mate}).start()
        emit(0, src, k, j)

    def gathered(i):
        def lagged(lag, act):
            @pl.when(jnp.logical_and(i >= lag, i < pairs + lag))
            def _():
                for n in range(2):
                    act((i - lag) * 2 + n)

        def core(k):
            arrived(from_core, core_sem, k)
            emit(1, from_core, k, mate)

        def side(k):
            arrived(from_y, y_sem, k)
            remote(from_y, from_last, k, 4, last_sem, {"cp": mate}).start()
            emit(2, from_y, k, across)

        def final(k):
            arrived(from_last, last_sem, k)
            emit(3, from_last, k, corner)

        lagged(LAG_CORE, core)
        lagged(LAG_Y, side)
        lagged(LAG_LAST, final)

    def add(k, *others):
        rows = pl.ds(pl.multiple_of(k * tokens, tokens), tokens)
        total = acc[rows, :]
        for other in others:
            total = total + other[rows, :]
        acc[rows, :] = total

    @pl.loop(0, CHUNKS)
    def _(k):
        load(k).start()

    steps = pairs + LAG_LAST + 1

    def run(near, far):
        @pl.loop(0, steps)
        def _(i):
            @pl.when(i < pairs)
            def _():
                near(i)

            @pl.when(jnp.logical_and(i >= LAG_BACK, i < pairs + LAG_BACK))
            def _():
                far(i - LAG_BACK)

            gathered(i)

    def end(first, send):
        inbox, sem = (from_right, right_sem) if first else (from_left, left_sem)

        @pl.loop(0, CHUNKS)
        def _(k):
            load(k).wait()
            send(acc, k)

        def got(k):
            arrived(inbox, sem, k)
            finish(inbox, k)

        near_bit = 0 if first else 1
        run(lambda i: got(2 * i + near_bit), lambda i: got(2 * i + 1 - near_bit))

    def inner(left_side):
        mine = 0 if left_side else 1
        if left_side:
            (outer, outer_sem, to_outer), (inward, inward_sem, to_inner) = (
                (from_left, left_sem, send_left), (from_right, right_sem, send_right))
        else:
            (outer, outer_sem, to_outer), (inward, inward_sem, to_inner) = (
                (from_right, right_sem, send_right), (from_left, left_sem, send_left))

        def near(i):
            passed, rooted = 2 * i + 1 - mine, 2 * i + mine
            load(passed).wait()
            arrived(outer, outer_sem, passed)
            add(passed, outer)
            to_inner(acc, passed)
            load(rooted).wait()
            arrived(outer, outer_sem, rooted)
            arrived(inward, inward_sem, rooted)
            add(rooted, from_left, from_right)
            to_outer(acc, rooted)
            to_inner(acc, rooted)
            finish(acc, rooted)

        def far(i):
            k = 2 * i + 1 - mine
            arrived(inward, inward_sem, k)
            to_outer(inward, k)
            finish(inward, k)

        run(near, far)

    @pl.when(z == 0)
    def _():
        end(True, send_right)

    @pl.when(z == root_a)
    def _():
        inner(True)

    @pl.when(z == root_b)
    def _():
        inner(False)

    @pl.when(z == last)
    def _():
        end(False, send_left)

    @pl.when(z < last)
    def _():
        drained(acc, 0)

    @pl.when(z > 0)
    def _():
        drained(acc, 1)

    for which in (2, 3, 4):
        drained(acc, which)
    for stream in range(4):
        for slot in range(STAGES):
            pltpu.make_async_copy(stage.at[stream, slot], at(out_ref.at[0], 0), stage_sem.at[stream, slot]).wait()


def share(part, num_rows, tp_size):
    chunk_len, d_model = part.shape
    tokens = chunk_len // CHUNKS
    buffer = pltpu.VMEM((chunk_len, d_model), F32)
    arrivals = pltpu.SemaphoreType.DMA((CHUNKS,))
    return pl.pallas_call(
        functools.partial(share_kernel, tp_size),
        in_specs=[pl.BlockSpec(memory_space=pl.ANY)],
        out_specs=pl.BlockSpec(memory_space=pl.ANY),
        out_shape=jax.ShapeDtypeStruct((num_rows, chunk_len, d_model), BF16),
        scratch_shapes=[buffer] * 6
        + [pltpu.VMEM((4, STAGES, tokens, d_model), BF16)]
        + [arrivals] * 6
        + [pltpu.SemaphoreType.DMA((5,)), pltpu.SemaphoreType.DMA((4, STAGES))],
        compiler_params=pltpu.CompilerParams(collective_id=0, has_side_effects=True, vmem_limit_bytes=VMEM_LIMIT),
        cost_estimate=pl.CostEstimate(flops=100_000_000_000, bytes_accessed=chunk_len * d_model * 16, transcendentals=0),
        name="share",
    )(part)


def solution(mesh):
    in_specs = (P("dp", None, None), P("dp"), P("dp", "tp", "cp", None), P("dp", "tp", "cp", None), P(), P(), P(), P(), P(None, "tp"), P("tp"), P("tp", None), P(), P(None, "tp"), P("tp"), P("tp", None), P())
    out_specs = (P("dp", None, None), P("dp", "tp", None, None), P("dp", "tp", None, None))
    tp_size = mesh.shape["tp"]
    cp_size = mesh.shape["cp"]
    swap_core = [(i, i ^ 1) for i in range(cp_size)]
    swap_y = [(i, i ^ 2) for i in range(cp_size)]

    def local_layer(hidden_in, lengths, k_block, v_block, ln1_gain, ln1_bias, ln2_gain, ln2_bias, w_qkv, b_qkv, w_out, b_out, w_up, b_up, w_down, b_down):
        num_rows, chunk_len, d_model = hidden_in.shape
        heads, block_len, head_dim = k_block.shape[1:]
        j = lax.axis_index("cp")
        start = j * block_len
        table = rope_table(lengths, chunk_len, head_dim)
        q_rot, k_new, v_new = project_qkv(hidden_in, ln1_gain, ln1_bias, w_qkv, b_qkv, table, heads, head_dim)

        far_rows = jnp.stack([j ^ 3, j ^ 2]).astype(jnp.int32)
        near_rows = jnp.stack([j ^ 1, j]).astype(jnp.int32)
        o_s, s_s, o_k, s_k = attend(far_rows, lengths, start, q_rot, k_block, v_block)
        o_r, s_r = lax.ppermute(o_s, "cp", swap_core), lax.ppermute(s_s, "cp", swap_core)
        o_far, peak, total = merge(heads, [(o_k, s_k), (o_r, s_r)])
        s_far = jnp.concatenate([peak, total], axis=0)
        o_y, s_y = lax.ppermute(o_far, "cp", swap_y), lax.ppermute(s_far, "cp", swap_y)

        o_s, s_s, o_own, s_own = attend(near_rows, lengths, start, q_rot, k_block, v_block, k_new, v_new)
        o_c, s_c = lax.ppermute(o_s, "cp", swap_core), lax.ppermute(s_s, "cp", swap_core)

        own_in = lax.dynamic_index_in_dim(hidden_in, j, 0, keepdims=False)
        normed_mlp = layer_norm(own_in, ln2_gain, ln2_bias)
        hidden = jax.nn.gelu(jnp.dot(normed_mlp, w_up, preferred_element_type=F32) + b_up.astype(F32), approximate=False).astype(BF16)
        hidden = lax.optimization_barrier(hidden)
        extra = own_in.astype(F32) + b_out.astype(F32) + b_down.astype(F32)
        mlp_part = jnp.dot(hidden, w_down, preferred_element_type=F32) + jnp.where(lax.axis_index("tp") == 0, extra, 0.0)
        mlp_part = lax.optimization_barrier(mlp_part)

        out, _, total = merge(heads, [(o_own, s_own), (o_c, s_c), (o_y, s_y)])
        context = (out / total[..., None]).astype(BF16)
        attn_part = jnp.einsum("hcd,hde->ce", context, w_out.reshape(heads, head_dim, d_model), preferred_element_type=F32)
        part = attn_part + mlp_part
        return share(part, num_rows, tp_size), k_new, v_new

    return jax.shard_map(local_layer, mesh=mesh, in_specs=in_specs, out_specs=out_specs, check_vma=False)
```

time: 1720 us -> 519 us (0.30)
  waiting for transfers between devices: 1200 us -> 32.7 us
  Pallas kernels: 0 us -> 379 us
  matrix products: 342 us -> 52.9 us
  other arithmetic: 98.8 us -> 21.8 us
  local copies, waits for them, and re-layouts: 59.4 us -> 27.8 us
    psum x2 -> x0, waiting for transfers between devices: 1190 us -> none  [the longest x1 1090 us: local_layer(): branch_sum = lax.psum(attn_part + mlp_part, 'tp')]
    pallas_call x0 -> x4, Pallas kernels: none -> 379 us  [the longest x1 258 us: share(): pl.pallas_call(functools.partial(share_kernel, tp_size), in_specs=[pl.Blo...]
    dot_general x8 -> x3, matrix products: 342 us -> 52.9 us  [the longest x1 32.4 us: local_layer(): jnp.dot(normed_mlp, w_up, preferred_element_type=F32) + b_up.astype(F32)]
    reduce_sum x2 -> x0, other arithmetic: 43.4 us -> none  [the longest x1 21.8 us: self_piece(): return (piece_max, probs.sum(axis=-1), piece_out)]
    ppermute x0 -> x6, waiting for transfers between devices: none -> 32.7 us  [the longest x1 32.7 us: local_layer(): lax.ppermute(o_far, 'cp', swap_y)]
    convert_element_type x7 -> x4, other arithmetic: 25.7 us -> 0.86 us  [the longest x1 0.85 us: rope_table(): angles = positions.astype(F32)[..., None] * inv_freq]
    transpose x1 -> x0, local copies, waits for them, and re-layouts: 22.6 us -> none  [local_layer(): jnp.swapaxes(v_chunk, 1, 2)]
  transfers between devices with their start and end apart: 3 -> 6, of which waited for: 3 -> 1; matrix products, arithmetic and copies ran while one was open for 5% -> 11% of each run, Pallas kernels for 0% -> 8%
where the time goes in v1:
time: 519 us; the launch traced here: 518 us
  Pallas kernels  379 us (73%)
  matrix products  52.9 us (10%)
  waiting for transfers between devices  32.7 us (6%)
  local copies, waits for them, and re-layouts  27.8 us (5%)
  other arithmetic  21.8 us (4%)
    pallas_call x1, Pallas kernels, share(): pl.pallas_call(functools.partial(share_kernel, tp_size), in_specs=[pl.Blo...  258 us
    pallas_call x2, Pallas kernels, attend(): pl.pallas_call(functools.partial(attn_kernel, heads, head_dim, q_tile, ke...  77.1 us
    pallas_call x1, Pallas kernels, project_qkv(): pl.pallas_call(functools.partial(qkv_kernel, heads, head_dim), grid=(rows...  43.5 us
    ppermute x1, waiting for transfers between devices, local_layer(): lax.ppermute(o_far, 'cp', swap_y)  32.7 us
    dot_general x1, matrix products, local_layer(): jnp.dot(normed_mlp, w_up, preferred_element_type=F32) + b_up.astype(F32)  32.4 us
    unnamed x21, local copies, waits for them, and re-layouts  14.4 us
    dot_general x1, matrix products, local_layer(): jnp.dot(hidden, w_down, preferred_element_type=F32)  13.1 us
  transfers between devices with their start and end apart: 6, of which 1 were waited for; matrix products, arithmetic and copies ran while one was open for 11% of the time, Pallas kernels for 8%

profile of v1, /device:TPU:0, one launch (start us, length us, event | category | flops | bytes accessed | tf_op | source)
XLA Modules:
  0.0 518.0 jit_solution(2726550200128821508)
XLA Ops:
  0.6 0.0 copy-start
  0.7 0.1 fusion.39
  0.8 0.9 add_convert_fusion
  1.6 1.3 gather_fusion.1
  2.9 0.1 fusion.38
  3.0 1.3 gather_fusion
  4.3 1.3 reshape.231.wb_ref
  5.6 9.7 %multiply_sine_fusion = (f32[4,1024,16]{2,1,0:T(8,128)}, f32[4,1024,16]{2,1,0:T(8,128)}, f32[4,1024,16]{2,1,0:T(8,128)}) fusion(f32[16]{0:T(128)S(1)} %multiply_power_fusion, f32[4,1024]{1,0:T(4,128)S(1)} %add_convert_fusion), kind=kLoop, calls=%fused_computation.40 | loop fusion | flops 131072 | bytes 802880 | tf_op jit(solution)/shard_map/sin | solution.py:43
  15.2 0.6 pad_add_fusion.1.meta
  15.9 1.5 broadcast_in_dim.15
  17.3 8.1 %concatenate.53.tab_ref = f32[4,1024,128]{2,1,0:T(8,128)} concatenate(f32[4,1024,16]{2,1,0:T(8,128)} %get-tuple-element.35, f32[4,1024,16]{2,1,0:T(8,128)} %get-tuple-element.35, f32[4,1024,16]{2,1,0:T(8,128)} %get-tuple-element.34, f32[4,1024,16]{2,1,0:T(8,128)} %get-tuple-element.33, f32[4,1024,64]{2,1,0:T(8,128)} %broadcast_in_dim.15), dimensions={2} | concatenate | bytes 4194304 | tf_op jit(solution)/shard_map/concatenate | solution.py:45
  25.5 43.5 %qkv_rope.1 = (bf16[4,4,1024,128]{3,2,1,0:T(8,128)(2,1)}, bf16[4,4,1024,128]{3,2,1,0:T(8,128)(2,1)}, bf16[4,4,1024,128]{3,2,1,0:T(8,128)(2,1)}) custom-call(bf16[4,1024,2048]{2,1,0:T(8,128)(2,1)} %x_ref.1, f32[1,2048]{1,0:T(1,128)} %bitcast.49, f32[1,2048]{1,0:T(1,128)} %bitcast.50, bf16[2048,1536]{1,0:T(8,128)(2,1)} %w_ref.1, f32[1,1536]{1,0:T(1,128)} %reshape.231.wb_ref, ...), custom_call_target="tpu_custom_call" | custom-call | flops 25769803776 | bytes 35651584 | tf_op jit(solution)/shard_map/qkv_rope/pallas_call | solution.py:80
  69.0 35.5 %attend.1 = (f32[4,1024,128]{2,1,0:T(8,128)}, f32[8,1024]{1,0:T(8,128)}, f32[4,1024,128]{2,1,0:T(8,128)}, f32[8,1024]{1,0:T(8,128)}) custom-call(s32[4]{0:T(128)} %pad_add_fusion.1.meta, bf16[4,4,1024,128]{3,2,1,0:T(8,128)(2,1)} %get-tuple-element.14.q_ref, bf16[4,4,1024,128]{3,2,1,0:T(8,128)(2,1)} %k_ref.3, bf16[4,4,1024,128]{3,2,1,0:T(8,128)(2,1)} %v_ref.3), custom_call_target="tpu_custom_call" | custom-call | flops 8589934592 | bytes 12582912 | tf_op jit(solution)/shard_map/attend/pallas_call | solution.py:204
  104.5 0.0 collective-permute-start.1
  104.5 0.6 pad_add_fusion.meta
  105.1 41.6 %attend_own.1 = (f32[4,1024,128]{2,1,0:T(8,128)}, f32[8,1024]{1,0:T(8,128)}, f32[4,1024,128]{2,1,0:T(8,128)}, f32[8,1024]{1,0:T(8,128)}) custom-call(s32[4]{0:T(128)} %pad_add_fusion.meta, bf16[4,4,1024,128]{3,2,1,0:T(8,128)(2,1)} %get-tuple-element.14.q_ref, bf16[4,4,1024,128]{3,2,1,0:T(8,128)(2,1)} %k_ref.3, bf16[4,4,1024,128]{3,2,1,0:T(8,128)(2,1)} %v_ref.3, ...), custom_call_target="tpu_custom_call" | custom-call | flops 10737418240 | bytes 12582912 | tf_op jit(solution)/shard_map/attend_own/pallas_call | solution.py:204
  146.7 0.0 copy-start.5
  146.7 0.0 copy-start.8
  146.7 0.0 copy-start.9
  146.7 0.1 collective-permute-start
  146.8 0.5 collective-permute-start.3
  147.3 0.1 collective-permute-start.4
  147.3 2.8 convert_reduce_fusion
  150.2 3.4 fusion.4
  153.6 0.0 copy-done.5
  153.6 0.0 copy-done.8
  153.6 0.0 copy-done.9
  153.6 0.0 copy-start.6
  153.6 0.0 copy-start.7
  153.6 0.0 copy-start.4
  153.7 32.4 %fusion.13 = bf16[1024,2048]{1,0:T(8,128)(2,1)} fusion(f32[2048]{0:T(1024)S(1)} %convert_element_type.38, bf16[2048,2048]{1,0:T(8,128)(2,1)} %param.28, f32[2048]{0:T(1024)S(1)} %copy-done.8, f32[2048]{0:T(1024)S(1)} %copy-done.9, f32[1024]{0:T(1024)S(1)} %add_rsqrt_fusion, f32[1024]{0:T(1024)S(1)} %broadcast_multiply_fusion, ...), kind=kOutput, calls=%fused_computation.18 | convolution fusion | flops 8740929536 | bytes 16809988 | tf_op jit(solution)/shard_map/dot_general | solution.py:490
  186.1 0.0 copy-done.6
  186.1 0.0 copy-done.7
  186.1 0.0 collective-permute-done.1
  186.1 0.0 copy-done.4
  186.2 0.1 collective-permute-start.2
  186.2 0.0 collective-permute-done.4
  186.2 3.6 multiply_add_fusion
  189.8 0.0 copy-start.3
  189.8 0.0 copy-start.2
  189.8 2.1 collective-permute-start.5
  191.9 13.1 %fusion.10 = f32[1024,2048]{1,0:T(8,128)S(1)} fusion(f32[2048]{0:T(1024)S(1)} %convert_element_type.41, f32[2048]{0:T(1024)S(1)} %convert_element_type.40, pred[]{:T(512)S(6)} %eq.3, bf16[1024,2048]{1,0:T(8,128)(2,1)} %fusion.13, bf16[2048,2048]{1,0:T(8,128)(2,1)} %param.30, bf16[4,1024,2048]{2,1,0:T(8,128)(2,1)} %x_ref.1, s32[]{:T(128)S(6)} %select_n.34), kind=kOutput, calls=%fused_computation.15 | convolution fusion | flops 8600420352 | bytes 25182212 | tf_op jit(solution)/shard_map/dot_general | solution.py:493
  205.0 0.0 collective-permute-done
  205.1 0.0 collective-permute-done.2
  205.1 0.0 copy-done.3
  205.1 0.0 collective-permute-done.3
  205.1 32.7 %collective-permute-done.5 = f32[4,1024,128]{2,1,0:T(8,128)S(1)} collective-permute-done((f32[4,1024,128]{2,1,0:T(8,128)S(1)}, f32[4,1024,128]{2,1,0:T(8,128)S(1)}, u32[]{:S(2)}, u32[]{:S(2)}) %collective-permute-start.5) | collective-permute-done | bytes 2097184 | tf_op jit(solution)/shard_map/ppermute | solution.py:483
  237.9 0.0 copy-done
  237.9 0.0 copy-done.2
  237.9 7.3 %bitcast_add_fusion.part = f32[1024,2048]{1,0:T(8,128)} fusion(f32[1024,2048]{1,0:T(8,128)S(1)} %fusion.10, bf16[4,128,2048]{2,1,0:T(8,128)(2,1)S(1)} %bitcast.48, f32[4,1024,128]{2,1,0:T(8,128)S(1)} %collective-permute-done.5, f32[4,1024,128]{2,1,0:T(8,128)} %collective-permute-done.3, f32[4,1024,128]{2,1,0:T(8,128)S(1)} %copy-done.2, ...), kind=kOutput, calls=%fused_computation.19 | convolution fusion | flops 2153250816 | bytes 25231360 | tf_op jit(solution)/shard_map/hcd,hde->ce/dot_general | solution.py:498
  245.2 258.5 %share.1 = bf16[4,1024,2048]{2,1,0:T(8,128)(2,1)} custom-call(f32[1024,2048]{1,0:T(8,128)} %bitcast_add_fusion.part), custom_call_target="tpu_custom_call" | custom-call | flops 99999997952 | bytes 33554432 | tf_op jit(solution)/shard_map/share/pallas_call | solution.py:446
  503.7 0.0 copy-start.1
  503.7 14.3 %copy.21 = bf16[4,1024,2048]{2,1,0:T(8,128)(2,1)} copy(bf16[4,1024,2048]{2,1,0:T(8,128)(2,1)} %share.1) | data formatting | bytes 33554432
  518.0 0.0 copy-done.1
  (12 shorter events, 0.1 us)
Async XLA Ops:
  0.6 237.2 %copy-start = (bf16[512,2048]{1,0:T(8,128)(2,1)S(1)}, bf16[512,2048]{1,0:T(8,128)(2,1)}, u32[]{:S(2)}) copy-start(bf16[512,2048]{1,0:T(8,128)(2,1)} %param.26) | copy-start | bytes 6291460
  104.5 81.6 %collective-permute-start.1 = (f32[8,1024]{1,0:T(8,128)}, f32[8,1024]{1,0:T(8,128)S(1)}, u32[]{:S(2)}, u32[]{:S(2)}) collective-permute-start(f32[8,1024]{1,0:T(8,128)} %get-tuple-element.21), channel_id=1, source_target_pairs={{0,1},{1,0},{2,3},{3,2},{4,5},{5,4},{6,7},{7,6},{8,9},{9,8},{10,11... | collective-permute-start | bytes 98312 | tf_op jit(solution)/shard_map/ppermute | solution.py:480
  146.7 6.9 %copy-start.5 = (bf16[2048]{0:T(1024)(128)(2,1)S(1)}, bf16[2048]{0:T(1024)(128)(2,1)}, u32[]{:S(2)}) copy-start(bf16[2048]{0:T(1024)(128)(2,1)} %param.29) | copy-start | bytes 12292
  146.7 6.9 %copy-start.8 = (f32[2048]{0:T(1024)S(1)}, f32[2048]{0:T(1024)}, u32[]{:S(2)}) copy-start(f32[2048]{0:T(1024)} %param.23) | copy-start | bytes 24580
  146.7 6.9 %copy-start.9 = (f32[2048]{0:T(1024)S(1)}, f32[2048]{0:T(1024)}, u32[]{:S(2)}) copy-start(f32[2048]{0:T(1024)} %param.22) | copy-start | bytes 24580
  146.7 58.4 %collective-permute-start = (f32[8,1024]{1,0:T(8,128)}, f32[8,1024]{1,0:T(8,128)S(1)}, u32[]{:S(2)}, u32[]{:S(2)}) collective-permute-start(f32[8,1024]{1,0:T(8,128)} %get-tuple-element.19), channel_id=1, source_target_pairs={{0,1},{1,0},{2,3},{3,2},{4,5},{5,4},{6,7},{7,6},{8,9},{9,8},{10,11... | collective-permute-start | bytes 98312 | tf_op jit(solution)/shard_map/ppermute | solution.py:486
  146.8 58.4 %collective-permute-start.3 = (f32[4,1024,128]{2,1,0:T(8,128)}, f32[4,1024,128]{2,1,0:T(8,128)}, u32[]{:S(2)}, u32[]{:S(2)}) collective-permute-start(f32[4,1024,128]{2,1,0:T(8,128)} %get-tuple-element.22), channel_id=1, source_target_pairs={{0,1},{1,0},{2,3},{3,2},{4,5},{5,4},{6,7},{7,6},{8,9},{9,8},{10,11... | collective-permute-start | bytes 6291464 | tf_op jit(solution)/shard_map/ppermute | solution.py:486
  147.3 39.0 %collective-permute-start.4 = (f32[4,1024,128]{2,1,0:T(8,128)}, f32[4,1024,128]{2,1,0:T(8,128)}, u32[]{:S(2)}, u32[]{:S(2)}) collective-permute-start(f32[4,1024,128]{2,1,0:T(8,128)} %get-tuple-element.24), channel_id=1, source_target_pairs={{0,1},{1,0},{2,3},{3,2},{4,5},{5,4},{6,7},{7,6},{8,9},{9,8},{10,11... | collective-permute-start | bytes 6291464 | tf_op jit(solution)/shard_map/ppermute | solution.py:480
  153.6 32.4 %copy-start.6 = (bf16[2048]{0:T(1024)(128)(2,1)S(1)}, bf16[2048]{0:T(1024)(128)(2,1)}, u32[]{:S(2)}) copy-start(bf16[2048]{0:T(1024)(128)(2,1)} %param.27) | copy-start | bytes 12292
  153.6 32.4 %copy-start.7 = (bf16[2048]{0:T(1024)(128)(2,1)S(1)}, bf16[2048]{0:T(1024)(128)(2,1)}, u32[]{:S(2)}) copy-start(bf16[2048]{0:T(1024)(128)(2,1)} %param.31) | copy-start | bytes 12292
  153.6 32.5 %copy-start.4 = (f32[8,1024]{1,0:T(8,128)S(1)}, f32[8,1024]{1,0:T(8,128)}, u32[]{:S(2)}) copy-start(f32[8,1024]{1,0:T(8,128)} %get-tuple-element.20) | copy-start | bytes 98308
  186.2 18.9 %collective-permute-start.2 = (f32[8,1024]{1,0:T(8,128)S(1)}, f32[8,1024]{1,0:T(8,128)S(1)}, u32[]{:S(2)}, u32[]{:S(2)}) collective-permute-start(f32[8,1024]{1,0:T(8,128)S(1)} %pad_maximum_fusion), channel_id=1, source_target_pairs={{0,2},{1,3},{2,0},{3,1},{4,6},{5,7},{6,4},{7,5},{8,10},{9,11},{10,... | collective-permute-start | bytes 98312 | tf_op jit(solution)/shard_map/ppermute | solution.py:483
  189.8 15.3 %copy-start.3 = (f32[8,1024]{1,0:T(8,128)S(1)}, f32[8,1024]{1,0:T(8,128)}, u32[]{:S(2)}) copy-start(f32[8,1024]{1,0:T(8,128)} %get-tuple-element.18) | copy-start | bytes 98308
  189.8 48.0 %copy-start.2 = (f32[4,1024,128]{2,1,0:T(8,128)S(1)}, f32[4,1024,128]{2,1,0:T(8,128)}, u32[]{:S(2)}) copy-start(f32[4,1024,128]{2,1,0:T(8,128)} %get-tuple-element.17) | copy-start | bytes 6291460
  189.8 48.0 %collective-permute-start.5 = (f32[4,1024,128]{2,1,0:T(8,128)S(1)}, f32[4,1024,128]{2,1,0:T(8,128)S(1)}, u32[]{:S(2)}, u32[]{:S(2)}) collective-permute-start(f32[4,1024,128]{2,1,0:T(8,128)S(1)} %multiply_add_fusion), channel_id=1, source_target_pairs={{0,2},{1,3},{2,0},{3,1},{4,6},{5,7},{6,4},{7,5},{8,10},{9,11},{10,... | collective-permute-start | bytes 6291464 | tf_op jit(solution)/shard_map/ppermute | solution.py:483
  503.7 14.3 %copy-start.1 = (bf16[512,2048]{1,0:T(8,128)(2,1)S(1)}, bf16[512,2048]{1,0:T(8,128)(2,1)}, u32[]{:S(2)}) copy-start(bf16[512,2048]{1,0:T(8,128)(2,1)} %param.26) | copy-start | bytes 6291460

commit v2 on v1

--- a/solution.py
+++ b/solution.py
@@ -19,10 +19,11 @@
 VMEM_LIMIT = 60 * 1024 * 1024
 CHUNKS = 64
 STAGES = 4
-LAG_BACK = 2
-LAG_CORE = 3
-LAG_Y = 6
-LAG_LAST = 7
+LAG_AHEAD = 1
+LAG_BACK = 1
+LAG_CORE = 2
+LAG_Y = 5
+LAG_LAST = 6
 
 
 def layer_norm(values_in, gain_vec, bias_vec):
@@ -38,18 +39,19 @@
     half_rot = rot_dim // 2
     positions = lengths[:, None] + jnp.arange(chunk_len, dtype=jnp.int32)[None, :]
     inv_freq = ROPE_BASE ** (-2.0 * jnp.arange(half_rot, dtype=F32) / rot_dim)
-    angles = positions.astype(F32)[..., None] * inv_freq
+    angles = positions.astype(F32)[:, None, :] * inv_freq[:, None]
     cos_tab = jnp.cos(angles)
     sin_tab = jnp.sin(angles)
-    pad = jnp.zeros(angles.shape[:-1] + (head_dim - 2 * rot_dim,), F32)
-    return jnp.concatenate([cos_tab, cos_tab, -sin_tab, sin_tab, pad], axis=-1)
-
-
-def qkv_kernel(heads, head_dim, x_ref, gain_ref, bias_ref, w_ref, wb_ref, tab_ref, q_ref, k_ref, v_ref):
+    return jnp.concatenate([cos_tab, cos_tab, -sin_tab, sin_tab], axis=1)
+
+
+def qkv_kernel(heads, head_dim, rows, x_ref, gain_ref, bias_ref, w_ref, wb_ref, tab_ref, *rest):
+    q_ref, k_ref, v_ref = rest[-3:]
     rot_dim = head_dim // ROTARY_SHARE
     half_rot = rot_dim // 2
     normed = layer_norm(x_ref[0], gain_ref[...], bias_ref[...])
     tab = tab_ref[0]
+    tab = jnp.concatenate([tab] * (head_dim // tab.shape[0]), axis=0).T
     lane = lax.broadcasted_iota(jnp.int32, tab.shape, 1)
     cos_tab = jnp.where(lane < rot_dim, tab, 1.0)
     sin_tab = jnp.where(lane < rot_dim, pltpu.roll(tab, head_dim - rot_dim, 1), 0.0)
@@ -70,34 +72,40 @@
             v_ref[0, h] = both[:, base + 2 * head_dim:base + 3 * head_dim]
 
 
-def project_qkv(hidden_in, gain, bias, w_qkv, b_qkv, table, heads, head_dim):
-    rows, chunk_len, d_model = hidden_in.shape
+def project_qkv(rows, hidden_in, gain, bias, w_qkv, b_qkv, table, heads, head_dim, filled=()):
+    num_rows, chunk_len, d_model = hidden_in.shape
+    here = rows.shape[0]
     tile = chunk_len // 4
     width = w_qkv.shape[1]
-    out = jax.ShapeDtypeStruct((rows, heads, chunk_len, head_dim), BF16)
-    head_spec = pl.BlockSpec((1, heads, tile, head_dim), lambda b, t: (b, 0, t, 0))
+    out = jax.ShapeDtypeStruct((num_rows, heads, chunk_len, head_dim), BF16)
     once = dict(pipeline_mode=pl.Buffered(1))
+    fixed = lambda b, t, rows: (0, 0)
     return pl.pallas_call(
         functools.partial(qkv_kernel, heads, head_dim),
-        grid=(rows, chunk_len // tile),
-        in_specs=[
-            pl.BlockSpec((1, tile, d_model), lambda b, t: (b, t, 0)),
-            pl.BlockSpec((1, d_model), lambda b, t: (0, 0), **once),
-            pl.BlockSpec((1, d_model), lambda b, t: (0, 0), **once),
-            pl.BlockSpec((d_model, width), lambda b, t: (0, 0), **once),
-            pl.BlockSpec((1, width), lambda b, t: (0, 0), **once),
-            pl.BlockSpec((1, tile, head_dim), lambda b, t: (b, t, 0)),
-        ],
-        out_specs=[head_spec] * 3,
-        out_shape=[out] * 3,
+        grid_spec=pltpu.PrefetchScalarGridSpec(
+            num_scalar_prefetch=1,
+            grid=(here, chunk_len // tile),
+            in_specs=[
+                pl.BlockSpec((1, tile, d_model), lambda b, t, rows: (rows[b], t, 0)),
+                pl.BlockSpec((1, d_model), fixed, **once),
+                pl.BlockSpec((1, d_model), fixed, **once),
+                pl.BlockSpec((d_model, width), fixed, **once),
+                pl.BlockSpec((1, width), fixed, **once),
+                pl.BlockSpec((1, table.shape[1], tile), lambda b, t, rows: (rows[b], 0, t)),
+            ] + [pl.BlockSpec(memory_space=pl.ANY)] * len(filled),
+            out_specs=[pl.BlockSpec((1, heads, tile, head_dim), lambda b, t, rows: (b, 0, t, 0))]
+            + [pl.BlockSpec((1, heads, tile, head_dim), lambda b, t, rows: (rows[b], 0, t, 0))] * 2,
+        ),
+        out_shape=[jax.ShapeDtypeStruct((here, heads, chunk_len, head_dim), BF16), out, out],
+        input_output_aliases={7: 1, 8: 2} if filled else {},
         compiler_params=pltpu.CompilerParams(vmem_limit_bytes=VMEM_LIMIT),
         cost_estimate=pl.CostEstimate(
-            flops=2 * rows * chunk_len * d_model * width,
-            bytes_accessed=2 * (rows * chunk_len * (d_model + width) + d_model * width),
+            flops=2 * here * chunk_len * d_model * width,
+            bytes_accessed=2 * (here * chunk_len * (d_model + width) + d_model * width),
             transcendentals=0,
         ),
-        name="qkv_rope",
-    )(hidden_in, gain[None], bias[None], w_qkv, b_qkv.astype(F32)[None], table)
+        name="qkv_rope_near" if filled else "qkv_rope_far",
+    )(rows, hidden_in, gain[None], bias[None], w_qkv, b_qkv.astype(F32)[None], table, *filled)
 
 
 def block_step(heads, scale, q_of, k_of, v_of, m_scr, l_scr, o_scr, mask):
@@ -120,7 +128,7 @@
     os_ref, ss_ref, ok_ref, sk_ref, m_scr, l_scr, o_scr = rest
     slot = pl.program_id(0)
     tile = pl.program_id(1)
-    valid = meta[2 + slot]
+    valid = jnp.clip(meta[3 + meta[slot]] - meta[2], 0, k_ref.shape[2])
     scale = head_dim ** -0.5 * LOG2E
     m_scr[...] = jnp.full(m_scr.shape, NEG_BIG, F32)
     l_scr[...] = jnp.zeros(l_scr.shape, F32)
@@ -186,14 +194,13 @@
         sk_ref[...] = stats
 
 
-def attend(rows, lengths, block_start, q_all, k_block, v_block, k_new=None, v_new=None):
-    heads, chunk_len, head_dim = q_all.shape[1:]
+def attend(rows, lengths, block_start, q_rows, k_block, v_block, k_new=None, v_new=None):
+    heads, chunk_len, head_dim = q_rows.shape[1:]
     block_len = k_block.shape[2]
     q_tile = chunk_len // 4
     key_block = block_len // 2
     tiles = chunk_len // q_tile
-    valid = jnp.clip(lengths[rows] - block_start, 0, block_len)
-    meta = jnp.concatenate([rows, valid]).astype(jnp.int32)
+    meta = jnp.concatenate([rows, block_start[None], lengths])
     with_self = k_new is not None
     keys = pl.BlockSpec((1, heads, block_len, head_dim), lambda s, t, meta: (meta[s], 0, 0, 0))
     own = pl.BlockSpec((1, heads, chunk_len, head_dim), lambda s, t, meta: (meta[1], 0, 0, 0))
@@ -206,7 +213,7 @@
         grid_spec=pltpu.PrefetchScalarGridSpec(
             num_scalar_prefetch=1,
             grid=(2, tiles),
-            in_specs=[pl.BlockSpec((1, heads, q_tile, head_dim), lambda s, t, meta: (meta[s], 0, t, 0)), keys, keys]
+            in_specs=[pl.BlockSpec((1, heads, q_tile, head_dim), lambda s, t, meta: (s, 0, t, 0)), keys, keys]
             + ([own, own] if with_self else []),
             out_specs=[
                 pl.BlockSpec((heads, q_tile, head_dim), lambda s, t, meta: (0, sent(s, t), 0)),
@@ -224,7 +231,7 @@
             transcendentals=2 * heads * chunk_len * block_len,
         ),
         name="attend_own" if with_self else "attend",
-    )(meta, q_all, k_block, v_block, *((k_new, v_new) if with_self else ()))
+    )(meta, q_rows, k_block, v_block, *((k_new, v_new) if with_self else ()))
 
 
 def merge(heads, pieces):
@@ -348,9 +355,18 @@
 
     steps = pairs + LAG_LAST + 1
 
-    def run(near, far):
+    def run(near, far, early=None):
+        if early is not None:
+            for i in range(LAG_AHEAD):
+                early(i)
+
         @pl.loop(0, steps)
         def _(i):
+            if early is not None:
+                @pl.when(i + LAG_AHEAD < pairs)
+                def _():
+                    early(i + LAG_AHEAD)
+
             @pl.when(i < pairs)
             def _():
                 near(i)
@@ -385,12 +401,15 @@
             (outer, outer_sem, to_outer), (inward, inward_sem, to_inner) = (
                 (from_right, right_sem, send_right), (from_left, left_sem, send_left))
 
-        def near(i):
-            passed, rooted = 2 * i + 1 - mine, 2 * i + mine
+        def early(i):
+            passed = 2 * i + 1 - mine
             load(passed).wait()
             arrived(outer, outer_sem, passed)
             add(passed, outer)
             to_inner(acc, passed)
+
+        def near(i):
+            rooted = 2 * i + mine
             load(rooted).wait()
             arrived(outer, outer_sem, rooted)
             arrived(inward, inward_sem, rooted)
@@ -405,7 +424,7 @@
             to_outer(inward, k)
             finish(inward, k)
 
-        run(near, far)
+        run(near, far, early)
 
     @pl.when(z == 0)
     def _():
@@ -472,17 +491,20 @@
         j = lax.axis_index("cp")
         start = j * block_len
         table = rope_table(lengths, chunk_len, head_dim)
-        q_rot, k_new, v_new = project_qkv(hidden_in, ln1_gain, ln1_bias, w_qkv, b_qkv, table, heads, head_dim)
-
-        far_rows = jnp.stack([j ^ 3, j ^ 2]).astype(jnp.int32)
-        near_rows = jnp.stack([j ^ 1, j]).astype(jnp.int32)
-        o_s, s_s, o_k, s_k = attend(far_rows, lengths, start, q_rot, k_block, v_block)
+        far_rows = jnp.stack([j ^ 3, j ^ 2])
+        near_rows = jnp.stack([j ^ 1, j])
+        weights = (ln1_gain, ln1_bias, w_qkv, b_qkv, table, heads, head_dim)
+
+        q_far, *filled = project_qkv(far_rows, hidden_in, *weights)
+        o_s, s_s, o_k, s_k = attend(far_rows, lengths, start, q_far, k_block, v_block)
         o_r, s_r = lax.ppermute(o_s, "cp", swap_core), lax.ppermute(s_s, "cp", swap_core)
+        q_near, k_new, v_new = project_qkv(near_rows, hidden_in, *weights, filled=filled)
         o_far, peak, total = merge(heads, [(o_k, s_k), (o_r, s_r)])
         s_far = jnp.concatenate([peak, total], axis=0)
+        q_near, o_far, s_far = lax.optimization_barrier((q_near, o_far, s_far))
         o_y, s_y = lax.ppermute(o_far, "cp", swap_y), lax.ppermute(s_far, "cp", swap_y)
 
-        o_s, s_s, o_own, s_own = attend(near_rows, lengths, start, q_rot, k_block, v_block, k_new, v_new)
+        o_s, s_s, o_own, s_own = attend(near_rows, lengths, start, q_near, k_block, v_block, k_new, v_new)
         o_c, s_c = lax.ppermute(o_s, "cp", swap_core), lax.ppermute(s_s, "cp", swap_core)
 
         own_in = lax.dynamic_index_in_dim(hidden_in, j, 0, keepdims=False)

time: 519 us -> 432 us (0.83); the launches traced: 518 us -> 424 us
  Pallas kernels: 379 us -> 335 us
  waiting for transfers between devices: 32.7 us -> 0.02 us
  local copies, waits for them, and re-layouts: 27.8 us -> 15.8 us
  other arithmetic: 21.8 us -> 15.5 us
    pallas_call x1, Pallas kernels: 258 us -> 208 us  [share(): pl.pallas_call(functools.partial(share_kernel, tp_size), in_specs=[pl.Blo...]
    ppermute x1, waiting for transfers between devices: 32.7 us -> 0.01 us  [local_layer(): lax.ppermute(o_far, 'cp', swap_y)]
    sin x1 -> x0, other arithmetic: 9.66 us -> none  [rope_table(): sin_tab = jnp.sin(angles)]
    concatenate x1 -> x0, local copies, waits for them, and re-layouts: 8.13 us -> none  [rope_table(): return jnp.concatenate([cos_tab, cos_tab, -sin_tab, sin_tab, pad], axis=-1)]
    pallas_call x1 -> x2, Pallas kernels: 43.5 us -> 49.6 us  [project_qkv(): pl.pallas_call(functools.partial(qkv_kernel, heads, head_dim), grid_spec=...]
  transfers between devices with their start and end apart: 6 -> 6, of which waited for: 1 -> 0; matrix products, arithmetic and copies ran while one was open for 11% -> 12% of each run, Pallas kernels for 8% -> 17%
where the time goes in v2:
time: 432 us; the launch traced here: 424 us
  Pallas kernels  335 us (78%)
  matrix products  53.5 us (12%)
  local copies, waits for them, and re-layouts  15.8 us (4%)
  other arithmetic  15.5 us (4%)
    pallas_call x1, Pallas kernels, share(): pl.pallas_call(functools.partial(share_kernel, tp_size), in_specs=[pl.Blo...  208 us
    pallas_call x2, Pallas kernels, attend(): pl.pallas_call(functools.partial(attn_kernel, heads, head_dim, q_tile, ke...  77.1 us
    pallas_call x2, Pallas kernels, project_qkv(): pl.pallas_call(functools.partial(qkv_kernel, heads, head_dim), grid_spec=...  49.6 us
    dot_general x1, matrix products, local_layer(): jnp.dot(normed_mlp, w_up, preferred_element_type=F32) + b_up.astype(F32)  32.6 us
    unnamed x21, local copies, waits for them, and re-layouts  14.4 us
    dot_general x1, matrix products, local_layer(): jnp.dot(hidden, w_down, preferred_element_type=F32)  13.3 us
  transfers between devices with their start and end apart: 6, of which 0 were waited for; matrix products, arithmetic and copies ran while one was open for 12% of the time, Pallas kernels for 17%

profile of v2, /device:TPU:0, one launch (start us, length us, event | category | flops | bytes accessed | tf_op | source)
XLA Modules:
  0.0 424.3 jit_solution(2445552210069208354)
XLA Ops:
  0.6 0.0 copy-start
  0.7 1.4 reshape.57.wb_ref
  2.1 0.7 add_convert_fusion
  2.8 0.6 pad_add_fusion.1.rows
  3.4 1.0 multiply_cosine_fusion
  4.4 1.3 add_add_fusion
  5.7 1.2 pad_maximum_fusion.tab_ref
  6.9 24.7 %qkv_rope_far.1 = (bf16[2,4,1024,128]{3,2,1,0:T(8,128)(2,1)}, bf16[4,4,1024,128]{3,2,1,0:T(8,128)(2,1)}, bf16[4,4,1024,128]{3,2,1,0:T(8,128)(2,1)}) custom-call(s32[2]{0:T(128)} %pad_add_fusion.1.rows, bf16[4,1024,2048]{2,1,0:T(8,128)(2,1)} %x_ref.3, f32[1,2048]{1,0:T(1,128)} %bitcast.42, f32[1,2048]{1,0:T(1,128)} %bitcast.44, bf16[2048,1536]{1,0:T(8,128)(2,1)} %w_ref.3, ...), custom_call_target="tpu_custom_call" | custom-call | flops 12884901888 | bytes 20971520 | tf_op jit(solution)/shard_map/qkv_rope_far/pallas_call | solution.py:83
  31.6 28.1 %attend.1 = (f32[4,1024,128]{2,1,0:T(8,128)}, f32[8,1024]{1,0:T(8,128)}, f32[4,1024,128]{2,1,0:T(8,128)}, f32[8,1024]{1,0:T(8,128)}) custom-call(s32[7]{0:T(128)} %get-tuple-element.49.meta, bf16[2,4,1024,128]{3,2,1,0:T(8,128)(2,1)} %get-tuple-element.23.q_ref, bf16[4,4,1024,128]{3,2,1,0:T(8,128)(2,1)} %k_ref.3, bf16[4,4,1024,128]{3,2,1,0:T(8,128)(2,1)} %v_ref.3), custom_call_target="tpu_custom_call" | custom-call | flops 8589934592 | bytes 12582912 | tf_op jit(solution)/shard_map/attend/pallas_call | solution.py:211
  59.7 0.0 copy-start.5
  59.7 0.0 copy-start.8
  59.7 0.0 copy-start.9
  59.7 0.1 collective-permute-start
  59.8 0.5 collective-permute-start.1
  60.3 2.8 convert_reduce_fusion
  63.1 3.4 fusion.4
  66.6 0.0 copy-done.5
  66.6 0.0 copy-done.8
  66.6 0.0 copy-done.9
  66.6 32.6 %fusion.13 = bf16[1024,2048]{1,0:T(8,128)(2,1)} fusion(f32[2048]{0:T(1024)S(1)} %convert_element_type.39, bf16[2048,2048]{1,0:T(8,128)(2,1)} %param.28, f32[2048]{0:T(1024)S(1)} %copy-done.8, f32[2048]{0:T(1024)S(1)} %copy-done.9, f32[1024]{0:T(1024)S(1)} %add_rsqrt_fusion, f32[1024]{0:T(1024)S(1)} %broadcast_multiply_fusion, ...), kind=kOutput, calls=%fused_computation.16 | convolution fusion | flops 8740929536 | bytes 16809988 | tf_op jit(solution)/shard_map/dot_general | solution.py:512
  99.2 0.6 pad_add_fusion.rows
  99.8 0.0 copy-start.6
  99.8 0.0 copy-start.7
  99.8 0.0 copy-start.4
  99.8 24.9 %qkv_rope_near.1 = (bf16[2,4,1024,128]{3,2,1,0:T(8,128)(2,1)}, bf16[4,4,1024,128]{3,2,1,0:T(8,128)(2,1)}, bf16[4,4,1024,128]{3,2,1,0:T(8,128)(2,1)}) custom-call(s32[2]{0:T(128)} %pad_add_fusion.rows, bf16[4,1024,2048]{2,1,0:T(8,128)(2,1)} %x_ref.3, f32[1,2048]{1,0:T(1,128)} %bitcast.43, ...), custom_call_target="tpu_custom_call", output_to_operand_aliasing={{1}: (7, {}), {2}: (8, {})} | custom-call | flops 12884901888 | bytes 20971520 | tf_op jit(solution)/shard_map/qkv_rope_near/pallas_call | solution.py:83
  124.7 0.0 copy-done.6
  124.7 0.0 copy-done.7
  124.7 0.0 collective-permute-done
  124.8 0.0 copy-done.4
  124.8 0.0 collective-permute-done.1
  124.8 3.8 multiply_add_fusion
  128.6 0.0 collective-permute-start.3
  128.6 2.0 collective-permute-start.5
  130.6 49.0 %attend_own.1 = (f32[4,1024,128]{2,1,0:T(8,128)}, f32[8,1024]{1,0:T(8,128)}, f32[4,1024,128]{2,1,0:T(8,128)}, f32[8,1024]{1,0:T(8,128)}) custom-call(s32[7]{0:T(128)} %get-tuple-element.48.meta, bf16[2,4,1024,128]{3,2,1,0:T(8,128)(2,1)} %get-tuple-element.28.q_ref, bf16[4,4,1024,128]{3,2,1,0:T(8,128)(2,1)} %k_ref.3, bf16[4,4,1024,128]{3,2,1,0:T(8,128)(2,1)} %v_ref.3, ...), custom_call_target="tpu_custom_call" | custom-call | flops 10737418240 | bytes 12582912 | tf_op jit(solution)/shard_map/attend_own/pallas_call | solution.py:211
  179.6 0.0 collective-permute-start.2
  179.7 0.0 copy-start.3
  179.7 0.0 copy-start.2
  179.7 0.5 collective-permute-start.4
  180.2 13.3 %fusion.10 = f32[1024,2048]{1,0:T(8,128)S(1)} fusion(f32[2048]{0:T(1024)S(1)} %convert_element_type.42, f32[2048]{0:T(1024)S(1)} %convert_element_type.41, pred[]{:T(512)S(6)} %eq.3, bf16[1024,2048]{1,0:T(8,128)(2,1)} %fusion.13, bf16[2048,2048]{1,0:T(8,128)(2,1)} %param.30, bf16[4,1024,2048]{2,1,0:T(8,128)(2,1)} %x_ref.3, s32[]{:T(128)S(6)} %select_n.12), kind=kOutput, calls=%fused_computation.13 | convolution fusion | flops 8600420352 | bytes 25182212 | tf_op jit(solution)/shard_map/dot_general | solution.py:515
  193.4 0.0 collective-permute-done.3
  193.5 0.0 collective-permute-done.2
  193.5 0.0 copy-done.3
  193.5 0.0 collective-permute-done.5
  193.5 0.0 collective-permute-done.4
  193.5 0.0 copy-done
  193.5 0.0 copy-done.2
  193.6 7.6 %bitcast_add_fusion.part = f32[1024,2048]{1,0:T(8,128)} fusion(f32[1024,2048]{1,0:T(8,128)S(1)} %fusion.10, bf16[4,128,2048]{2,1,0:T(8,128)(2,1)S(1)} %bitcast.41, f32[4,1024,128]{2,1,0:T(8,128)} %collective-permute-done.5, f32[4,1024,128]{2,1,0:T(8,128)S(1)} %collective-permute-done.4, f32[4,1024,128]{2,1,0:T(8,128)S(1)} %copy-done.2, ...), kind=kOutput, calls=%fused_computation.17 | convolution fusion | flops 2153250816 | bytes 25231360 | tf_op jit(solution)/shard_map/hcd,hde->ce/dot_general | solution.py:520
  201.1 208.4 %share.1 = bf16[4,1024,2048]{2,1,0:T(8,128)(2,1)} custom-call(f32[1024,2048]{1,0:T(8,128)} %bitcast_add_fusion.part), custom_call_target="tpu_custom_call" | custom-call | flops 99999997952 | bytes 33554432 | tf_op jit(solution)/shard_map/share/pallas_call | solution.py:465
  409.6 0.0 copy-start.1
  409.6 14.3 %copy.24 = bf16[4,1024,2048]{2,1,0:T(8,128)(2,1)} copy(bf16[4,1024,2048]{2,1,0:T(8,128)(2,1)} %share.1) | data formatting | bytes 33554432
  423.9 0.0 copy-done.1
  (9 shorter events, 0.1 us)
Async XLA Ops:
  0.6 192.9 %copy-start = (bf16[512,2048]{1,0:T(8,128)(2,1)S(1)}, bf16[512,2048]{1,0:T(8,128)(2,1)}, u32[]{:S(2)}) copy-start(bf16[512,2048]{1,0:T(8,128)(2,1)} %param.26) | copy-start | bytes 6291460
  59.7 6.8 %copy-start.5 = (bf16[2048]{0:T(1024)(128)(2,1)S(1)}, bf16[2048]{0:T(1024)(128)(2,1)}, u32[]{:S(2)}) copy-start(bf16[2048]{0:T(1024)(128)(2,1)} %param.29) | copy-start | bytes 12292
  59.7 6.9 %copy-start.8 = (f32[2048]{0:T(1024)S(1)}, f32[2048]{0:T(1024)}, u32[]{:S(2)}) copy-start(f32[2048]{0:T(1024)} %param.23) | copy-start | bytes 24580
  59.7 6.9 %copy-start.9 = (f32[2048]{0:T(1024)S(1)}, f32[2048]{0:T(1024)}, u32[]{:S(2)}) copy-start(f32[2048]{0:T(1024)} %param.22) | copy-start | bytes 24580
  59.7 65.0 %collective-permute-start = (f32[8,1024]{1,0:T(8,128)}, f32[8,1024]{1,0:T(8,128)S(1)}, u32[]{:S(2)}, u32[]{:S(2)}) collective-permute-start(f32[8,1024]{1,0:T(8,128)} %get-tuple-element.26), channel_id=1, source_target_pairs={{0,1},{1,0},{2,3},{3,2},{4,5},{5,4},{6,7},{7,6},{8,9},{9,8},{10,11... | collective-permute-start | bytes 98312 | tf_op jit(solution)/shard_map/ppermute | solution.py:500
  59.8 65.0 %collective-permute-start.1 = (f32[4,1024,128]{2,1,0:T(8,128)}, f32[4,1024,128]{2,1,0:T(8,128)}, u32[]{:S(2)}, u32[]{:S(2)}) collective-permute-start(f32[4,1024,128]{2,1,0:T(8,128)} %get-tuple-element.27), channel_id=1, source_target_pairs={{0,1},{1,0},{2,3},{3,2},{4,5},{5,4},{6,7},{7,6},{8,9},{9,8},{10,11... | collective-permute-start | bytes 6291464 | tf_op jit(solution)/shard_map/ppermute | solution.py:500
  99.8 24.9 %copy-start.6 = (bf16[2048]{0:T(1024)(128)(2,1)S(1)}, bf16[2048]{0:T(1024)(128)(2,1)}, u32[]{:S(2)}) copy-start(bf16[2048]{0:T(1024)(128)(2,1)} %param.27) | copy-start | bytes 12292
  99.8 24.9 %copy-start.7 = (bf16[2048]{0:T(1024)(128)(2,1)S(1)}, bf16[2048]{0:T(1024)(128)(2,1)}, u32[]{:S(2)}) copy-start(bf16[2048]{0:T(1024)(128)(2,1)} %param.31) | copy-start | bytes 12292
  99.8 24.9 %copy-start.4 = (f32[8,1024]{1,0:T(8,128)S(1)}, f32[8,1024]{1,0:T(8,128)}, u32[]{:S(2)}) copy-start(f32[8,1024]{1,0:T(8,128)} %get-tuple-element.25) | copy-start | bytes 98308
  128.6 64.8 %collective-permute-start.3 = (f32[8,1024]{1,0:T(8,128)S(1)}, f32[8,1024]{1,0:T(8,128)S(1)}, u32[]{:S(2)}, u32[]{:S(2)}) collective-permute-start(f32[8,1024]{1,0:T(8,128)S(1)} %pad_maximum_fusion.1), channel_id=1, source_target_pairs={{0,2},{1,3},{2,0},{3,1},{4,6},{5,7},{6,4},{7,5},{8,10},{9,11},{10,... | collective-permute-start | bytes 98312 | tf_op jit(solution)/shard_map/ppermute | solution.py:505
  128.6 64.9 %collective-permute-start.5 = (f32[4,1024,128]{2,1,0:T(8,128)}, f32[4,1024,128]{2,1,0:T(8,128)}, u32[]{:S(2)}, u32[]{:S(2)}) collective-permute-start(f32[4,1024,128]{2,1,0:T(8,128)} %multiply_add_fusion), channel_id=1, source_target_pairs={{0,2},{1,3},{2,0},{3,1},{4,6},{5,7},{6,4},{7,5},{8,10},{9,11},{10,... | collective-permute-start | bytes 6291464 | tf_op jit(solution)/shard_map/ppermute | solution.py:505
  179.6 13.8 %collective-permute-start.2 = (f32[8,1024]{1,0:T(8,128)}, f32[8,1024]{1,0:T(8,128)S(1)}, u32[]{:S(2)}, u32[]{:S(2)}) collective-permute-start(f32[8,1024]{1,0:T(8,128)} %get-tuple-element.33), channel_id=1, source_target_pairs={{0,1},{1,0},{2,3},{3,2},{4,5},{5,4},{6,7},{7,6},{8,9},{9,8},{10,11... | collective-permute-start | bytes 98312 | tf_op jit(solution)/shard_map/ppermute | solution.py:508
  179.7 13.8 %copy-start.3 = (f32[8,1024]{1,0:T(8,128)S(1)}, f32[8,1024]{1,0:T(8,128)}, u32[]{:S(2)}) copy-start(f32[8,1024]{1,0:T(8,128)} %get-tuple-element.32) | copy-start | bytes 98308
  179.7 13.9 %copy-start.2 = (f32[4,1024,128]{2,1,0:T(8,128)S(1)}, f32[4,1024,128]{2,1,0:T(8,128)}, u32[]{:S(2)}) copy-start(f32[4,1024,128]{2,1,0:T(8,128)} %get-tuple-element.31) | copy-start | bytes 6291460
  179.7 13.9 %collective-permute-start.4 = (f32[4,1024,128]{2,1,0:T(8,128)}, f32[4,1024,128]{2,1,0:T(8,128)S(1)}, u32[]{:S(2)}, u32[]{:S(2)}) collective-permute-start(f32[4,1024,128]{2,1,0:T(8,128)} %get-tuple-element.35), channel_id=1, source_target_pairs={{0,1},{1,0},{2,3},{3,2},{4,5},{5,4},{6,7},{7,6},{8,9},{9,8},{10,11... | collective-permute-start | bytes 6291464 | tf_op jit(solution)/shard_map/ppermute | solution.py:508
  409.6 14.3 %copy-start.1 = (bf16[512,2048]{1,0:T(8,128)(2,1)S(1)}, bf16[512,2048]{1,0:T(8,128)(2,1)}, u32[]{:S(2)}) copy-start(bf16[512,2048]{1,0:T(8,128)(2,1)} %param.26) | copy-start | bytes 6291460

commit v3 on v2

--- a/solution.py
+++ b/solution.py
@@ -17,8 +17,12 @@
 F32 = jnp.float32
 BF16 = jnp.bfloat16
 VMEM_LIMIT = 60 * 1024 * 1024
+SHARE_LIMIT = 67_043_328
 CHUNKS = 64
 STAGES = 4
+BLOCKS = 8
+SLICES = 4
+LAG_START = 2
 LAG_AHEAD = 1
 LAG_BACK = 1
 LAG_CORE = 2
@@ -108,54 +112,80 @@
     )(rows, hidden_in, gain[None], bias[None], w_qkv, b_qkv.astype(F32)[None], table, *filled)
 
 
+def wide(column, lanes):
+    return jnp.concatenate([column] * (lanes // column.shape[1]), axis=1)
+
+
+def scores_of(query, keys, scale, mask):
+    scores = lax.dot_general(query, keys, (((1,), (1,)), ((), ())), preferred_element_type=F32) * scale
+    return scores if mask is None else jnp.where(mask, scores, NEG_BIG)
+
+
+def lane_sum(values, lanes):
+    return functools.reduce(jnp.add, [values[:, n:n + lanes] for n in range(0, values.shape[1], lanes)])
+
+
+def lane_max(values, lanes):
+    return functools.reduce(jnp.maximum, [values[:, n:n + lanes] for n in range(0, values.shape[1], lanes)])
+
+
+def first_step(heads, scale, q_of, k_of, v_of, m_scr, l_scr, o_scr, mask):
+    for h in range(heads):
+        lanes = o_scr.shape[2]
+        scores = scores_of(q_of(h), k_of(h), scale, mask)
+        peak = jnp.broadcast_to(jnp.max(lane_max(scores, lanes), axis=1, keepdims=True), m_scr.shape[1:])
+        probs = jnp.exp2(scores - wide(peak, scores.shape[1]))
+        m_scr[h] = peak
+        l_scr[h] = lane_sum(probs, lanes)
+        o_scr[h] = jnp.dot(probs.astype(BF16), v_of(h), preferred_element_type=F32)
+
+
 def block_step(heads, scale, q_of, k_of, v_of, m_scr, l_scr, o_scr, mask):
     for h in range(heads):
-        scores = lax.dot_general(q_of(h), k_of(h), (((1,), (1,)), ((), ())), preferred_element_type=F32) * scale
-        if mask is not None:
-            scores = jnp.where(mask, scores, NEG_BIG)
+        lanes = o_scr.shape[2]
+        scores = scores_of(q_of(h), k_of(h), scale, mask)
         m_old = m_scr[h]
-        m_new = jnp.maximum(m_old, jnp.max(scores, axis=1, keepdims=True))
-        probs = jnp.exp2(scores - m_new[:, :1])
+        m_new = jnp.maximum(m_old, jnp.max(lane_max(scores, lanes), axis=1, keepdims=True))
+        probs = jnp.exp2(scores - wide(m_new, scores.shape[1]))
         shrink = jnp.exp2(m_old - m_new)
-        l_scr[h] = l_scr[h] * shrink + jnp.sum(probs, axis=1, keepdims=True)
+        l_scr[h] = l_scr[h] * shrink + lane_sum(probs, lanes)
         m_scr[h] = m_new
         o_scr[h] = o_scr[h] * shrink + jnp.dot(probs.astype(BF16), v_of(h), preferred_element_type=F32)
 
 
-def attn_kernel(heads, head_dim, q_tile, key_block, with_self, meta, q_ref, k_ref, v_ref, *rest):
+def attn_kernel(heads, head_dim, q_tile, with_self, meta, q_ref, k_ref, v_ref, *rest):
     if with_self:
         kn_ref, vn_ref, *rest = rest
     os_ref, ss_ref, ok_ref, sk_ref, m_scr, l_scr, o_scr = rest
     slot = pl.program_id(0)
     tile = pl.program_id(1)
-    valid = jnp.clip(meta[3 + meta[slot]] - meta[2], 0, k_ref.shape[2])
+    block_len = k_ref.shape[2]
+    half = block_len // 2
+    valid = jnp.clip(meta[3 + meta[slot]] - meta[2], 0, block_len)
     scale = head_dim ** -0.5 * LOG2E
-    m_scr[...] = jnp.full(m_scr.shape, NEG_BIG, F32)
-    l_scr[...] = jnp.zeros(l_scr.shape, F32)
-    o_scr[...] = jnp.zeros(o_scr.shape, F32)
 
     def query(h):
         return q_ref[0, h]
 
-    def cache_block(block, mask):
-        start = pl.multiple_of(block * key_block, key_block)
-        block_step(
-            heads, scale, query,
-            lambda h: k_ref[0, h, pl.ds(start, key_block), :],
-            lambda h: v_ref[0, h, pl.ds(start, key_block), :],
-            m_scr, l_scr, o_scr, mask,
+    def cache_block(size):
+        mask = lax.broadcasted_iota(jnp.int32, (q_tile, size), 1) < valid
+        first_step(
+            heads, scale, query, lambda h: k_ref[0, h, :size, :], lambda h: v_ref[0, h, :size, :], m_scr, l_scr, o_scr, mask
         )
 
-    whole = lax.div(valid, key_block)
-
-    @pl.loop(0, whole)
-    def _(block):
-        cache_block(block, None)
-
-    @pl.when(lax.rem(valid, key_block) > 0)
-    def _():
-        keys = whole * key_block + lax.broadcasted_iota(jnp.int32, (q_tile, key_block), 1)
-        cache_block(whole, keys < valid)
+    @pl.when(valid == 0)
+    def _():
+        m_scr[...] = jnp.full(m_scr.shape, NEG_BIG, F32)
+        l_scr[...] = jnp.zeros(l_scr.shape, F32)
+        o_scr[...] = jnp.zeros(o_scr.shape, F32)
+
+    @pl.when(jnp.logical_and(valid > 0, valid <= half))
+    def _():
+        cache_block(half)
+
+    @pl.when(valid > half)
+    def _():
+        cache_block(block_len)
 
     if with_self:
         def own_block(block, mask):
@@ -180,7 +210,7 @@
     stats = jnp.zeros((q_tile, head_dim), F32)
     for h in range(heads):
         stats = jnp.where(lane == h, m_scr[h], stats)
-        stats = jnp.where(lane == heads + h, l_scr[h], stats)
+        stats = jnp.where(lane == heads + h, jnp.sum(l_scr[h], axis=1, keepdims=True), stats)
     stats = stats.T[:8]
 
     @pl.when(slot == 0)
@@ -198,7 +228,6 @@
     heads, chunk_len, head_dim = q_rows.shape[1:]
     block_len = k_block.shape[2]
     q_tile = chunk_len // 4
-    key_block = block_len // 2
     tiles = chunk_len // q_tile
     meta = jnp.concatenate([rows, block_start[None], lengths])
     with_self = k_new is not None
@@ -209,7 +238,7 @@
     o_shape = jax.ShapeDtypeStruct((heads, chunk_len, head_dim), F32)
     s_shape = jax.ShapeDtypeStruct((8, chunk_len), F32)
     return pl.pallas_call(
-        functools.partial(attn_kernel, heads, head_dim, q_tile, key_block, with_self),
+        functools.partial(attn_kernel, heads, head_dim, q_tile, with_self),
         grid_spec=pltpu.PrefetchScalarGridSpec(
             num_scalar_prefetch=1,
             grid=(2, tiles),
@@ -242,16 +271,47 @@
     return out, peak, total
 
 
-def share_kernel(tp_size, part, out_ref, acc, from_left, from_right, from_y, from_core, from_last, stage,
-                 in_sem, left_sem, right_sem, y_sem, core_sem, last_sem, send_sem, stage_sem):
+def share_kernel(tp_size, heads, hidden, o_own, o_core, o_far, s_own, s_core, s_far, gain_ref, bias_ref, w_up, b_up_ref,
+                 w_down, w_out, extra_ref, out_ref, core_box, last_box,
+                 acc, from_left, from_right, from_y, up, down, proj, x_buf, o_buf, s_buf, m_buf, c_buf, stage, land,
+                 up_sem, down_sem, proj_sem, x_sem, o_sem, s_sem,
+                 left_sem, right_sem, y_sem, core_sem, last_sem, send_sem, stage_sem, land_sem):
     z = lax.axis_index("tp")
     j = lax.axis_index("cp")
     y, c = lax.div(j, 2), lax.rem(j, 2)
     across, mate, corner = (1 - y) * 2 + c, y * 2 + (1 - c), (1 - y) * 2 + (1 - c)
-    tokens = part.shape[0] // CHUNKS
+    chunk_len, d_model = acc.shape
+    head_dim = o_own.shape[2]
+    tokens = chunk_len // CHUNKS
+    block = chunk_len // BLOCKS
     pairs = CHUNKS // 2
+    per_block = pairs // BLOCKS
+    width = up.shape[2]
     last = tp_size - 1
     root_a, root_b = (tp_size - 1) // 2, tp_size // 2
+
+
+    def weight_copies(f):
+        cols = pl.ds(f * width, width)
+        return (pltpu.make_async_copy(w_up.at[:, cols], up.at[f], up_sem.at[f]),
+                pltpu.make_async_copy(w_down.at[cols, :], down.at[f], down_sem.at[f]))
+
+    def block_copies(b):
+        rows = pl.ds(pl.multiple_of(b * block, block), block)
+        slot = lax.rem(b, 2)
+        copies = [pltpu.make_async_copy(hidden.at[j, rows, :], x_buf.at[slot], x_sem.at[slot])]
+        for n, (o_ref, s_ref) in enumerate(((o_own, s_own), (o_core, s_core), (o_far, s_far))):
+            copies.append(pltpu.make_async_copy(o_ref.at[:, rows, :], o_buf.at[slot, n], o_sem.at[slot, n]))
+            copies.append(pltpu.make_async_copy(s_ref.at[:, rows], s_buf.at[slot, n], s_sem.at[slot, n]))
+        return copies
+
+    for copy in block_copies(0):
+        copy.start()
+    proj_copy = pltpu.make_async_copy(w_out, proj, proj_sem)
+    proj_copy.start()
+    for f in range(SLICES):
+        for copy in weight_copies(f):
+            copy.start()
 
     barrier = pltpu.get_barrier_semaphore()
     pl.semaphore_signal(barrier, inc=1, device_id={"cp": across}, device_id_type=MESH)
@@ -275,11 +335,57 @@
     def _():
         pl.semaphore_wait(barrier, 3)
 
+
+    def begin(b):
+        slot = lax.rem(b, 2)
+        rows = pl.ds(pl.multiple_of(b * block, block), block)
+
+        @pl.when(b + 1 < BLOCKS)
+        def _():
+            for copy in block_copies(b + 1):
+                copy.start()
+
+        for copy in block_copies(b):
+            copy.wait()
+
+        @pl.when(b == 0)
+        def _():
+            proj_copy.wait()
+
+        maxima = [s_buf[slot, n, :heads, :] for n in range(3)]
+        peak = jnp.maximum(jnp.maximum(maxima[0], maxima[1]), maxima[2])
+        weights = [jnp.exp2(m - peak) for m in maxima]
+        total = functools.reduce(jnp.add, [s_buf[slot, n, heads:2 * heads, :] * w for n, w in enumerate(weights)])
+        shares = [w / total for w in weights]
+        spare = jnp.zeros((head_dim - 3 * heads, block), F32)
+        columns = jnp.concatenate(shares + [spare], axis=0).T
+        for h in range(heads):
+            context = functools.reduce(
+                jnp.add, [o_buf[slot, n, h] * columns[:, n * heads + h:n * heads + h + 1] for n in range(3)])
+            c_buf[:, h * head_dim:(h + 1) * head_dim] = context.astype(BF16)
+        x = x_buf[slot]
+        m_buf[...] = layer_norm(x, gain_ref[...], bias_ref[...])
+        acc[rows, :] = jnp.dot(c_buf[...], proj[...], preferred_element_type=F32)
+
+        @pl.when(z == 0)
+        def _():
+            acc[rows, :] += x.astype(F32) + extra_ref[...]
+
+    def slice_of(b, f):
+        rows = pl.ds(pl.multiple_of(b * block, block), block)
+
+        @pl.when(b == 0)
+        def _():
+            for copy in weight_copies(f):
+                copy.wait()
+
+        wide_h = jnp.dot(m_buf[...], up[f], preferred_element_type=F32) + b_up_ref[f]
+        act = (0.5 * wide_h * (1.0 + lax.erf(wide_h * math.sqrt(0.5)))).astype(BF16)
+        acc[rows, :] += jnp.dot(act, down[f], preferred_element_type=F32)
+
+
     def at(ref, k):
         return ref.at[pl.ds(pl.multiple_of(k * tokens, tokens), tokens), :]
-
-    def load(k):
-        return pltpu.make_async_copy(at(part, k), at(acc, k), in_sem.at[k])
 
     def remote(src, dst, k, which, arrive, device):
         return pltpu.make_async_remote_copy(
@@ -299,7 +405,7 @@
     def drained(ref, which):
         pltpu.make_async_copy(ref, ref, send_sem.at[which]).wait()
 
-    def emit(stream, src, k, row):
+    def emit(stream, values, k, row):
         slot = lax.rem(k, STAGES)
 
         def copy():
@@ -309,14 +415,20 @@
         def _():
             copy().wait()
 
-        rows = pl.ds(pl.multiple_of(k * tokens, tokens), tokens)
-        stage[stream, slot] = src[rows, :].astype(BF16)
+        stage[stream, slot] = values.astype(BF16)
         copy().start()
+
+    def chunk(ref, k):
+        return ref[pl.ds(pl.multiple_of(k * tokens, tokens), tokens), :]
 
     def finish(src, k):
         remote(src, from_y, k, 2, y_sem, {"cp": across}).start()
-        remote(src, from_core, k, 3, core_sem, {"cp": mate}).start()
-        emit(0, src, k, j)
+        remote(src, core_box, k, 3, core_sem, {"cp": mate}).start()
+        emit(0, chunk(src, k), k, j)
+
+    def landing(n, box, k):
+        slot = lax.rem(k, STAGES)
+        return pltpu.make_async_copy(at(box, k), land.at[n, slot], land_sem.at[n, slot])
 
     def gathered(i):
         def lagged(lag, act):
@@ -326,18 +438,28 @@
                     act((i - lag) * 2 + n)
 
         def core(k):
-            arrived(from_core, core_sem, k)
-            emit(1, from_core, k, mate)
+            arrived(core_box, core_sem, k)
+            landing(0, core_box, k).start()
+
+        def core_out(k):
+            landing(0, core_box, k).wait()
+            emit(1, land[0, lax.rem(k, STAGES)], k, mate)
 
         def side(k):
             arrived(from_y, y_sem, k)
-            remote(from_y, from_last, k, 4, last_sem, {"cp": mate}).start()
-            emit(2, from_y, k, across)
+            remote(from_y, last_box, k, 4, last_sem, {"cp": mate}).start()
+            emit(2, chunk(from_y, k), k, across)
 
         def final(k):
-            arrived(from_last, last_sem, k)
-            emit(3, from_last, k, corner)
-
+            arrived(last_box, last_sem, k)
+            landing(1, last_box, k).start()
+
+        def final_out(k):
+            landing(1, last_box, k).wait()
+            emit(3, land[1, lax.rem(k, STAGES)], k, corner)
+
+        lagged(LAG_CORE + 1, core_out)
+        lagged(LAG_LAST + 1, final_out)
         lagged(LAG_CORE, core)
         lagged(LAG_Y, side)
         lagged(LAG_LAST, final)
@@ -349,50 +471,23 @@
             total = total + other[rows, :]
         acc[rows, :] = total
 
-    @pl.loop(0, CHUNKS)
-    def _(k):
-        load(k).start()
-
-    steps = pairs + LAG_LAST + 1
-
-    def run(near, far, early=None):
-        if early is not None:
-            for i in range(LAG_AHEAD):
-                early(i)
-
-        @pl.loop(0, steps)
-        def _(i):
-            if early is not None:
-                @pl.when(i + LAG_AHEAD < pairs)
-                def _():
-                    early(i + LAG_AHEAD)
-
-            @pl.when(i < pairs)
-            def _():
-                near(i)
-
-            @pl.when(jnp.logical_and(i >= LAG_BACK, i < pairs + LAG_BACK))
-            def _():
-                far(i - LAG_BACK)
-
-            gathered(i)
-
-    def end(first, send):
+    def when(cond, act, *args):
+        @pl.when(cond)
+        def _():
+            act(*args)
+
+    def end(i, first):
         inbox, sem = (from_right, right_sem) if first else (from_left, left_sem)
-
-        @pl.loop(0, CHUNKS)
-        def _(k):
-            load(k).wait()
-            send(acc, k)
+        near_bit = 0 if first else 1
 
         def got(k):
             arrived(inbox, sem, k)
             finish(inbox, k)
 
-        near_bit = 0 if first else 1
-        run(lambda i: got(2 * i + near_bit), lambda i: got(2 * i + 1 - near_bit))
-
-    def inner(left_side):
+        when(jnp.logical_and(i >= 0, i < pairs), lambda: got(2 * i + near_bit))
+        when(jnp.logical_and(i >= LAG_BACK, i < pairs + LAG_BACK), lambda: got(2 * (i - LAG_BACK) + 1 - near_bit))
+
+    def inner(i, left_side):
         mine = 0 if left_side else 1
         if left_side:
             (outer, outer_sem, to_outer), (inward, inward_sem, to_inner) = (
@@ -401,16 +496,14 @@
             (outer, outer_sem, to_outer), (inward, inward_sem, to_inner) = (
                 (from_right, right_sem, send_right), (from_left, left_sem, send_left))
 
-        def early(i):
-            passed = 2 * i + 1 - mine
-            load(passed).wait()
+        def early(p):
+            passed = 2 * p + 1 - mine
             arrived(outer, outer_sem, passed)
             add(passed, outer)
             to_inner(acc, passed)
 
-        def near(i):
-            rooted = 2 * i + mine
-            load(rooted).wait()
+        def near(p):
+            rooted = 2 * p + mine
             arrived(outer, outer_sem, rooted)
             arrived(inward, inward_sem, rooted)
             add(rooted, from_left, from_right)
@@ -418,29 +511,40 @@
             to_inner(acc, rooted)
             finish(acc, rooted)
 
-        def far(i):
-            k = 2 * i + 1 - mine
+        def far(p):
+            k = 2 * p + 1 - mine
             arrived(inward, inward_sem, k)
             to_outer(inward, k)
             finish(inward, k)
 
-        run(near, far, early)
-
-    @pl.when(z == 0)
-    def _():
-        end(True, send_right)
-
-    @pl.when(z == root_a)
-    def _():
-        inner(True)
-
-    @pl.when(z == root_b)
-    def _():
-        inner(False)
-
-    @pl.when(z == last)
-    def _():
-        end(False, send_left)
+        when(jnp.logical_and(i + LAG_AHEAD >= 0, i + LAG_AHEAD < pairs), early, i + LAG_AHEAD)
+        when(jnp.logical_and(i >= 0, i < pairs), near, i)
+        when(jnp.logical_and(i >= LAG_BACK, i < pairs + LAG_BACK), far, i - LAG_BACK)
+
+    lead = SLICES + LAG_START
+
+    @pl.loop(0, lead + pairs + LAG_LAST + 2)
+    def _(s):
+        @pl.when(s < BLOCKS * SLICES)
+        def _():
+            b, f = lax.div(s, SLICES), lax.rem(s, SLICES)
+            when(f == 0, begin, b)
+            slice_of(b, f)
+
+            def push(send):
+                @pl.loop(0, 2 * per_block)
+                def _(n):
+                    send(acc, b * 2 * per_block + n)
+
+            when(jnp.logical_and(f == SLICES - 1, z == 0), push, send_right)
+            when(jnp.logical_and(f == SLICES - 1, z == last), push, send_left)
+
+        i = s - lead
+        when(z == 0, end, i, True)
+        when(z == root_a, inner, i, True)
+        when(z == root_b, inner, i, False)
+        when(z == last, end, i, False)
+        gathered(i)
 
     @pl.when(z < last)
     def _():
@@ -457,24 +561,51 @@
             pltpu.make_async_copy(stage.at[stream, slot], at(out_ref.at[0], 0), stage_sem.at[stream, slot]).wait()
 
 
-def share(part, num_rows, tp_size):
-    chunk_len, d_model = part.shape
+def share(pieces, hidden_in, gain, bias, w_up, b_up, w_down, w_out, extra, tp_size):
+    (o_own, s_own), (o_core, s_core), (o_far, s_far) = pieces
+    num_rows, chunk_len, d_model = hidden_in.shape
+    heads, _, head_dim = o_own.shape
+    ff = w_up.shape[1]
+    width = ff // SLICES
     tokens = chunk_len // CHUNKS
+    block = chunk_len // BLOCKS
     buffer = pltpu.VMEM((chunk_len, d_model), F32)
+    box = jax.ShapeDtypeStruct((chunk_len, d_model), F32)
     arrivals = pltpu.SemaphoreType.DMA((CHUNKS,))
-    return pl.pallas_call(
-        functools.partial(share_kernel, tp_size),
-        in_specs=[pl.BlockSpec(memory_space=pl.ANY)],
-        out_specs=pl.BlockSpec(memory_space=pl.ANY),
-        out_shape=jax.ShapeDtypeStruct((num_rows, chunk_len, d_model), BF16),
-        scratch_shapes=[buffer] * 6
-        + [pltpu.VMEM((4, STAGES, tokens, d_model), BF16)]
-        + [arrivals] * 6
-        + [pltpu.SemaphoreType.DMA((5,)), pltpu.SemaphoreType.DMA((4, STAGES))],
-        compiler_params=pltpu.CompilerParams(collective_id=0, has_side_effects=True, vmem_limit_bytes=VMEM_LIMIT),
+    hbm = pl.BlockSpec(memory_space=pl.ANY)
+    vmem = pl.BlockSpec(memory_space=pltpu.VMEM)
+    out, _, _ = pl.pallas_call(
+        functools.partial(share_kernel, tp_size, heads),
+        in_specs=[hbm] * 7 + [vmem, vmem, hbm, vmem, hbm, hbm, vmem],
+        out_specs=[hbm] * 3,
+        out_shape=[jax.ShapeDtypeStruct((num_rows, chunk_len, d_model), BF16), box, box],
+        scratch_shapes=[buffer] * 4
+        + [
+            pltpu.VMEM((SLICES, d_model, width), BF16),
+            pltpu.VMEM((SLICES, width, d_model), BF16),
+            pltpu.VMEM((heads * head_dim, d_model), BF16),
+            pltpu.VMEM((2, block, d_model), BF16),
+            pltpu.VMEM((2, 3, heads, block, head_dim), F32),
+            pltpu.VMEM((2, 3, 8, block), F32),
+            pltpu.VMEM((block, d_model), BF16),
+            pltpu.VMEM((block, heads * head_dim), BF16),
+            pltpu.VMEM((4, STAGES, tokens, d_model), BF16),
+            pltpu.VMEM((2, STAGES, tokens, d_model), F32),
+            pltpu.SemaphoreType.DMA((SLICES,)),
+            pltpu.SemaphoreType.DMA((SLICES,)),
+            pltpu.SemaphoreType.DMA,
+            pltpu.SemaphoreType.DMA((2,)),
+            pltpu.SemaphoreType.DMA((2, 3)),
+            pltpu.SemaphoreType.DMA((2, 3)),
+        ]
+        + [arrivals] * 5
+        + [pltpu.SemaphoreType.DMA((5,)), pltpu.SemaphoreType.DMA((4, STAGES)), pltpu.SemaphoreType.DMA((2, STAGES))],
+        compiler_params=pltpu.CompilerParams(collective_id=0, has_side_effects=True, vmem_limit_bytes=SHARE_LIMIT),
         cost_estimate=pl.CostEstimate(flops=100_000_000_000, bytes_accessed=chunk_len * d_model * 16, transcendentals=0),
         name="share",
-    )(part)
+    )(hidden_in, o_own, o_core, o_far, s_own, s_core, s_far, gain[None], bias[None], w_up,
+      b_up.astype(F32).reshape(SLICES, 1, width), w_down, w_out, extra[None])
+    return out
 
 
 def solution(mesh):
@@ -498,27 +629,18 @@
         q_far, *filled = project_qkv(far_rows, hidden_in, *weights)
         o_s, s_s, o_k, s_k = attend(far_rows, lengths, start, q_far, k_block, v_block)
         o_r, s_r = lax.ppermute(o_s, "cp", swap_core), lax.ppermute(s_s, "cp", swap_core)
+        o_far, peak, total = merge(heads, [(o_k, s_k), (o_r, s_r)])
+        s_far = jnp.concatenate([peak, total, s_k[2 * heads:]], axis=0)
+        near_rows, o_far, s_far = lax.optimization_barrier((near_rows, o_far, s_far))
+        o_y, s_y = lax.ppermute(o_far, "cp", swap_y), lax.ppermute(s_far, "cp", swap_y)
         q_near, k_new, v_new = project_qkv(near_rows, hidden_in, *weights, filled=filled)
-        o_far, peak, total = merge(heads, [(o_k, s_k), (o_r, s_r)])
-        s_far = jnp.concatenate([peak, total], axis=0)
-        q_near, o_far, s_far = lax.optimization_barrier((q_near, o_far, s_far))
-        o_y, s_y = lax.ppermute(o_far, "cp", swap_y), lax.ppermute(s_far, "cp", swap_y)
 
         o_s, s_s, o_own, s_own = attend(near_rows, lengths, start, q_near, k_block, v_block, k_new, v_new)
         o_c, s_c = lax.ppermute(o_s, "cp", swap_core), lax.ppermute(s_s, "cp", swap_core)
 
-        own_in = lax.dynamic_index_in_dim(hidden_in, j, 0, keepdims=False)
-        normed_mlp = layer_norm(own_in, ln2_gain, ln2_bias)
-        hidden = jax.nn.gelu(jnp.dot(normed_mlp, w_up, preferred_element_type=F32) + b_up.astype(F32), approximate=False).astype(BF16)
-        hidden = lax.optimization_barrier(hidden)
-        extra = own_in.astype(F32) + b_out.astype(F32) + b_down.astype(F32)
-        mlp_part = jnp.dot(hidden, w_down, preferred_element_type=F32) + jnp.where(lax.axis_index("tp") == 0, extra, 0.0)
-        mlp_part = lax.optimization_barrier(mlp_part)
-
-        out, _, total = merge(heads, [(o_own, s_own), (o_c, s_c), (o_y, s_y)])
-        context = (out / total[..., None]).astype(BF16)
-        attn_part = jnp.einsum("hcd,hde->ce", context, w_out.reshape(heads, head_dim, d_model), preferred_element_type=F32)
-        part = attn_part + mlp_part
-        return share(part, num_rows, tp_size), k_new, v_new
+        pieces = [(o_own, s_own), (o_c, s_c), (o_y, s_y)]
+        extra = b_out.astype(F32) + b_down.astype(F32)
+        out = share(pieces, hidden_in, ln2_gain, ln2_bias, w_up, b_up, w_down, w_out, extra, tp_size)
+        return out, k_new, v_new
 
     return jax.shard_map(local_layer, mesh=mesh, in_specs=in_specs, out_specs=out_specs, check_vma=False)

time: 432 us -> 358 us (0.83); the launches traced: 424 us -> 357 us
  matrix products: 53.5 us -> 0 us
  Pallas kernels: 335 us -> 321 us
  waiting for transfers between devices: 0.02 us -> 6.12 us
  other arithmetic: 15.5 us -> 11 us
    dot_general x3 -> x0, matrix products: 53.5 us -> none  [the longest x1 32.6 us: local_layer(): jnp.dot(normed_mlp, w_up, preferred_element_type=F32) + b_up.astype(F32)]
    pallas_call x3, Pallas kernels: 285 us -> 271 us  [the longest x1 219 us: share(): pl.pallas_call(functools.partial(share_kernel, tp_size, heads), in_specs=...]
    reduce_sum x2 -> x0, other arithmetic: 6.22 us -> none  [the longest x1 3.42 us: layer_norm(): variance = jnp.mean(centered * centered, axis=-1, keepdims=True)]
    unnamed x21 -> x17, local copies, waits for them, and re-layouts: 14.4 us -> 16.1 us
  transfers between devices with their start and end apart: 6 -> 6, of which waited for: 0 -> 3; matrix products, arithmetic and copies ran while one was open for 12% -> 1% of each run, Pallas kernels for 17% -> 15%
where the time goes in v3:
time: 358 us; the launch traced here: 357 us
  Pallas kernels  321 us (90%)
  local copies, waits for them, and re-layouts  17.4 us (5%)
  other arithmetic  11 us (3%)
  waiting for transfers between devices  6.12 us (2%)
    pallas_call x1, Pallas kernels, share(): pl.pallas_call(functools.partial(share_kernel, tp_size, heads), in_specs=...  219 us
    pallas_call x2, Pallas kernels, attend(): pl.pallas_call(functools.partial(attn_kernel, heads, head_dim, q_tile, wi...  51.7 us
    pallas_call x2, Pallas kernels, project_qkv(): pl.pallas_call(functools.partial(qkv_kernel, heads, head_dim), grid_spec=...  49.5 us
    unnamed x17, local copies, waits for them, and re-layouts  16.1 us
  transfers between devices with their start and end apart: 6, of which 3 were waited for; matrix products, arithmetic and copies ran while one was open for 1% of the time, Pallas kernels for 15%

profile of v3, /device:TPU:0, one launch (start us, length us, event | category | flops | bytes accessed | tf_op | source)
XLA Modules:
  0.0 356.8 jit_solution(15707632008832441503)
XLA Ops:
  0.7 0.7 add_convert_fusion
  1.4 0.6 pad_add_fusion.1.rows
  2.0 1.3 add_add_fusion.meta
  3.2 1.3 reshape.38.wb_ref
  4.5 1.0 multiply_cosine_fusion
  5.5 1.1 pad_maximum_fusion.tab_ref
  6.6 24.7 %qkv_rope_far.1 = (bf16[2,4,1024,128]{3,2,1,0:T(8,128)(2,1)}, bf16[4,4,1024,128]{3,2,1,0:T(8,128)(2,1)}, bf16[4,4,1024,128]{3,2,1,0:T(8,128)(2,1)}) custom-call(s32[2]{0:T(128)} %pad_add_fusion.1.rows, bf16[4,1024,2048]{2,1,0:T(8,128)(2,1)} %hidden.1, f32[1,2048]{1,0:T(1,128)} %bitcast.13, f32[1,2048]{1,0:T(1,128)} %bitcast.15, bf16[2048,1536]{1,0:T(8,128)(2,1)} %w_ref.3, ...), custom_call_target="tpu_custom_call" | custom-call | flops 12884901888 | bytes 20971520 | tf_op jit(solution)/shard_map/qkv_rope_far/pallas_call | solution.py:87
  31.4 22.4 %attend.1 = (f32[4,1024,128]{2,1,0:T(8,128)}, f32[8,1024]{1,0:T(8,128)}, f32[4,1024,128]{2,1,0:T(8,128)}, f32[8,1024]{1,0:T(8,128)}) custom-call(s32[7]{0:T(128)} %add_add_fusion.meta, bf16[2,4,1024,128]{3,2,1,0:T(8,128)(2,1)} %get-tuple-element.21.q_ref, bf16[4,4,1024,128]{3,2,1,0:T(8,128)(2,1)} %k_ref.3, bf16[4,4,1024,128]{3,2,1,0:T(8,128)(2,1)} %v_ref.3), custom_call_target="tpu_custom_call" | custom-call | flops 8589934592 | bytes 12582912 | tf_op jit(solution)/shard_map/attend/pallas_call | solution.py:240
  53.8 0.0 collective-permute-start.1
  53.8 0.5 collective-permute-start
  54.3 0.1 pad_add_fusion.rows
  54.4 0.0 copy-start.5
  54.4 3.6 %collective-permute-done = f32[8,1024]{1,0:T(8,128)S(1)} collective-permute-done((f32[8,1024]{1,0:T(8,128)}, f32[8,1024]{1,0:T(8,128)S(1)}, u32[]{:S(2)}, u32[]{:S(2)}) %collective-permute-start) | collective-permute-done | bytes 32800 | tf_op jit(solution)/shard_map/ppermute | solution.py:631
  58.0 0.9 fusion.1
  58.9 0.0 collective-permute-done.1
  58.9 0.0 copy-start
  58.9 1.3 copy-done
  60.2 0.0 copy-start.1
  60.2 3.5 multiply_add_fusion
  63.8 0.0 copy-done.5
  63.8 0.0 copy-done.1
  63.8 0.6 add_add_fusion.1.meta
  64.4 0.0 collective-permute-start.3
  64.4 24.7 %qkv_rope_near.1 = (bf16[2,4,1024,128]{3,2,1,0:T(8,128)(2,1)}, bf16[4,4,1024,128]{3,2,1,0:T(8,128)(2,1)}, bf16[4,4,1024,128]{3,2,1,0:T(8,128)(2,1)}) custom-call(s32[2]{0:T(128)} %copy-done.5, bf16[4,1024,2048]{2,1,0:T(8,128)(2,1)} %hidden.1, f32[1,2048]{1,0:T(1,128)} %bitcast.14, f32[1,2048]{1,0:T(1,128)} %bitcast.16, ...), custom_call_target="tpu_custom_call", output_to_operand_aliasing={{1}: (7, {}), {2}: (8, {})} | custom-call | flops 12884901888 | bytes 20971520 | tf_op jit(solution)/shard_map/qkv_rope_near/pallas_call | solution.py:87
  89.1 0.0 copy-start.3
  89.1 0.0 copy-start.4
  89.2 0.0 copy-start.2
  89.2 29.3 %attend_own.1 = (f32[4,1024,128]{2,1,0:T(8,128)}, f32[8,1024]{1,0:T(8,128)}, f32[4,1024,128]{2,1,0:T(8,128)}, f32[8,1024]{1,0:T(8,128)}) custom-call(s32[7]{0:T(128)} %add_add_fusion.1.meta, bf16[2,4,1024,128]{3,2,1,0:T(8,128)(2,1)} %get-tuple-element.29.q_ref, bf16[4,4,1024,128]{3,2,1,0:T(8,128)(2,1)} %k_ref.3, bf16[4,4,1024,128]{3,2,1,0:T(8,128)(2,1)} %v_ref.3, ...), custom_call_target="tpu_custom_call" | custom-call | flops 10737418240 | bytes 12582912 | tf_op jit(solution)/shard_map/attend_own/pallas_call | solution.py:240
  118.5 0.0 collective-permute-start.2
  118.5 0.1 collective-permute-start.5
  118.5 0.4 collective-permute-start.4
  119.0 0.0 copy-done.3
  119.0 0.0 copy-done.4
  119.0 0.6 convert_add_fusion
  119.6 0.0 copy-done.2
  119.6 0.6 reshape.39
  120.2 2.3 collective-permute-done.5.s_far
  122.4 0.0 copy-start.6
  122.5 0.2 collective-permute-done.4.s_core
  122.7 0.0 copy-start.7
  122.7 0.0 collective-permute-done.3.o_far
  122.7 0.4 copy-done.6
  123.1 0.0 collective-permute-done.2.o_core
  123.1 0.2 copy-done.7
  123.3 219.4 %share.1 = (bf16[4,1024,2048]{2,1,0:T(8,128)(2,1)}, f32[1024,2048]{1,0:T(8,128)}, f32[1024,2048]{1,0:T(8,128)}) custom-call(bf16[4,1024,2048]{2,1,0:T(8,128)(2,1)} %hidden.1, f32[4,1024,128]{2,1,0:T(8,128)} %get-tuple-element.32.o_own, f32[4,1024,128]{2,1,0:T(8,128)} %collective-permute-done.2.o_core, f32[4,1024,128]{2,1,0:T(8,128)} %collective-permute-done.3.o_far, ...), custom_call_target="tpu_custom_call" | custom-call | flops 99999997952 | bytes 33554432 | tf_op jit(solution)/shard_map/share/pallas_call | solution.py:577
  342.6 14.2 %copy.24 = bf16[4,1024,2048]{2,1,0:T(8,128)(2,1)} copy(bf16[4,1024,2048]{2,1,0:T(8,128)(2,1)} %get-tuple-element.49) | data formatting | bytes 33554432
  (2 shorter events, 0.0 us)
Async XLA Ops:
  53.8 5.1 %collective-permute-start.1 = (f32[4,1024,128]{2,1,0:T(8,128)}, f32[4,1024,128]{2,1,0:T(8,128)S(1)}, u32[]{:S(2)}, u32[]{:S(2)}) collective-permute-start(f32[4,1024,128]{2,1,0:T(8,128)} %get-tuple-element.25), channel_id=1, source_target_pairs={{0,1},{1,0},{2,3},{3,2},{4,5},{5,4},{6,7},{7,6},{8,9},{9,8},{10,11... | collective-permute-start | bytes 6291464 | tf_op jit(solution)/shard_map/ppermute | solution.py:631
  53.8 4.2 %collective-permute-start = (f32[8,1024]{1,0:T(8,128)}, f32[8,1024]{1,0:T(8,128)S(1)}, u32[]{:S(2)}, u32[]{:S(2)}) collective-permute-start(f32[8,1024]{1,0:T(8,128)} %get-tuple-element.24), channel_id=1, source_target_pairs={{0,1},{1,0},{2,3},{3,2},{4,5},{5,4},{6,7},{7,6},{8,9},{9,8},{10,11... | collective-permute-start | bytes 98312 | tf_op jit(solution)/shard_map/ppermute | solution.py:631
  54.4 9.4 %copy-start.5 = (s32[2]{0:T(128)}, s32[2]{0:T(128)S(1)}, u32[]{:S(2)}) copy-start(s32[2]{0:T(128)S(1)} %pad_add_fusion.rows) | copy-start | bytes 28
  58.9 1.3 copy-start
  60.2 3.6 copy-start.1
  64.4 58.3 %collective-permute-start.3 = (f32[4,1024,128]{2,1,0:T(8,128)S(1)}, f32[4,1024,128]{2,1,0:T(8,128)}, u32[]{:S(2)}, u32[]{:S(2)}) collective-permute-start(f32[4,1024,128]{2,1,0:T(8,128)S(1)} %multiply_add_fusion), channel_id=1, source_target_pairs={{0,2},{1,3},{2,0},{3,1},{4,6},{5,7},{6,4},{7,5},{8,10},{9,11},{10,... | collective-permute-start | bytes 6291464 | tf_op jit(solution)/shard_map/ppermute | solution.py:635
  89.1 29.8 %copy-start.3 = (bf16[2048]{0:T(1024)(128)(2,1)S(1)}, bf16[2048]{0:T(1024)(128)(2,1)}, u32[]{:S(2)}) copy-start(bf16[2048]{0:T(1024)(128)(2,1)} %param.31) | copy-start | bytes 12292
  89.1 29.8 %copy-start.4 = (bf16[2048]{0:T(1024)(128)(2,1)S(1)}, bf16[2048]{0:T(1024)(128)(2,1)}, u32[]{:S(2)}) copy-start(bf16[2048]{0:T(1024)(128)(2,1)} %param.27) | copy-start | bytes 12292
  89.2 30.4 %copy-start.2 = (bf16[2048]{0:T(1024)(128)(2,1)S(1)}, bf16[2048]{0:T(1024)(128)(2,1)}, u32[]{:S(2)}) copy-start(bf16[2048]{0:T(1024)(128)(2,1)} %param.29) | copy-start | bytes 12292
  118.5 4.6 %collective-permute-start.2 = (f32[4,1024,128]{2,1,0:T(8,128)}, f32[4,1024,128]{2,1,0:T(8,128)}, u32[]{:S(2)}, u32[]{:S(2)}) collective-permute-start(f32[4,1024,128]{2,1,0:T(8,128)} %get-tuple-element.33), channel_id=1, source_target_pairs={{0,1},{1,0},{2,3},{3,2},{4,5},{5,4},{6,7},{7,6},{8,9},{9,8},{10,11... | collective-permute-start | bytes 6291464 | tf_op jit(solution)/shard_map/ppermute | solution.py:639
  118.5 4.0 %collective-permute-start.5 = (f32[8,1024]{1,0:T(8,128)S(1)}, f32[8,1024]{1,0:T(8,128)S(1)}, u32[]{:S(2)}, u32[]{:S(2)}) collective-permute-start(f32[8,1024]{1,0:T(8,128)S(1)} %pad_maximum_fusion.1), channel_id=1, source_target_pairs={{0,2},{1,3},{2,0},{3,1},{4,6},{5,7},{6,4},{7,5},{8,10},{9,11},{10,... | collective-permute-start | bytes 98312 | tf_op jit(solution)/shard_map/ppermute | solution.py:635
  118.5 4.1 %collective-permute-start.4 = (f32[8,1024]{1,0:T(8,128)}, f32[8,1024]{1,0:T(8,128)S(1)}, u32[]{:S(2)}, u32[]{:S(2)}) collective-permute-start(f32[8,1024]{1,0:T(8,128)} %get-tuple-element.36), channel_id=1, source_target_pairs={{0,1},{1,0},{2,3},{3,2},{4,5},{5,4},{6,7},{7,6},{8,9},{9,8},{10,11... | collective-permute-start | bytes 98312 | tf_op jit(solution)/shard_map/ppermute | solution.py:639
  122.4 0.6 copy-start.6
  122.7 0.6 copy-start.7

commit v4 on v3

v4 whole, which is shorter than its diff:
```python
import functools
import math

import jax
import jax.numpy as jnp
from jax import lax
from jax.experimental import pallas as pl
from jax.experimental.pallas import tpu as pltpu
from jax.sharding import PartitionSpec as P

EPSILON = 1e-5
NEG_BIG = -1e30
ROTARY_SHARE = 4
ROPE_BASE = 10000.0
LOG2E = math.log2(math.e)
MESH = pl.DeviceIdType.MESH
F32 = jnp.float32
BF16 = jnp.bfloat16
VMEM_LIMIT = 60 * 1024 * 1024
LAYER_LIMIT = 67_043_328
EMPTY = -1e29
CHUNKS = 64
STAGES = 4
BLOCKS = 8
SLICES = 4
TILES = 4
HALVES = 2
LAG_START = 2
LAG_AHEAD = 1
LAG_BACK = 1
LAG_CORE = 2
LAG_Y = 5
LAG_LAST = 6


def layer_norm(values_in, gain_vec, bias_vec):
    x_f32 = values_in.astype(F32)
    row_mean = jnp.mean(x_f32, axis=-1, keepdims=True)
    centered = x_f32 - row_mean
    variance = jnp.mean(centered * centered, axis=-1, keepdims=True)
    return (centered * lax.rsqrt(variance + EPSILON) * gain_vec + bias_vec).astype(BF16)


def rope_table(lengths, chunk_len, head_dim):
    rot_dim = head_dim // ROTARY_SHARE
    half_rot = rot_dim // 2
    positions = lengths[:, None] + jnp.arange(chunk_len, dtype=jnp.int32)[None, :]
    inv_freq = ROPE_BASE ** (-2.0 * jnp.arange(half_rot, dtype=F32) / rot_dim)
    angles = positions.astype(F32)[:, None, :] * inv_freq[:, None]
    cos_tab = jnp.cos(angles)
    sin_tab = jnp.sin(angles)
    return jnp.concatenate([cos_tab, cos_tab, -sin_tab, sin_tab], axis=1)


def wide(column, lanes):
    return jnp.concatenate([column] * (lanes // column.shape[1]), axis=1)


def scores_of(query, keys, scale, mask):
    scores = lax.dot_general(query, keys, (((1,), (1,)), ((), ())), preferred_element_type=F32) * scale
    return scores if mask is None else jnp.where(mask, scores, NEG_BIG)


def lane_sum(values, lanes):
    return functools.reduce(jnp.add, [values[:, n:n + lanes] for n in range(0, values.shape[1], lanes)])


def lane_max(values, lanes):
    return functools.reduce(jnp.maximum, [values[:, n:n + lanes] for n in range(0, values.shape[1], lanes)])


def first_step(heads, scale, q_of, k_of, v_of, m_scr, l_scr, o_scr, mask):
    for h in range(heads):
        lanes = o_scr.shape[2]
        scores = scores_of(q_of(h), k_of(h), scale, mask)
        peak = jnp.maximum(jnp.max(lane_max(scores, lanes), axis=1, keepdims=True), EMPTY)
        peak = jnp.broadcast_to(peak, m_scr.shape[1:])
        probs = jnp.exp2(scores - wide(peak, scores.shape[1]))
        m_scr[h] = peak
        l_scr[h] = lane_sum(probs, lanes)
        o_scr[h] = jnp.dot(probs.astype(BF16), v_of(h), preferred_element_type=F32)


def block_step(heads, scale, q_of, k_of, v_of, m_scr, l_scr, o_scr, mask):
    for h in range(heads):
        lanes = o_scr.shape[2]
        scores = scores_of(q_of(h), k_of(h), scale, mask)
        m_old = m_scr[h]
        m_new = jnp.maximum(m_old, jnp.max(lane_max(scores, lanes), axis=1, keepdims=True))
        probs = jnp.exp2(scores - wide(m_new, scores.shape[1]))
        shrink = jnp.exp2(m_old - m_new)
        l_scr[h] = l_scr[h] * shrink + lane_sum(probs, lanes)
        m_scr[h] = m_new
        o_scr[h] = o_scr[h] * shrink + jnp.dot(probs.astype(BF16), v_of(h), preferred_element_type=F32)


def piece_weights(heads, stats, head_dim):
    peak = functools.reduce(jnp.maximum, [s[:heads] for s in stats])
    weights = [jnp.exp2(s[:heads] - peak) for s in stats]
    total = functools.reduce(jnp.add, [s[heads:2 * heads] * w for s, w in zip(stats, weights)])
    return peak, weights, total


def as_columns(parts, head_dim):
    count = sum(p.shape[0] for p in parts)
    return jnp.concatenate(parts + [jnp.zeros((head_dim - count, parts[0].shape[1]), F32)], axis=0).T


def layer_kernel(tp_size, heads, lengths, hidden, table, k_cache, v_cache, w_qkv, w_up, w_down, w_out,
                 gain1, bias1, gain2, bias2, b_qkv, b_up_ref, extra_ref,
                 out_ref, y_box, core_box, last_box, pk, qb, ob,
                 acc, from_left, from_right, up, down, proj, x_big, tab_buf, kv, ob_far, m_scr, l_scr, o_scr, st, sbox,
                 stage, land,
                 up_sem, down_sem, proj_sem, xb_sem, tab_sem, pk_sem, kv_sem, q_sem, x_sem, o_sem,
                 qs_sem, qr_sem, fs_sem, fr_sem, ns_sem, nr_sem, ys_sem, yr_sem, ss_sem, sr_sem,
                 left_sem, right_sem, y_sem, core_sem, last_sem, send_sem, stage_sem, land_sem):
    z = lax.axis_index("tp")
    j = lax.axis_index("cp")
    y, c = lax.div(j, 2), lax.rem(j, 2)
    across, mate, corner = (1 - y) * 2 + c, y * 2 + (1 - c), (1 - y) * 2 + (1 - c)
    chunk_len, d_model = acc.shape
    head_dim = o_scr.shape[2]
    span = heads * head_dim
    slots = k_cache.shape[2]
    tokens = chunk_len // CHUNKS
    block = chunk_len // BLOCKS
    half = chunk_len // HALVES
    tile = chunk_len // TILES
    pairs = CHUNKS // 2
    per_block = pairs // BLOCKS
    width = up.shape[2]
    last = tp_size - 1
    root_a, root_b = (tp_size - 1) // 2, tp_size // 2
    rot_dim = head_dim // ROTARY_SHARE
    half_rot = rot_dim // 2
    scale = head_dim ** -0.5 * LOG2E
    own_at, sent_at, kept_at, q_at = 0, span, 2 * span, 3 * span

    def rows_of(n, size):
        return pl.ds(pl.multiple_of(n * size, size), size)

    def weight_copies(f):
        cols = pl.ds(f * width, width)
        return (pltpu.make_async_copy(w_up.at[:, cols], up.at[f], up_sem.at[f]),
                pltpu.make_async_copy(w_down.at[cols, :], down.at[f], down_sem.at[f]))

    def row_of(n):
        return across * (1 - n) + j * n

    def big_x(i):
        return pltpu.make_async_copy(
            hidden.at[row_of(lax.div(i, TILES)), rows_of(lax.rem(i, TILES), tile), :], x_big.at[lax.rem(i, 2)], xb_sem.at[lax.rem(i, 2)])

    def cache_copies(row, slot):
        return (pltpu.make_async_copy(k_cache.at[row], kv.at[slot, 0], kv_sem.at[slot, 0]),
                pltpu.make_async_copy(v_cache.at[row], kv.at[slot, 1], kv_sem.at[slot, 1]))

    def start(copies):
        for copy in copies:
            copy.start()

    def wait(copies):
        for copy in copies:
            copy.wait()

    qkv_copies = [pltpu.make_async_copy(w_qkv.at[:, pl.ds(s * width, width)], up.at[s], up_sem.at[s]) for s in range(3)]
    tab_copies = [pltpu.make_async_copy(table.at[row], tab_buf.at[n], tab_sem.at[n]) for n, row in enumerate((across, j))]
    proj_copy = pltpu.make_async_copy(w_out, proj, proj_sem)
    big_x(0).start()
    start(qkv_copies)
    start(tab_copies)
    start(cache_copies(corner, 0))
    start(cache_copies(across, 1))
    proj_copy.start()

    barrier = pltpu.get_barrier_semaphore()
    pl.semaphore_signal(barrier, inc=1, device_id={"cp": across}, device_id_type=MESH)
    pl.semaphore_signal(barrier, inc=1, device_id={"cp": mate}, device_id_type=MESH)

    @pl.when(z > 0)
    def _():
        pl.semaphore_signal(barrier, inc=1, device_id={"tp": z - 1}, device_id_type=MESH)

    @pl.when(z < last)
    def _():
        pl.semaphore_signal(barrier, inc=1, device_id={"tp": z + 1}, device_id_type=MESH)

    inside = jnp.logical_and(z > 0, z < last)

    @pl.when(inside)
    def _():
        pl.semaphore_wait(barrier, 4)

    @pl.when(jnp.logical_not(inside))
    def _():
        pl.semaphore_wait(barrier, 3)

    def to_core(src, dst, send, arrive):
        return pltpu.make_async_remote_copy(
            src_ref=src, dst_ref=dst, send_sem=send, recv_sem=arrive, device_id={"cp": mate}, device_id_type=MESH)

    def to_y(src, dst, send, arrive):
        return pltpu.make_async_remote_copy(
            src_ref=src, dst_ref=dst, send_sem=send, recv_sem=arrive, device_id={"cp": across}, device_id_type=MESH)


    def sent_tile(n, t):
        slot = lax.rem(t, 2)
        return to_core(acc.at[rows_of(slot, tile), pl.ds(0, 3 * span)], qb.at[n, rows_of(t, tile), :], qs_sem.at[slot], qr_sem.at[n, t])

    wait(qkv_copies)
    wait(tab_copies)

    @pl.loop(0, 2 * TILES)
    def _(i):
        n, t, slot = lax.div(i, TILES), lax.rem(i, TILES), lax.rem(i, 2)

        @pl.when(i + 1 < 2 * TILES)
        def _():
            big_x(i + 1).start()

        big_x(i).wait()

        @pl.when(i >= 2)
        def _():
            sent_tile(n, t).wait_send()

        normed = layer_norm(x_big[slot], gain1[...], bias1[...])
        tab = tab_buf[n, :, rows_of(t, tile)]
        tab = jnp.concatenate([tab] * (head_dim // tab.shape[0]), axis=0).T
        lane = lax.broadcasted_iota(jnp.int32, tab.shape, 1)
        cos_tab = jnp.where(lane < rot_dim, tab, 1.0)
        sin_tab = jnp.where(lane < rot_dim, pltpu.roll(tab, head_dim - rot_dim, 1), 0.0)

        def rotate(values):
            long = values.astype(F32)
            other = jnp.where(lane < half_rot, pltpu.roll(long, head_dim - half_rot, 1), pltpu.roll(long, half_rot, 1))
            return (long * cos_tab + other * sin_tab).astype(BF16)

        place = down.at[n * HALVES + lax.div(t, TILES // HALVES), rows_of(lax.rem(t, TILES // HALVES), tile), :]
        hold = acc.at[rows_of(slot, tile), :]
        for s in range(3):
            part = slice(s * width, (s + 1) * width)
            some = (jnp.dot(normed, up[s], preferred_element_type=F32) + b_qkv[:, part]).astype(BF16)
            for g in range(width // head_dim):
                group = s * (width // head_dim) + g
                values = some[:, g * head_dim:(g + 1) * head_dim]
                if group % 3 < 2:
                    values = rotate(values)
                cols = slice(group * head_dim, (group + 1) * head_dim)
                place[:, cols] = values
                hold[:, cols] = values.astype(F32)
        sent_tile(n, t).start()

    for f in range(SLICES):
        weight_copies(f)[0].start()
    pack_copies = [
        pltpu.make_async_copy(down.at[n * HALVES + e, pl.ds(0, half), pl.ds(0, 3 * span)], pk.at[n, pl.ds(e * half, half), :],
                              pk_sem.at[n, e])
        for n in range(2) for e in range(HALVES)]
    start(pack_copies)
    for t in range(2):
        sent_tile(1, TILES - 2 + t).wait_send()


    def got_queries(n):
        for t in range(TILES):
            sent_tile(n, t).wait_recv()
        copies = [pltpu.make_async_copy(qb.at[n, :, pl.ds(3 * h * head_dim, head_dim)],
                                        acc.at[:, pl.ds(q_at + h * head_dim, head_dim)], q_sem.at[h]) for h in range(heads)]
        start(copies)
        return copies

    def attend(row, slot, query, at, kind, after=None, own=False):
        valid = jnp.clip(lengths[row] - j * slots, 0, slots)

        @pl.loop(0, HALVES)
        def _(e):
            def keys(h):
                return kv[slot, 0, h]

            def values(h):
                return kv[slot, 1, h]

            mask = lax.broadcasted_iota(jnp.int32, (half, slots), 1) < valid
            first_step(heads, scale, lambda h: query(e, h), keys, values, m_scr, l_scr, o_scr, mask)

            def own_block(b, mask):
                def part(p):
                    return lambda h: down[HALVES + b, :half, (3 * h + p) * head_dim:(3 * h + p + 1) * head_dim]

                block_step(heads, scale, lambda h: query(e, h), part(1), part(2), m_scr, l_scr, o_scr, mask)

            if own:
                @pl.loop(0, e)
                def _(b):
                    own_block(b, None)

                shape = (half, half)
                own_block(e, lax.broadcasted_iota(jnp.int32, shape, 0) >= lax.broadcasted_iota(jnp.int32, shape, 1))

            lane = lax.broadcasted_iota(jnp.int32, (half, head_dim), 1)
            stats = jnp.zeros((half, head_dim), F32)
            for h in range(heads):
                stats = jnp.where(lane == h, m_scr[h], stats)
                stats = jnp.where(lane == heads + h, jnp.sum(l_scr[h], axis=1, keepdims=True), stats)
                acc[rows_of(e, half), at + h * head_dim:at + (h + 1) * head_dim] = o_scr[h]
            st[kind, :, rows_of(e, half)] = stats.T[:8]
            if after is not None:
                after(e)

    def held(n):
        return lambda e, h: down[n * HALVES + e, :half, 3 * h * head_dim:(3 * h + 1) * head_dim]

    def taken(e, h):
        return acc[rows_of(e, half), q_at + h * head_dim:q_at + (h + 1) * head_dim].astype(BF16)

    def far_piece(e):
        return to_core(acc.at[rows_of(e, half), pl.ds(sent_at, span)], ob_far.at[rows_of(e, half), :], fs_sem.at[e], fr_sem.at[e])

    def near_piece(e):
        return to_core(acc.at[rows_of(e, half), pl.ds(sent_at, span)], ob.at[0, rows_of(e, half), :], ns_sem.at[e], nr_sem.at[e])

    def y_piece(b):
        return to_y(acc.at[rows_of(b, block), pl.ds(kept_at, span)], ob.at[1, rows_of(b, block), :], ys_sem.at[b], yr_sem.at[b])

    far_stats = to_core(st.at[0], sbox.at[0], ss_sem.at[0], sr_sem.at[0])
    y_stats = to_y(st.at[1], sbox.at[2], ss_sem.at[1], sr_sem.at[2])
    near_stats = to_core(st.at[2], sbox.at[1], ss_sem.at[2], sr_sem.at[1])

    wait(got_queries(0))
    wait(cache_copies(corner, 0))
    attend(corner, 0, taken, sent_at, 0, after=lambda e: far_piece(e).start())
    far_stats.start()
    start(cache_copies(mate, 0))
    near_queries = got_queries(1)
    wait(cache_copies(across, 1))
    attend(across, 1, held(0), kept_at, 1)
    start(cache_copies(j, 1))

    far_stats.wait()
    _, weights, total = piece_weights(heads, [st[1], sbox[0]], head_dim)
    peak = jnp.maximum(st[1, :heads, :], sbox[0, :heads, :])

    @pl.loop(0, HALVES)
    def _(e):
        far_piece(e).wait_recv()

    for b in range(BLOCKS):
        part = slice(b * block, (b + 1) * block)
        columns = as_columns([w[:, part] for w in weights], head_dim)
        for h in range(heads):
            mine = slice(kept_at + h * head_dim, kept_at + (h + 1) * head_dim)
            acc[part, mine] = (acc[part, mine] * columns[:, h:h + 1]
                               + ob_far[part, h * head_dim:(h + 1) * head_dim] * columns[:, heads + h:heads + h + 1])
        y_piece(b).start()
    st[1, :heads, :] = peak
    st[1, heads:2 * heads, :] = total
    y_stats.start()

    for e in range(HALVES):
        far_piece(e).wait_send()
    wait(near_queries)
    wait(cache_copies(mate, 0))
    attend(mate, 0, taken, sent_at, 2, after=lambda e: near_piece(e).start())
    near_stats.start()
    wait(cache_copies(j, 1))
    wait(pack_copies)
    for f in range(HALVES):
        weight_copies(f)[1].start()
    attend(j, 1, held(1), own_at, 3, own=True)
    for f in range(HALVES, SLICES):
        weight_copies(f)[1].start()

    def block_copies(b):
        rows = rows_of(b, block)
        slot = lax.rem(b, 2)
        return [pltpu.make_async_copy(hidden.at[j, rows, :], x_big.at[slot, pl.ds(0, block), :], x_sem.at[slot])] + [
            pltpu.make_async_copy(ob.at[n, rows, :], ob_far.at[rows_of(2 * slot + n, block), :], o_sem.at[slot, n]) for n in range(2)]

    def fetch(b):
        y_piece(b).wait_recv()
        start(block_copies(b))

    near_stats.wait()
    y_stats.wait()
    for e in range(HALVES):
        near_piece(e).wait_recv()
        near_piece(e).wait_send()
    proj_copy.wait()
    fetch(0)


    def begin(b):
        slot = lax.rem(b, 2)
        rows = rows_of(b, block)

        @pl.when(b + 1 < BLOCKS)
        def _():
            fetch(b + 1)

        wait(block_copies(b))
        y_piece(b).wait_send()
        _, weights, total = piece_weights(heads, [st[3, :, rows], sbox[1, :, rows], sbox[2, :, rows]], head_dim)
        columns = as_columns([w / total for w in weights], head_dim)
        for h in range(heads):
            cols = slice(h * head_dim, (h + 1) * head_dim)
            pieces = [acc[rows, own_at + h * head_dim:own_at + (h + 1) * head_dim]]
            pieces += [ob_far[rows_of(2 * slot + n, block), cols] for n in range(2)]
            context = functools.reduce(
                jnp.add, [o * columns[:, n * heads + h:n * heads + h + 1] for n, o in enumerate(pieces)])
            x_big[1, block:2 * block, cols] = context.astype(BF16)
        x = x_big[slot, :block, :]
        x_big[0, block:2 * block, :] = layer_norm(x, gain2[...], bias2[...])
        acc[rows, :] = jnp.dot(x_big[1, block:2 * block, :span], proj[...], preferred_element_type=F32)

        @pl.when(z == 0)
        def _():
            acc[rows, :] += x.astype(F32) + extra_ref[...]

    def slice_of(b, f):
        rows = rows_of(b, block)

        @pl.when(b == 0)
        def _():
            wait(weight_copies(f))

        wide_h = jnp.dot(x_big[0, block:2 * block, :], up[f], preferred_element_type=F32) + b_up_ref[f]
        act = (0.5 * wide_h * (1.0 + lax.erf(wide_h * math.sqrt(0.5)))).astype(BF16)
        acc[rows, :] += jnp.dot(act, down[f], preferred_element_type=F32)


    def at(ref, k):
        return ref.at[pl.ds(pl.multiple_of(k * tokens, tokens), tokens), :]

    def remote(src, dst, k, which, arrive, device):
        return pltpu.make_async_remote_copy(
            src_ref=at(src, k), dst_ref=at(dst, k), send_sem=send_sem.at[which], recv_sem=arrive.at[k],
            device_id=device, device_id_type=MESH,
        )

    def send_right(src, k):
        remote(src, from_left, k, 0, left_sem, {"tp": z + 1}).start()

    def send_left(src, k):
        remote(src, from_right, k, 1, right_sem, {"tp": z - 1}).start()

    def arrived(ref, sem, k):
        remote(ref, ref, k, 0, sem, {"cp": j}).wait_recv()

    def drained(ref, which):
        pltpu.make_async_copy(ref, ref, send_sem.at[which]).wait()

    def emit(stream, values, k, row):
        slot = lax.rem(k, STAGES)

        def copy():
            return pltpu.make_async_copy(stage.at[stream, slot], at(out_ref.at[row], k), stage_sem.at[stream, slot])

        @pl.when(k >= STAGES)
        def _():
            copy().wait()

        stage[stream, slot] = values.astype(BF16)
        copy().start()

    def chunk(ref, k):
        return ref[pl.ds(pl.multiple_of(k * tokens, tokens), tokens), :]

    def finish(src, k):
        remote(src, y_box, k, 2, y_sem, {"cp": across}).start()
        remote(src, core_box, k, 3, core_sem, {"cp": mate}).start()
        emit(0, chunk(src, k), k, j)

    def landing(n, box, k):
        slot = lax.rem(k, STAGES)
        return pltpu.make_async_copy(at(box, k), land.at[n, slot], land_sem.at[n, slot])

    def gathered(i):
        def lagged(lag, act):
            @pl.when(jnp.logical_and(i >= lag, i < pairs + lag))
            def _():
                for n in range(2):
                    act((i - lag) * 2 + n)

        def core(k):
            arrived(core_box, core_sem, k)
            landing(0, core_box, k).start()

        def core_out(k):
            landing(0, core_box, k).wait()
            emit(1, land[0, lax.rem(k, STAGES)], k, mate)

        def side(k):
            arrived(y_box, y_sem, k)
            remote(y_box, last_box, k, 4, last_sem, {"cp": mate}).start()
            landing(2, y_box, k).start()

        def side_out(k):
            landing(2, y_box, k).wait()
            emit(2, land[2, lax.rem(k, STAGES)], k, across)

        def final(k):
            arrived(last_box, last_sem, k)
            landing(1, last_box, k).start()

        def final_out(k):
            landing(1, last_box, k).wait()
            emit(3, land[1, lax.rem(k, STAGES)], k, corner)

        lagged(LAG_CORE + 1, core_out)
        lagged(LAG_Y + 1, side_out)
        lagged(LAG_LAST + 1, final_out)
        lagged(LAG_CORE, core)
        lagged(LAG_Y, side)
        lagged(LAG_LAST, final)

    def add(k, *others):
        rows = pl.ds(pl.multiple_of(k * tokens, tokens), tokens)
        total = acc[rows, :]
        for other in others:
            total = total + other[rows, :]
        acc[rows, :] = total

    def when(cond, act, *args):
        @pl.when(cond)
        def _():
            act(*args)

    def end(i, first):
        inbox, sem = (from_right, right_sem) if first else (from_left, left_sem)
        near_bit = 0 if first else 1

        def got(k):
            arrived(inbox, sem, k)
            finish(inbox, k)

        when(jnp.logical_and(i >= 0, i < pairs), lambda: got(2 * i + near_bit))
        when(jnp.logical_and(i >= LAG_BACK, i < pairs + LAG_BACK), lambda: got(2 * (i - LAG_BACK) + 1 - near_bit))

    def inner(i, left_side):
        mine = 0 if left_side else 1
        if left_side:
            (outer, outer_sem, to_outer), (inward, inward_sem, to_inner) = (
                (from_left, left_sem, send_left), (from_right, right_sem, send_right))
        else:
            (outer, outer_sem, to_outer), (inward, inward_sem, to_inner) = (
                (from_right, right_sem, send_right), (from_left, left_sem, send_left))

        def early(p):
            passed = 2 * p + 1 - mine
            arrived(outer, outer_sem, passed)
            add(passed, outer)
            to_inner(acc, passed)

        def near(p):
            rooted = 2 * p + mine
            arrived(outer, outer_sem, rooted)
            arrived(inward, inward_sem, rooted)
            add(rooted, from_left, from_right)
            to_outer(acc, rooted)
            to_inner(acc, rooted)
            finish(acc, rooted)

        def far(p):
            k = 2 * p + 1 - mine
            arrived(inward, inward_sem, k)
            to_outer(inward, k)
            finish(inward, k)

        when(jnp.logical_and(i + LAG_AHEAD >= 0, i + LAG_AHEAD < pairs), early, i + LAG_AHEAD)
        when(jnp.logical_and(i >= 0, i < pairs), near, i)
        when(jnp.logical_and(i >= LAG_BACK, i < pairs + LAG_BACK), far, i - LAG_BACK)

    lead = SLICES + LAG_START

    @pl.loop(0, lead + pairs + LAG_LAST + 2)
    def _(s):
        @pl.when(s < BLOCKS * SLICES)
        def _():
            b, f = lax.div(s, SLICES), lax.rem(s, SLICES)
            when(f == 0, begin, b)
            slice_of(b, f)

            def push(send):
                @pl.loop(0, 2 * per_block)
                def _(n):
                    send(acc, b * 2 * per_block + n)

            when(jnp.logical_and(f == SLICES - 1, z == 0), push, send_right)
            when(jnp.logical_and(f == SLICES - 1, z == last), push, send_left)

        i = s - lead
        when(z == 0, end, i, True)
        when(z == root_a, inner, i, True)
        when(z == root_b, inner, i, False)
        when(z == last, end, i, False)
        gathered(i)

    @pl.when(z < last)
    def _():
        drained(acc, 0)

    @pl.when(z > 0)
    def _():
        drained(acc, 1)

    for which in (2, 3, 4):
        drained(acc, which)
    for stream in range(4):
        for slot in range(STAGES):
            pltpu.make_async_copy(stage.at[stream, slot], at(out_ref.at[0], 0), stage_sem.at[stream, slot]).wait()


def run_layer(lengths, hidden_in, table, k_block, v_block, w_qkv, w_up, w_down, w_out, norms, b_qkv, b_up, extra, tp_size):
    num_rows, chunk_len, d_model = hidden_in.shape
    heads, slots, head_dim = k_block.shape[1:]
    span = heads * head_dim
    width = w_up.shape[1] // SLICES
    tokens = chunk_len // CHUNKS
    block = chunk_len // BLOCKS
    half = chunk_len // HALVES
    tile = chunk_len // TILES
    dma = pltpu.SemaphoreType.DMA
    buffer = pltpu.VMEM((chunk_len, d_model), F32)
    box = jax.ShapeDtypeStruct((chunk_len, d_model), F32)
    hbm = pl.BlockSpec(memory_space=pl.ANY)
    vmem = pl.BlockSpec(memory_space=pltpu.VMEM)
    out, _, _, _, pk, qb, _ = pl.pallas_call(
        functools.partial(layer_kernel, tp_size, heads),
        in_specs=[pl.BlockSpec(memory_space=pltpu.SMEM)] + [hbm] * 8 + [vmem] * 7,
        out_specs=[hbm] * 7,
        out_shape=[
            jax.ShapeDtypeStruct((num_rows, chunk_len, d_model), BF16), box, box, box,
            jax.ShapeDtypeStruct((2, chunk_len, 3 * span), BF16),
            jax.ShapeDtypeStruct((2, chunk_len, 3 * span), F32),
            jax.ShapeDtypeStruct((2, chunk_len, span), F32),
        ],
        scratch_shapes=[buffer] * 3
        + [
            pltpu.VMEM((SLICES, d_model, width), BF16),
            pltpu.VMEM((SLICES, width, d_model), BF16),
            pltpu.VMEM((span, d_model), BF16),
            pltpu.VMEM((2, tile, d_model), BF16),
            pltpu.VMEM((2,) + table.shape[1:], F32),
            pltpu.VMEM((2, 2, heads, slots, head_dim), BF16),
            pltpu.VMEM((chunk_len, span), F32),
            pltpu.VMEM((heads, half, head_dim), F32),
            pltpu.VMEM((heads, half, head_dim), F32),
            pltpu.VMEM((heads, half, head_dim), F32),
            pltpu.VMEM((4, 8, chunk_len), F32),
            pltpu.VMEM((3, 8, chunk_len), F32),
            pltpu.VMEM((4, STAGES, tokens, d_model), BF16),
            pltpu.VMEM((3, STAGES, tokens, d_model), F32),
        ]
        + [dma((SLICES,)), dma((SLICES,)), dma, dma((2,)), dma((2,)), dma((2, HALVES)), dma((2, 2)), dma((heads,)), dma((2,)), dma((2, 2))]
        + [dma((2,)), dma((2, TILES)), dma((HALVES,)), dma((HALVES,)), dma((HALVES,)), dma((HALVES,)), dma((BLOCKS,)), dma((BLOCKS,)),
           dma((3,)), dma((3,))]
        + [dma((CHUNKS,))] * 5
        + [dma((5,)), dma((4, STAGES)), dma((3, STAGES))],
        compiler_params=pltpu.CompilerParams(collective_id=0, has_side_effects=True, vmem_limit_bytes=LAYER_LIMIT),
        cost_estimate=pl.CostEstimate(flops=100_000_000_000, bytes_accessed=chunk_len * d_model * 16, transcendentals=0),
        name="layer",
    )(lengths, hidden_in, table, k_block, v_block, w_qkv, w_up, w_down, w_out, *norms, b_qkv.astype(F32)[None],
      b_up.astype(F32).reshape(SLICES, 1, width), extra[None])
    return out, pk, qb


def finish_kernel(heads, meta, in_ref, pk, qb, out_ref, k_ref, v_ref, buf, low, high, in_sem, out_sem, low_sem, high_sem, kv_sem):
    pieces = in_sem.shape[1]
    tile = buf.shape[1] // pieces
    head_dim = k_ref.shape[3]
    places = [(b, pl.ds(t * tile, tile), t) for b in range(buf.shape[0]) for t in range(pieces)]
    inward = [pltpu.make_async_copy(in_ref.at[b, rows], buf.at[b, rows], in_sem.at[b, t]) for b, rows, t in places]
    outward = [pltpu.make_async_copy(buf.at[b, rows], out_ref.at[b, rows], out_sem.at[b, t]) for b, rows, t in places]
    lows = [pltpu.make_async_copy(pk.at[n], low.at[n], low_sem.at[n]) for n in range(2)]
    highs = [pltpu.make_async_copy(qb.at[n], high.at[n], high_sem.at[n]) for n in range(2)]
    stored = []

    def store(src, n, row):
        for h in range(heads):
            for p, ref in ((1, k_ref), (2, v_ref)):
                cols = pl.ds((3 * h + p) * head_dim, head_dim)
                copy = pltpu.make_async_copy(src.at[:, cols], ref.at[row, h], kv_sem.at[n, h, p - 1])
                copy.start()
                stored.append(copy)

    for copy in highs + lows + inward:
        copy.start()
    j = meta[0]
    for n in range(2):
        lows[n].wait()
        store(low.at[n], n, j ^ (2 - 2 * n))
    for n in range(2):
        highs[n].wait()
        for h in range(heads):
            for p in (1, 2):
                cols = slice((3 * h + p) * head_dim, (3 * h + p + 1) * head_dim)
                low[2 + n, :, cols] = high[n, :, cols].astype(BF16)
        store(low.at[2 + n], 2 + n, j ^ (3 - 2 * n))
    for one, other in zip(inward, outward):
        one.wait()
        other.start()
    for copy in outward + stored:
        copy.wait()


def finish(meta, out, pk, qb, heads, head_dim):
    rows, chunk_len, _ = out.shape
    span = pk.shape[2]
    hbm = pl.BlockSpec(memory_space=pl.ANY)
    cache = jax.ShapeDtypeStruct((rows, heads, chunk_len, head_dim), BF16)
    dma = pltpu.SemaphoreType.DMA
    return pl.pallas_call(
        functools.partial(finish_kernel, heads),
        in_specs=[pl.BlockSpec(memory_space=pltpu.SMEM)] + [hbm] * 3,
        out_specs=[hbm] * 3,
        out_shape=[jax.ShapeDtypeStruct(out.shape, out.dtype), cache, cache],
        scratch_shapes=[
            pltpu.VMEM(out.shape, out.dtype), pltpu.VMEM((4, chunk_len, span), BF16), pltpu.VMEM((2, chunk_len, span), F32),
            dma((rows, 4)), dma((rows, 4)), dma((2,)), dma((2,)), dma((4, heads, 2)),
        ],
        compiler_params=pltpu.CompilerParams(vmem_limit_bytes=VMEM_LIMIT),
        name="finish",
    )(meta, out, pk, qb)


def solution(mesh):
    in_specs = (P("dp", None, None), P("dp"), P("dp", "tp", "cp", None), P("dp", "tp", "cp", None), P(), P(), P(), P(), P(None, "tp"), P("tp"), P("tp", None), P(), P(None, "tp"), P("tp"), P("tp", None), P())
    out_specs = (P("dp", None, None), P("dp", "tp", None, None), P("dp", "tp", None, None))
    tp_size = mesh.shape["tp"]

    def local_layer(hidden_in, lengths, k_block, v_block, ln1_gain, ln1_bias, ln2_gain, ln2_bias, w_qkv, b_qkv, w_out, b_out, w_up, b_up, w_down, b_down):
        num_rows, chunk_len, d_model = hidden_in.shape
        heads, block_len, head_dim = k_block.shape[1:]
        table = rope_table(lengths, chunk_len, head_dim)
        norms = [p[None] for p in (ln1_gain, ln1_bias, ln2_gain, ln2_bias)]
        extra = b_out.astype(F32) + b_down.astype(F32)
        out, pk, qb = run_layer(
            lengths, hidden_in, table, k_block, v_block, w_qkv, w_up, w_down, w_out, norms, b_qkv, b_up, extra, tp_size)
        return tuple(finish(lax.axis_index("cp")[None], out, pk, qb, heads, head_dim))

    return jax.shard_map(local_layer, mesh=mesh, in_specs=in_specs, out_specs=out_specs, check_vma=False)
```

time: 358 us -> 339 us (0.947)
  local copies, waits for them, and re-layouts: 17.4 us -> 1.28 us
  Pallas kernels: 321 us -> 331 us
  waiting for transfers between devices: 6.12 us -> 0 us
  other arithmetic: 11 us -> 5.44 us
    unnamed x17 -> x0, local copies, waits for them, and re-layouts: 16.1 us -> none
    pallas_call x5 -> x2, Pallas kernels: 321 us -> 331 us  [the longest x1 311 us: run_layer(): pl.pallas_call(functools.partial(layer_kernel, tp_size, heads), in_specs=...]
    ppermute x6 -> x0, waiting for transfers between devices: 6.12 us -> none  [the longest x2 3.83 us: local_layer(): lax.ppermute(s_s, 'cp', swap_core)]
    add x2 -> x0, other arithmetic: 4.4 us -> none  [the longest x1 3.55 us: merge(): functools.reduce(jnp.add, [o * w[..., None] for (o, _), w in zip(pieces,...]
  transfers between devices with their start and end apart: 6 -> 0, of which waited for: 3 -> 0; matrix products, arithmetic and copies ran while one was open for 1% -> 0% of each run, Pallas kernels for 15% -> 0%
where the time goes in v4:
time: 339 us
  Pallas kernels  331 us (98%)
  other arithmetic  5.44 us (2%)
    pallas_call x1, Pallas kernels, run_layer(): pl.pallas_call(functools.partial(layer_kernel, tp_size, heads), in_specs=...  311 us
    pallas_call x1, Pallas kernels, finish(): pl.pallas_call(functools.partial(finish_kernel, heads), in_specs=[pl.Bloc...  20.1 us

profile of v4, /device:TPU:0, one launch (start us, length us, event | category | flops | bytes accessed | tf_op | source)
XLA Modules:
  0.0 338.7 jit_solution(9268021631751865753)
XLA Ops:
  0.6 0.7 add_convert_fusion
  1.4 1.0 multiply_cosine_fusion
  2.4 1.1 pad_maximum_fusion.table
  3.5 1.3 reshape.37
  4.8 1.3 convert_add_fusion
  6.1 1.3 reshape.36.b_qkv
  7.4 311.0 %layer.1 = (bf16[4,1024,2048]{2,1,0:T(8,128)(2,1)}, f32[1024,2048]{1,0:T(8,128)}, f32[1024,2048]{1,0:T(8,128)}, f32[1024,2048]{1,0:T(8,128)}, bf16[2,1024,1536]{...) custom-call(s32[4]{0:T(128)} %lengths.1, bf16[4,1024,2048]{2,1,0:T(8,128)(2,1)} %hidden.1, ...), custom_call_target="tpu_custom_call" | custom-call | flops 99999997952 | bytes 33554432 | tf_op jit(solution)/shard_map/layer/pallas_call | solution.py:629
  318.4 20.1 %finish.1 = (bf16[4,1024,2048]{2,1,0:T(8,128)(2,1)}, bf16[4,4,1024,128]{3,2,1,0:T(8,128)(2,1)}, bf16[4,4,1024,128]{3,2,1,0:T(8,128)(2,1)}) custom-call(s32[1]{0:T(128)} %bitcast.meta, bf16[4,1024,2048]{2,1,0:T(8,128)(2,1)} %get-tuple-element.6.in_ref, bf16[2,1024,1536]{2,1,0:T(8,128)(2,1)} %get-tuple-element.7.pk, f32[2,1024,1536]{2,1,0:T(8,128)} %get-tuple-element.8.qb), custom_call_target="tpu_custom_call" | custom-call | tf_op jit(solution)/shard_map/finish/pallas_call | solution.py:714
  (1 shorter events, 0.0 us)

commit v5 on v4

--- a/solution.py
+++ b/solution.py
@@ -107,7 +107,7 @@
 
 
 def layer_kernel(tp_size, heads, lengths, hidden, table, k_cache, v_cache, w_qkv, w_up, w_down, w_out,
-                 gain1, bias1, gain2, bias2, b_qkv, b_up_ref, extra_ref,
+                 gain1, bias1, gain2, bias2, small,
                  out_ref, y_box, core_box, last_box, pk, qb, ob,
                  acc, from_left, from_right, up, down, proj, x_big, tab_buf, kv, ob_far, m_scr, l_scr, o_scr, st, sbox,
                  stage, land,
@@ -135,6 +135,7 @@
     half_rot = rot_dim // 2
     scale = head_dim ** -0.5 * LOG2E
     own_at, sent_at, kept_at, q_at = 0, span, 2 * span, 3 * span
+    extra_at = 3 * span + SLICES * width
 
     def rows_of(n, size):
         return pl.ds(pl.multiple_of(n * size, size), size)
@@ -241,7 +242,7 @@
         hold = acc.at[rows_of(slot, tile), :]
         for s in range(3):
             part = slice(s * width, (s + 1) * width)
-            some = (jnp.dot(normed, up[s], preferred_element_type=F32) + b_qkv[:, part]).astype(BF16)
+            some = (jnp.dot(normed, up[s], preferred_element_type=F32) + small[:, part]).astype(BF16)
             for g in range(width // head_dim):
                 group = s * (width // head_dim) + g
                 values = some[:, g * head_dim:(g + 1) * head_dim]
@@ -342,6 +343,10 @@
     _, weights, total = piece_weights(heads, [st[1], sbox[0]], head_dim)
     peak = jnp.maximum(st[1, :heads, :], sbox[0, :heads, :])
 
+    st[1, :heads, :] = peak
+    st[1, heads:2 * heads, :] = total
+    y_stats.start()
+
     @pl.loop(0, HALVES)
     def _(e):
         far_piece(e).wait_recv()
@@ -354,9 +359,6 @@
             acc[part, mine] = (acc[part, mine] * columns[:, h:h + 1]
                                + ob_far[part, h * head_dim:(h + 1) * head_dim] * columns[:, heads + h:heads + h + 1])
         y_piece(b).start()
-    st[1, :heads, :] = peak
-    st[1, heads:2 * heads, :] = total
-    y_stats.start()
 
     for e in range(HALVES):
         far_piece(e).wait_send()
@@ -416,7 +418,7 @@
 
         @pl.when(z == 0)
         def _():
-            acc[rows, :] += x.astype(F32) + extra_ref[...]
+            acc[rows, :] += x.astype(F32) + small[:, extra_at:]
 
     def slice_of(b, f):
         rows = rows_of(b, block)
@@ -425,7 +427,8 @@
         def _():
             wait(weight_copies(f))
 
-        wide_h = jnp.dot(x_big[0, block:2 * block, :], up[f], preferred_element_type=F32) + b_up_ref[f]
+        b_up = small[:, pl.ds(pl.multiple_of(3 * span + f * width, width), width)]
+        wide_h = jnp.dot(x_big[0, block:2 * block, :], up[f], preferred_element_type=F32) + b_up
         act = (0.5 * wide_h * (1.0 + lax.erf(wide_h * math.sqrt(0.5)))).astype(BF16)
         acc[rows, :] += jnp.dot(act, down[f], preferred_element_type=F32)
 
@@ -612,7 +615,7 @@
             pltpu.make_async_copy(stage.at[stream, slot], at(out_ref.at[0], 0), stage_sem.at[stream, slot]).wait()
 
 
-def run_layer(lengths, hidden_in, table, k_block, v_block, w_qkv, w_up, w_down, w_out, norms, b_qkv, b_up, extra, tp_size):
+def run_layer(lengths, hidden_in, table, k_block, v_block, w_qkv, w_up, w_down, w_out, norms, small, tp_size):
     num_rows, chunk_len, d_model = hidden_in.shape
     heads, slots, head_dim = k_block.shape[1:]
     span = heads * head_dim
@@ -628,7 +631,7 @@
     vmem = pl.BlockSpec(memory_space=pltpu.VMEM)
     out, _, _, _, pk, qb, _ = pl.pallas_call(
         functools.partial(layer_kernel, tp_size, heads),
-        in_specs=[pl.BlockSpec(memory_space=pltpu.SMEM)] + [hbm] * 8 + [vmem] * 7,
+        in_specs=[pl.BlockSpec(memory_space=pltpu.SMEM)] + [hbm] * 8 + [vmem] * 5,
         out_specs=[hbm] * 7,
         out_shape=[
             jax.ShapeDtypeStruct((num_rows, chunk_len, d_model), BF16), box, box, box,
@@ -661,8 +664,7 @@
         compiler_params=pltpu.CompilerParams(collective_id=0, has_side_effects=True, vmem_limit_bytes=LAYER_LIMIT),
         cost_estimate=pl.CostEstimate(flops=100_000_000_000, bytes_accessed=chunk_len * d_model * 16, transcendentals=0),
         name="layer",
-    )(lengths, hidden_in, table, k_block, v_block, w_qkv, w_up, w_down, w_out, *norms, b_qkv.astype(F32)[None],
-      b_up.astype(F32).reshape(SLICES, 1, width), extra[None])
+    )(lengths, hidden_in, table, k_block, v_block, w_qkv, w_up, w_down, w_out, *norms, small[None])
     return out, pk, qb
 
 
@@ -673,31 +675,35 @@
     places = [(b, pl.ds(t * tile, tile), t) for b in range(buf.shape[0]) for t in range(pieces)]
     inward = [pltpu.make_async_copy(in_ref.at[b, rows], buf.at[b, rows], in_sem.at[b, t]) for b, rows, t in places]
     outward = [pltpu.make_async_copy(buf.at[b, rows], out_ref.at[b, rows], out_sem.at[b, t]) for b, rows, t in places]
-    lows = [pltpu.make_async_copy(pk.at[n], low.at[n], low_sem.at[n]) for n in range(2)]
-    highs = [pltpu.make_async_copy(qb.at[n], high.at[n], high_sem.at[n]) for n in range(2)]
+    both = 2 * head_dim
+
+    def taken(src, dst, sem):
+        return [[pltpu.make_async_copy(src.at[n, :, pl.ds((3 * h + 1) * head_dim, both)], dst.at[n, :, pl.ds(h * both, both)], sem.at[n, h])
+                 for h in range(heads)] for n in range(2)]
+
+    lows, highs = taken(pk, low, low_sem), taken(qb, high, high_sem)
     stored = []
 
-    def store(src, n, row):
-        for h in range(heads):
-            for p, ref in ((1, k_ref), (2, v_ref)):
-                cols = pl.ds((3 * h + p) * head_dim, head_dim)
-                copy = pltpu.make_async_copy(src.at[:, cols], ref.at[row, h], kv_sem.at[n, h, p - 1])
-                copy.start()
-                stored.append(copy)
-
-    for copy in highs + lows + inward:
+    def store(n, h, row):
+        for p, ref in enumerate((k_ref, v_ref)):
+            cols = pl.ds(h * both + p * head_dim, head_dim)
+            copy = pltpu.make_async_copy(low.at[n, :, cols], ref.at[row, h], kv_sem.at[n, h, p])
+            copy.start()
+            stored.append(copy)
+
+    for copy in highs[0] + highs[1] + lows[0] + lows[1] + inward:
         copy.start()
     j = meta[0]
     for n in range(2):
-        lows[n].wait()
-        store(low.at[n], n, j ^ (2 - 2 * n))
+        for h in range(heads):
+            lows[n][h].wait()
+            store(n, h, j ^ (2 - 2 * n))
     for n in range(2):
-        highs[n].wait()
         for h in range(heads):
-            for p in (1, 2):
-                cols = slice((3 * h + p) * head_dim, (3 * h + p + 1) * head_dim)
-                low[2 + n, :, cols] = high[n, :, cols].astype(BF16)
-        store(low.at[2 + n], 2 + n, j ^ (3 - 2 * n))
+            highs[n][h].wait()
+            cols = slice(h * both, (h + 1) * both)
+            low[2 + n, :, cols] = high[n, :, cols].astype(BF16)
+            store(2 + n, h, j ^ (3 - 2 * n))
     for one, other in zip(inward, outward):
         one.wait()
         other.start()
@@ -707,7 +713,7 @@
 
 def finish(meta, out, pk, qb, heads, head_dim):
     rows, chunk_len, _ = out.shape
-    span = pk.shape[2]
+    span = 2 * heads * head_dim
     hbm = pl.BlockSpec(memory_space=pl.ANY)
     cache = jax.ShapeDtypeStruct((rows, heads, chunk_len, head_dim), BF16)
     dma = pltpu.SemaphoreType.DMA
@@ -718,7 +724,7 @@
         out_shape=[jax.ShapeDtypeStruct(out.shape, out.dtype), cache, cache],
         scratch_shapes=[
             pltpu.VMEM(out.shape, out.dtype), pltpu.VMEM((4, chunk_len, span), BF16), pltpu.VMEM((2, chunk_len, span), F32),
-            dma((rows, 4)), dma((rows, 4)), dma((2,)), dma((2,)), dma((4, heads, 2)),
+            dma((rows, 4)), dma((rows, 4)), dma((2, heads)), dma((2, heads)), dma((4, heads, 2)),
         ],
         compiler_params=pltpu.CompilerParams(vmem_limit_bytes=VMEM_LIMIT),
         name="finish",
@@ -735,9 +741,8 @@
         heads, block_len, head_dim = k_block.shape[1:]
         table = rope_table(lengths, chunk_len, head_dim)
         norms = [p[None] for p in (ln1_gain, ln1_bias, ln2_gain, ln2_bias)]
-        extra = b_out.astype(F32) + b_down.astype(F32)
-        out, pk, qb = run_layer(
-            lengths, hidden_in, table, k_block, v_block, w_qkv, w_up, w_down, w_out, norms, b_qkv, b_up, extra, tp_size)
+        small = jnp.concatenate([b_qkv.astype(F32), b_up.astype(F32), b_out.astype(F32) + b_down.astype(F32)])
+        out, pk, qb = run_layer(lengths, hidden_in, table, k_block, v_block, w_qkv, w_up, w_down, w_out, norms, small, tp_size)
         return tuple(finish(lax.axis_index("cp")[None], out, pk, qb, heads, head_dim))
 
     return jax.shard_map(local_layer, mesh=mesh, in_specs=in_specs, out_specs=out_specs, check_vma=False)

time: 339 us -> 311 us (0.917)
  Pallas kernels: 331 us -> 304 us
    pallas_call x1, Pallas kernels: 311 us -> 286 us  [run_layer(): pl.pallas_call(functools.partial(layer_kernel, tp_size, heads), in_specs=...]
where the time goes in v5:
time: 311 us; the launch traced here: 310 us
  Pallas kernels  304 us (98%)
  other arithmetic  4.94 us (2%)
    pallas_call x1, Pallas kernels, run_layer(): pl.pallas_call(functools.partial(layer_kernel, tp_size, heads), in_specs=...  286 us
    pallas_call x1, Pallas kernels, finish(): pl.pallas_call(functools.partial(finish_kernel, heads), in_specs=[pl.Bloc...  18.3 us

profile of v5, /device:TPU:0, one launch (start us, length us, event | category | flops | bytes accessed | tf_op | source)
XLA Modules:
  0.0 310.3 jit_solution(15050723416903527901)
XLA Ops:
  0.6 0.7 add_convert_fusion
  1.4 1.0 multiply_cosine_fusion
  2.4 1.1 pad_maximum_fusion.table
  3.5 0.7 convert_add_fusion
  4.2 0.7 convert_element_type.20
  4.9 0.7 convert_element_type.21
  5.6 0.6 broadcast_in_dim.26.small
  6.2 285.7 %layer.1 = (bf16[4,1024,2048]{2,1,0:T(8,128)(2,1)}, f32[1024,2048]{1,0:T(8,128)}, f32[1024,2048]{1,0:T(8,128)}, f32[1024,2048]{1,0:T(8,128)}, bf16[2,1024,1536]{...) custom-call(s32[4]{0:T(128)} %lengths.1, bf16[4,1024,2048]{2,1,0:T(8,128)(2,1)} %hidden.1, ...), custom_call_target="tpu_custom_call" | custom-call | flops 99999997952 | bytes 33554432 | tf_op jit(solution)/shard_map/layer/pallas_call | solution.py:632
  291.9 18.3 %finish.1 = (bf16[4,1024,2048]{2,1,0:T(8,128)(2,1)}, bf16[4,4,1024,128]{3,2,1,0:T(8,128)(2,1)}, bf16[4,4,1024,128]{3,2,1,0:T(8,128)(2,1)}) custom-call(s32[1]{0:T(128)} %bitcast.meta, bf16[4,1024,2048]{2,1,0:T(8,128)(2,1)} %get-tuple-element.6.in_ref, bf16[2,1024,1536]{2,1,0:T(8,128)(2,1)} %get-tuple-element.7.pk, f32[2,1024,1536]{2,1,0:T(8,128)} %get-tuple-element.8.qb), custom_call_target="tpu_custom_call" | custom-call | tf_op jit(solution)/shard_map/finish/pallas_call | solution.py:720
  (2 shorter events, 0.0 us)

commit v6 on v5

--- a/solution.py
+++ b/solution.py
@@ -24,7 +24,7 @@
 BLOCKS = 8
 SLICES = 4
 TILES = 4
-HALVES = 2
+HALVES = 4
 LAG_START = 2
 LAG_AHEAD = 1
 LAG_BACK = 1
@@ -109,10 +109,11 @@
 def layer_kernel(tp_size, heads, lengths, hidden, table, k_cache, v_cache, w_qkv, w_up, w_down, w_out,
                  gain1, bias1, gain2, bias2, small,
                  out_ref, y_box, core_box, last_box, pk, qb, ob,
-                 acc, from_left, from_right, up, down, proj, x_big, tab_buf, kv, ob_far, m_scr, l_scr, o_scr, st, sbox,
+                 acc, from_left, from_right, up, down, proj, mine, x_big, tab_buf, kv, ob_far, m_scr, l_scr, o_scr, st, sbox,
                  stage, land,
-                 up_sem, down_sem, proj_sem, xb_sem, tab_sem, pk_sem, kv_sem, q_sem, x_sem, o_sem,
-                 qs_sem, qr_sem, fs_sem, fr_sem, ns_sem, nr_sem, ys_sem, yr_sem, ss_sem, sr_sem,
+                 up_sem, down_sem, proj_sem, xb_sem, tab_sem, pk_sem, mine_sem, kv_sem, q_sem, x_sem, o_sem,
+                 qs_sem, qr_sem, fs_sem, fr_sem, ns_sem, nr_sem, ys_sem, yr_sem,
+                 fss_sem, fsr_sem, nss_sem, nsr_sem, yss_sem, ysr_sem,
                  left_sem, right_sem, y_sem, core_sem, last_sem, send_sem, stage_sem, land_sem):
     z = lax.axis_index("tp")
     j = lax.axis_index("cp")
@@ -136,6 +137,8 @@
     scale = head_dim ** -0.5 * LOG2E
     own_at, sent_at, kept_at, q_at = 0, span, 2 * span, 3 * span
     extra_at = 3 * span + SLICES * width
+    per_half = BLOCKS // HALVES
+    waited = per_half * SLICES
 
     def rows_of(n, size):
         return pl.ds(pl.multiple_of(n * size, size), size)
@@ -205,28 +208,28 @@
             src_ref=src, dst_ref=dst, send_sem=send, recv_sem=arrive, device_id={"cp": across}, device_id_type=MESH)
 
 
+    def staged(t, part):
+        return acc.at[rows_of(t, tile), pl.ds(part * span, span)]
+
     def sent_tile(n, t):
-        slot = lax.rem(t, 2)
-        return to_core(acc.at[rows_of(slot, tile), pl.ds(0, 3 * span)], qb.at[n, rows_of(t, tile), :], qs_sem.at[slot], qr_sem.at[n, t])
-
-    wait(qkv_copies)
-    wait(tab_copies)
-
-    @pl.loop(0, 2 * TILES)
-    def _(i):
-        n, t, slot = lax.div(i, TILES), lax.rem(i, TILES), lax.rem(i, 2)
+        return [to_core(staged(t, p), qb.at[n, rows_of(t, tile), pl.ds(p * span, span)], qs_sem.at[n, t, p], qr_sem.at[n, t, p])
+                for p in range(3)]
+
+    def sent_off(n, t):
+        for copy in sent_tile(n, t):
+            copy.wait_send()
+
+    def project(n, t, place):
+        i = n * TILES + t
 
         @pl.when(i + 1 < 2 * TILES)
         def _():
             big_x(i + 1).start()
 
         big_x(i).wait()
-
-        @pl.when(i >= 2)
-        def _():
-            sent_tile(n, t).wait_send()
-
-        normed = layer_norm(x_big[slot], gain1[...], bias1[...])
+        if n == 1:
+            sent_off(0, t)
+        normed = layer_norm(x_big[lax.rem(i, 2)], gain1[...], bias1[...])
         tab = tab_buf[n, :, rows_of(t, tile)]
         tab = jnp.concatenate([tab] * (head_dim // tab.shape[0]), axis=0).T
         lane = lax.broadcasted_iota(jnp.int32, tab.shape, 1)
@@ -238,80 +241,88 @@
             other = jnp.where(lane < half_rot, pltpu.roll(long, head_dim - half_rot, 1), pltpu.roll(long, half_rot, 1))
             return (long * cos_tab + other * sin_tab).astype(BF16)
 
-        place = down.at[n * HALVES + lax.div(t, TILES // HALVES), rows_of(lax.rem(t, TILES // HALVES), tile), :]
-        hold = acc.at[rows_of(slot, tile), :]
-        for s in range(3):
-            part = slice(s * width, (s + 1) * width)
-            some = (jnp.dot(normed, up[s], preferred_element_type=F32) + small[:, part]).astype(BF16)
-            for g in range(width // head_dim):
-                group = s * (width // head_dim) + g
+        for p in range(3):
+            part = slice(p * span, (p + 1) * span)
+            some = (jnp.dot(normed, up[p], preferred_element_type=F32) + small[:, part]).astype(BF16)
+            for g in range(heads):
+                group = p * heads + g
                 values = some[:, g * head_dim:(g + 1) * head_dim]
                 if group % 3 < 2:
                     values = rotate(values)
-                cols = slice(group * head_dim, (group + 1) * head_dim)
-                place[:, cols] = values
-                hold[:, cols] = values.astype(F32)
-        sent_tile(n, t).start()
+                place[:, group * head_dim:(group + 1) * head_dim] = values
+                staged(t, p)[:, g * head_dim:(g + 1) * head_dim] = values.astype(F32)
+        start(sent_tile(n, t))
+
+    per_slice = width // tile
+
+    def far_place(t):
+        return down.at[lax.div(t, per_slice), rows_of(lax.rem(t, per_slice), tile), pl.ds(0, 3 * span)]
+
+    def mine_out(t):
+        return pltpu.make_async_copy(mine.at[t], pk.at[1, rows_of(t, tile), :], mine_sem.at[t])
+
+    wait(qkv_copies)
+    wait(tab_copies)
+
+    @pl.loop(0, TILES)
+    def _(t):
+        project(0, t, far_place(t))
+
+    pack_copies = [pltpu.make_async_copy(far_place(t), pk.at[0, rows_of(t, tile), :], pk_sem.at[t]) for t in range(TILES)]
+    start(pack_copies)
+
+    @pl.loop(0, TILES)
+    def _(t):
+        project(1, t, mine.at[t])
+        mine_out(t).start()
 
     for f in range(SLICES):
         weight_copies(f)[0].start()
-    pack_copies = [
-        pltpu.make_async_copy(down.at[n * HALVES + e, pl.ds(0, half), pl.ds(0, 3 * span)], pk.at[n, pl.ds(e * half, half), :],
-                              pk_sem.at[n, e])
-        for n in range(2) for e in range(HALVES)]
-    start(pack_copies)
-    for t in range(2):
-        sent_tile(1, TILES - 2 + t).wait_send()
 
 
     def got_queries(n):
         for t in range(TILES):
-            sent_tile(n, t).wait_recv()
+            for copy in sent_tile(n, t):
+                copy.wait_recv()
         copies = [pltpu.make_async_copy(qb.at[n, :, pl.ds(3 * h * head_dim, head_dim)],
                                         acc.at[:, pl.ds(q_at + h * head_dim, head_dim)], q_sem.at[h]) for h in range(heads)]
         start(copies)
         return copies
 
-    def attend(row, slot, query, at, kind, after=None, own=False):
+    def attend(row, slot, query, e):
         valid = jnp.clip(lengths[row] - j * slots, 0, slots)
-
-        @pl.loop(0, HALVES)
-        def _(e):
-            def keys(h):
-                return kv[slot, 0, h]
-
-            def values(h):
-                return kv[slot, 1, h]
-
-            mask = lax.broadcasted_iota(jnp.int32, (half, slots), 1) < valid
-            first_step(heads, scale, lambda h: query(e, h), keys, values, m_scr, l_scr, o_scr, mask)
-
-            def own_block(b, mask):
-                def part(p):
-                    return lambda h: down[HALVES + b, :half, (3 * h + p) * head_dim:(3 * h + p + 1) * head_dim]
-
-                block_step(heads, scale, lambda h: query(e, h), part(1), part(2), m_scr, l_scr, o_scr, mask)
-
-            if own:
-                @pl.loop(0, e)
-                def _(b):
-                    own_block(b, None)
-
-                shape = (half, half)
-                own_block(e, lax.broadcasted_iota(jnp.int32, shape, 0) >= lax.broadcasted_iota(jnp.int32, shape, 1))
-
-            lane = lax.broadcasted_iota(jnp.int32, (half, head_dim), 1)
-            stats = jnp.zeros((half, head_dim), F32)
-            for h in range(heads):
-                stats = jnp.where(lane == h, m_scr[h], stats)
-                stats = jnp.where(lane == heads + h, jnp.sum(l_scr[h], axis=1, keepdims=True), stats)
-                acc[rows_of(e, half), at + h * head_dim:at + (h + 1) * head_dim] = o_scr[h]
-            st[kind, :, rows_of(e, half)] = stats.T[:8]
-            if after is not None:
-                after(e)
-
-    def held(n):
-        return lambda e, h: down[n * HALVES + e, :half, 3 * h * head_dim:(3 * h + 1) * head_dim]
+        mask = lax.broadcasted_iota(jnp.int32, (half, slots), 1) < valid
+        first_step(heads, scale, lambda h: query(e, h), lambda h: kv[slot, 0, h], lambda h: kv[slot, 1, h],
+                   m_scr, l_scr, o_scr, mask)
+
+    def attend_own(e):
+        def own_block(b, mask):
+            def part(p):
+                return lambda h: mine[b, :, (3 * h + p) * head_dim:(3 * h + p + 1) * head_dim]
+
+            block_step(heads, scale, lambda h: held_mine(e, h), part(1), part(2), m_scr, l_scr, o_scr, mask)
+
+        @pl.loop(0, e)
+        def _(b):
+            own_block(b, None)
+
+        shape = (half, half)
+        own_block(e, lax.broadcasted_iota(jnp.int32, shape, 0) >= lax.broadcasted_iota(jnp.int32, shape, 1))
+
+    def keep(e, at, kind):
+        lane = lax.broadcasted_iota(jnp.int32, (half, head_dim), 1)
+        stats = jnp.zeros((half, head_dim), F32)
+        for h in range(heads):
+            stats = jnp.where(lane == h, m_scr[h], stats)
+            stats = jnp.where(lane == heads + h, jnp.sum(l_scr[h], axis=1, keepdims=True), stats)
+            acc[rows_of(e, half), at + h * head_dim:at + (h + 1) * head_dim] = o_scr[h]
+        st[kind, :, rows_of(e, half)] = stats.T[:8]
+
+    def held_far(e, h):
+        return far_place(e)[:, 3 * h * head_dim:(3 * h + 1) * head_dim]
+
+    def held_mine(e, h):
+        return mine[e, :, 3 * h * head_dim:(3 * h + 1) * head_dim]
 
     def taken(e, h):
         return acc[rows_of(e, half), q_at + h * head_dim:q_at + (h + 1) * head_dim].astype(BF16)
@@ -322,57 +333,81 @@
     def near_piece(e):
         return to_core(acc.at[rows_of(e, half), pl.ds(sent_at, span)], ob.at[0, rows_of(e, half), :], ns_sem.at[e], nr_sem.at[e])
 
-    def y_piece(b):
-        return to_y(acc.at[rows_of(b, block), pl.ds(kept_at, span)], ob.at[1, rows_of(b, block), :], ys_sem.at[b], yr_sem.at[b])
-
-    far_stats = to_core(st.at[0], sbox.at[0], ss_sem.at[0], sr_sem.at[0])
-    y_stats = to_y(st.at[1], sbox.at[2], ss_sem.at[1], sr_sem.at[2])
-    near_stats = to_core(st.at[2], sbox.at[1], ss_sem.at[2], sr_sem.at[1])
+    def y_piece(e):
+        return to_y(acc.at[rows_of(e, half), pl.ds(kept_at, span)], ob.at[1, rows_of(e, half), :], ys_sem.at[e], yr_sem.at[e])
+
+    def far_stats(e):
+        return to_core(st.at[0, :, rows_of(e, half)], sbox.at[0, :, rows_of(e, half)], fss_sem.at[e], fsr_sem.at[e])
+
+    def near_stats(e):
+        return to_core(st.at[2, :, rows_of(e, half)], sbox.at[1, :, rows_of(e, half)], nss_sem.at[e], nsr_sem.at[e])
+
+    def y_stats(e):
+        return to_y(st.at[1, :, rows_of(e, half)], sbox.at[2, :, rows_of(e, half)], yss_sem.at[e], ysr_sem.at[e])
 
     wait(got_queries(0))
     wait(cache_copies(corner, 0))
-    attend(corner, 0, taken, sent_at, 0, after=lambda e: far_piece(e).start())
-    far_stats.start()
+
+    @pl.loop(0, HALVES)
+    def _(e):
+        sent_off(1, e)
+        attend(corner, 0, taken, e)
+        keep(e, sent_at, 0)
+        far_stats(e).start()
+        far_piece(e).start()
+
     start(cache_copies(mate, 0))
     near_queries = got_queries(1)
     wait(cache_copies(across, 1))
-    attend(across, 1, held(0), kept_at, 1)
-    start(cache_copies(j, 1))
-
-    far_stats.wait()
-    _, weights, total = piece_weights(heads, [st[1], sbox[0]], head_dim)
-    peak = jnp.maximum(st[1, :heads, :], sbox[0, :heads, :])
-
-    st[1, :heads, :] = peak
-    st[1, heads:2 * heads, :] = total
-    y_stats.start()
 
     @pl.loop(0, HALVES)
     def _(e):
+        attend(across, 1, held_far, e)
+        keep(e, kept_at, 1)
+
+        far_stats(e).wait_recv()
         far_piece(e).wait_recv()
-
-    for b in range(BLOCKS):
-        part = slice(b * block, (b + 1) * block)
-        columns = as_columns([w[:, part] for w in weights], head_dim)
+        rows = rows_of(e, half)
+        peak, weights, total = piece_weights(heads, [st[1, :, rows], sbox[0, :, rows]], head_dim)
+        columns = as_columns(weights, head_dim)
         for h in range(heads):
-            mine = slice(kept_at + h * head_dim, kept_at + (h + 1) * head_dim)
-            acc[part, mine] = (acc[part, mine] * columns[:, h:h + 1]
-                               + ob_far[part, h * head_dim:(h + 1) * head_dim] * columns[:, heads + h:heads + h + 1])
-        y_piece(b).start()
-
+            at = kept_at + h * head_dim
+            acc[rows, at:at + head_dim] = (acc[rows, at:at + head_dim] * columns[:, h:h + 1]
+                                           + ob_far[rows, h * head_dim:(h + 1) * head_dim] * columns[:, heads + h:heads + h + 1])
+        st[1, :heads, rows] = peak
+        st[1, heads:2 * heads, rows] = total
+        y_stats(e).start()
+        y_piece(e).start()
+
+    start(cache_copies(j, 1))
+    wait(pack_copies)
+    for f in range(SLICES):
+        weight_copies(f)[1].start()
     for e in range(HALVES):
+        far_stats(e).wait_send()
         far_piece(e).wait_send()
     wait(near_queries)
     wait(cache_copies(mate, 0))
-    attend(mate, 0, taken, sent_at, 2, after=lambda e: near_piece(e).start())
-    near_stats.start()
     wait(cache_copies(j, 1))
-    wait(pack_copies)
-    for f in range(HALVES):
-        weight_copies(f)[1].start()
-    attend(j, 1, held(1), own_at, 3, own=True)
-    for f in range(HALVES, SLICES):
-        weight_copies(f)[1].start()
+    proj_copy.wait()
+
+
+    def near(e, phase):
+        @pl.when(phase == 2)
+        def _():
+            attend(mate, 0, taken, e)
+            keep(e, sent_at, 2)
+            near_stats(e).start()
+            near_piece(e).start()
+
+        @pl.when(phase == 4)
+        def _():
+            attend(j, 1, held_mine, e)
+
+        @pl.when(phase == 5)
+        def _():
+            attend_own(e)
+            keep(e, own_at, 3)
 
     def block_copies(b):
         rows = rows_of(b, block)
@@ -381,17 +416,15 @@
             pltpu.make_async_copy(ob.at[n, rows, :], ob_far.at[rows_of(2 * slot + n, block), :], o_sem.at[slot, n]) for n in range(2)]
 
     def fetch(b):
-        y_piece(b).wait_recv()
+        @pl.when(lax.rem(b, per_half) == 0)
+        def _():
+            e = lax.div(b, per_half)
+            near_stats(e).wait_recv()
+            near_piece(e).wait_recv()
+            y_stats(e).wait_recv()
+            y_piece(e).wait_recv()
+
         start(block_copies(b))
-
-    near_stats.wait()
-    y_stats.wait()
-    for e in range(HALVES):
-        near_piece(e).wait_recv()
-        near_piece(e).wait_send()
-    proj_copy.wait()
-    fetch(0)
-
 
     def begin(b):
         slot = lax.rem(b, 2)
@@ -402,7 +435,13 @@
             fetch(b + 1)
 
         wait(block_copies(b))
-        y_piece(b).wait_send()
+
+        @pl.when(lax.rem(b, per_half) == 0)
+        def _():
+            e = lax.div(b, per_half)
+            for copy in (near_stats(e), near_piece(e), y_stats(e), y_piece(e)):
+                copy.wait_send()
+
         _, weights, total = piece_weights(heads, [st[3, :, rows], sbox[1, :, rows], sbox[2, :, rows]], head_dim)
         columns = as_columns([w / total for w in weights], head_dim)
         for h in range(heads):
@@ -577,9 +616,19 @@
 
     lead = SLICES + LAG_START
 
-    @pl.loop(0, lead + pairs + LAG_LAST + 2)
-    def _(s):
-        @pl.when(s < BLOCKS * SLICES)
+    @pl.loop(0, waited + lead + pairs + LAG_LAST + 2)
+    def _(step):
+        s = step - waited
+
+        @pl.when(step < HALVES * waited)
+        def _():
+            near(lax.div(step, waited), lax.rem(step, waited))
+
+        @pl.when(step == waited - 1)
+        def _():
+            fetch(0)
+
+        @pl.when(jnp.logical_and(s >= 0, s < BLOCKS * SLICES))
         def _():
             b, f = lax.div(s, SLICES), lax.rem(s, SLICES)
             when(f == 0, begin, b)
@@ -610,6 +659,8 @@
 
     for which in (2, 3, 4):
         drained(acc, which)
+    for t in range(TILES):
+        mine_out(t).wait()
     for stream in range(4):
         for slot in range(STAGES):
             pltpu.make_async_copy(stage.at[stream, slot], at(out_ref.at[0], 0), stage_sem.at[stream, slot]).wait()
@@ -644,6 +695,7 @@
             pltpu.VMEM((SLICES, d_model, width), BF16),
             pltpu.VMEM((SLICES, width, d_model), BF16),
             pltpu.VMEM((span, d_model), BF16),
+            pltpu.VMEM((TILES, tile, 3 * span), BF16),
             pltpu.VMEM((2, tile, d_model), BF16),
             pltpu.VMEM((2,) + table.shape[1:], F32),
             pltpu.VMEM((2, 2, heads, slots, head_dim), BF16),
@@ -656,9 +708,10 @@
             pltpu.VMEM((4, STAGES, tokens, d_model), BF16),
             pltpu.VMEM((3, STAGES, tokens, d_model), F32),
         ]
-        + [dma((SLICES,)), dma((SLICES,)), dma, dma((2,)), dma((2,)), dma((2, HALVES)), dma((2, 2)), dma((heads,)), dma((2,)), dma((2, 2))]
-        + [dma((2,)), dma((2, TILES)), dma((HALVES,)), dma((HALVES,)), dma((HALVES,)), dma((HALVES,)), dma((BLOCKS,)), dma((BLOCKS,)),
-           dma((3,)), dma((3,))]
+        + [dma((SLICES,)), dma((SLICES,)), dma, dma((2,)), dma((2,)), dma((TILES,)), dma((TILES,)), dma((2, 2)), dma((heads,)),
+           dma((2,)), dma((2, 2))]
+        + [dma((2, TILES, 3))] * 2
+        + [dma((HALVES,))] * 12
         + [dma((CHUNKS,))] * 5
         + [dma((5,)), dma((4, STAGES)), dma((3, STAGES))],
         compiler_params=pltpu.CompilerParams(collective_id=0, has_side_effects=True, vmem_limit_bytes=LAYER_LIMIT),

time: 311 us -> 300 us (0.965)
  Pallas kernels: 304 us -> 293 us
    pallas_call x1, Pallas kernels: 286 us -> 275 us  [run_layer(): pl.pallas_call(functools.partial(layer_kernel, tp_size, heads), in_specs=...]
where the time goes in v6:
time: 300 us
  Pallas kernels  293 us (98%)
  other arithmetic  4.94 us (2%)
    pallas_call x1, Pallas kernels, run_layer(): pl.pallas_call(functools.partial(layer_kernel, tp_size, heads), in_specs=...  275 us
    pallas_call x1, Pallas kernels, finish(): pl.pallas_call(functools.partial(finish_kernel, heads), in_specs=[pl.Bloc...  18.3 us

profile of v6, /device:TPU:0, one launch (start us, length us, event | category | flops | bytes accessed | tf_op | source)
XLA Modules:
  0.0 299.7 jit_solution(10510159587520258072)
XLA Ops:
  0.6 0.7 add_convert_fusion
  1.4 1.0 multiply_cosine_fusion
  2.4 1.1 pad_maximum_fusion.table
  3.5 0.7 convert_add_fusion
  4.2 0.7 convert_element_type.20
  4.9 0.7 convert_element_type.21
  5.6 0.6 broadcast_in_dim.26.small
  6.2 275.1 %layer.1 = (bf16[4,1024,2048]{2,1,0:T(8,128)(2,1)}, f32[1024,2048]{1,0:T(8,128)}, f32[1024,2048]{1,0:T(8,128)}, f32[1024,2048]{1,0:T(8,128)}, bf16[2,1024,1536]{...) custom-call(s32[4]{0:T(128)} %lengths.1, bf16[4,1024,2048]{2,1,0:T(8,128)(2,1)} %hidden.1, ...), custom_call_target="tpu_custom_call" | custom-call | flops 99999997952 | bytes 33554432 | tf_op jit(solution)/shard_map/layer/pallas_call | solution.py:683
  281.3 18.3 %finish.1 = (bf16[4,1024,2048]{2,1,0:T(8,128)(2,1)}, bf16[4,4,1024,128]{3,2,1,0:T(8,128)(2,1)}, bf16[4,4,1024,128]{3,2,1,0:T(8,128)(2,1)}) custom-call(s32[1]{0:T(128)} %bitcast.meta, bf16[4,1024,2048]{2,1,0:T(8,128)(2,1)} %get-tuple-element.6.in_ref, bf16[2,1024,1536]{2,1,0:T(8,128)(2,1)} %get-tuple-element.7.pk, f32[2,1024,1536]{2,1,0:T(8,128)} %get-tuple-element.8.qb), custom_call_target="tpu_custom_call" | custom-call | tf_op jit(solution)/shard_map/finish/pallas_call | solution.py:773
  (2 shorter events, 0.0 us)

commit v7 on v6

--- a/solution.py
+++ b/solution.py
@@ -69,10 +69,18 @@
     return functools.reduce(jnp.maximum, [values[:, n:n + lanes] for n in range(0, values.shape[1], lanes)])
 
 
+def ahead(heads, scores):
+    coming = scores(0)
+    for h in range(heads):
+        now = coming
+        if h + 1 < heads:
+            coming = scores(h + 1)
+        yield h, now
+
+
 def first_step(heads, scale, q_of, k_of, v_of, m_scr, l_scr, o_scr, mask):
-    for h in range(heads):
-        lanes = o_scr.shape[2]
-        scores = scores_of(q_of(h), k_of(h), scale, mask)
+    lanes = o_scr.shape[2]
+    for h, scores in ahead(heads, lambda h: scores_of(q_of(h), k_of(h), scale, mask)):
         peak = jnp.maximum(jnp.max(lane_max(scores, lanes), axis=1, keepdims=True), EMPTY)
         peak = jnp.broadcast_to(peak, m_scr.shape[1:])
         probs = jnp.exp2(scores - wide(peak, scores.shape[1]))
@@ -82,9 +90,8 @@
 
 
 def block_step(heads, scale, q_of, k_of, v_of, m_scr, l_scr, o_scr, mask):
-    for h in range(heads):
-        lanes = o_scr.shape[2]
-        scores = scores_of(q_of(h), k_of(h), scale, mask)
+    lanes = o_scr.shape[2]
+    for h, scores in ahead(heads, lambda h: scores_of(q_of(h), k_of(h), scale, mask)):
         m_old = m_scr[h]
         m_new = jnp.maximum(m_old, jnp.max(lane_max(scores, lanes), axis=1, keepdims=True))
         probs = jnp.exp2(scores - wide(m_new, scores.shape[1]))
@@ -109,7 +116,7 @@
 def layer_kernel(tp_size, heads, lengths, hidden, table, k_cache, v_cache, w_qkv, w_up, w_down, w_out,
                  gain1, bias1, gain2, bias2, small,
                  out_ref, y_box, core_box, last_box, pk, qb, ob,
-                 acc, from_left, from_right, up, down, proj, mine, x_big, tab_buf, kv, ob_far, m_scr, l_scr, o_scr, st, sbox,
+                 acc, from_left, from_right, up, down, proj, mine, far_q, x_big, tab_buf, kv, ob_far, m_scr, l_scr, o_scr, st, sbox,
                  stage, land,
                  up_sem, down_sem, proj_sem, xb_sem, tab_sem, pk_sem, mine_sem, kv_sem, q_sem, x_sem, o_sem,
                  qs_sem, qr_sem, fs_sem, fr_sem, ns_sem, nr_sem, ys_sem, yr_sem,
@@ -241,9 +248,8 @@
             other = jnp.where(lane < half_rot, pltpu.roll(long, head_dim - half_rot, 1), pltpu.roll(long, half_rot, 1))
             return (long * cos_tab + other * sin_tab).astype(BF16)
 
-        for p in range(3):
-            part = slice(p * span, (p + 1) * span)
-            some = (jnp.dot(normed, up[p], preferred_element_type=F32) + small[:, part]).astype(BF16)
+        for p, product in ahead(3, lambda p: jnp.dot(normed, up[p], preferred_element_type=F32)):
+            some = (product + small[:, p * span:(p + 1) * span]).astype(BF16)
             for g in range(heads):
                 group = p * heads + g
                 values = some[:, g * head_dim:(g + 1) * head_dim]
@@ -268,6 +274,9 @@
     def _(t):
         project(0, t, far_place(t))
 
+    for t in range(TILES):
+        for h in range(heads):
+            far_q[t, :, h * head_dim:(h + 1) * head_dim] = far_place(t)[:, 3 * h * head_dim:(3 * h + 1) * head_dim]
     pack_copies = [pltpu.make_async_copy(far_place(t), pk.at[0, rows_of(t, tile), :], pk_sem.at[t]) for t in range(TILES)]
     start(pack_copies)
 
@@ -280,14 +289,15 @@
         weight_copies(f)[0].start()
 
 
-    def got_queries(n):
+    def arrived_tiles(n):
         for t in range(TILES):
             for copy in sent_tile(n, t):
                 copy.wait_recv()
-        copies = [pltpu.make_async_copy(qb.at[n, :, pl.ds(3 * h * head_dim, head_dim)],
-                                        acc.at[:, pl.ds(q_at + h * head_dim, head_dim)], q_sem.at[h]) for h in range(heads)]
-        start(copies)
-        return copies
+
+    def query_copies(n, part):
+        rows = pl.ds(part * (chunk_len // 2), chunk_len // 2)
+        return [pltpu.make_async_copy(qb.at[n, rows, pl.ds(3 * h * head_dim, head_dim)],
+                                      acc.at[rows, pl.ds(q_at + h * head_dim, head_dim)], q_sem.at[part, h]) for h in range(heads)]
 
     def attend(row, slot, query, e):
         valid = jnp.clip(lengths[row] - j * slots, 0, slots)
@@ -319,7 +329,7 @@
         st[kind, :, rows_of(e, half)] = stats.T[:8]
 
     def held_far(e, h):
-        return far_place(e)[:, 3 * h * head_dim:(3 * h + 1) * head_dim]
+        return far_q[e, :, h * head_dim:(h + 1) * head_dim]
 
     def held_mine(e, h):
         return mine[e, :, 3 * h * head_dim:(3 * h + 1) * head_dim]
@@ -345,26 +355,15 @@
     def y_stats(e):
         return to_y(st.at[1, :, rows_of(e, half)], sbox.at[2, :, rows_of(e, half)], yss_sem.at[e], ysr_sem.at[e])
 
-    wait(got_queries(0))
-    wait(cache_copies(corner, 0))
-
-    @pl.loop(0, HALVES)
-    def _(e):
-        sent_off(1, e)
+    def far_sent(e):
         attend(corner, 0, taken, e)
         keep(e, sent_at, 0)
         far_stats(e).start()
         far_piece(e).start()
 
-    start(cache_copies(mate, 0))
-    near_queries = got_queries(1)
-    wait(cache_copies(across, 1))
-
-    @pl.loop(0, HALVES)
-    def _(e):
+    def far_kept(e):
         attend(across, 1, held_far, e)
         keep(e, kept_at, 1)
-
         far_stats(e).wait_recv()
         far_piece(e).wait_recv()
         rows = rows_of(e, half)
@@ -379,35 +378,105 @@
         y_stats(e).start()
         y_piece(e).start()
 
+    first = HALVES // 2
+    arrived_tiles(0)
+    for part in range(2):
+        start(query_copies(0, part))
+    for part in range(2):
+        wait(query_copies(0, part))
+    wait(cache_copies(corner, 0))
+
+    @pl.loop(0, first)
+    def _(e):
+        sent_off(1, e)
+        far_sent(e)
+
+    for e in range(first, HALVES):
+        sent_off(1, e)
+    start(cache_copies(mate, 0))
+    arrived_tiles(1)
+    start(query_copies(1, 0))
+    wait(cache_copies(across, 1))
+
+    @pl.loop(0, first)
+    def _(e):
+        far_kept(e)
+
     start(cache_copies(j, 1))
     wait(pack_copies)
     for f in range(SLICES):
         weight_copies(f)[1].start()
-    for e in range(HALVES):
+    wait(query_copies(1, 0))
+    proj_copy.wait()
+
+
+    def near_mate(e):
         far_stats(e).wait_send()
         far_piece(e).wait_send()
-    wait(near_queries)
-    wait(cache_copies(mate, 0))
-    wait(cache_copies(j, 1))
-    proj_copy.wait()
-
-
-    def near(e, phase):
-        @pl.when(phase == 2)
-        def _():
-            attend(mate, 0, taken, e)
-            keep(e, sent_at, 2)
-            near_stats(e).start()
-            near_piece(e).start()
-
-        @pl.when(phase == 4)
+        attend(mate, 0, taken, e)
+        keep(e, sent_at, 2)
+        near_stats(e).start()
+        near_piece(e).start()
+
+    def near_own(e):
+        attend_own(e)
+        keep(e, own_at, 3)
+
+    def tasks(step):
+        e, phase = lax.div(step, waited), lax.rem(step, waited)
+
+        def at(n):
+            return phase == n
+
+        @pl.when(step == 0)
+        def _():
+            wait(cache_copies(mate, 0))
+            wait(cache_copies(j, 1))
+
+        @pl.when(at(1))
+        def _():
+            @pl.when(step == first * waited + 1)
+            def _():
+                wait(query_copies(1, 1))
+                wait(cache_copies(mate, 0))
+                wait(cache_copies(j, 1))
+
+            near_mate(e)
+
+        @pl.when(at(2))
         def _():
             attend(j, 1, held_mine, e)
 
-        @pl.when(phase == 5)
-        def _():
-            attend_own(e)
-            keep(e, own_at, 3)
+        @pl.when(at(3))
+        def _():
+            near_own(e)
+
+        @pl.when(step == (first - 1) * waited + 2)
+        def _():
+            start(cache_copies(corner, 0))
+
+        @pl.when(step == (first - 1) * waited + 3)
+        def _():
+            start(cache_copies(across, 1))
+
+        for n in range(HALVES - first):
+            @pl.when(step == (first - 1) * waited + 4 + 2 * n)
+            def _():
+                if n == 0:
+                    wait(cache_copies(corner, 0))
+                far_sent(first + n)
+
+            @pl.when(step == (first - 1) * waited + 5 + 2 * n)
+            def _():
+                if n == 0:
+                    wait(cache_copies(across, 1))
+                far_kept(first + n)
+
+        @pl.when(step == first * waited)
+        def _():
+            start(query_copies(1, 1))
+            start(cache_copies(mate, 0))
+            start(cache_copies(j, 1))
 
     def block_copies(b):
         rows = rows_of(b, block)
@@ -457,7 +526,7 @@
 
         @pl.when(z == 0)
         def _():
-            acc[rows, :] += x.astype(F32) + small[:, extra_at:]
+            acc[rows, :] += x.astype(F32) + (small[:, extra_at:extra_at + d_model] + small[:, extra_at + d_model:])
 
     def slice_of(b, f):
         rows = rows_of(b, block)
@@ -622,7 +691,7 @@
 
         @pl.when(step < HALVES * waited)
         def _():
-            near(lax.div(step, waited), lax.rem(step, waited))
+            tasks(step)
 
         @pl.when(step == waited - 1)
         def _():
@@ -696,6 +765,7 @@
             pltpu.VMEM((SLICES, width, d_model), BF16),
             pltpu.VMEM((span, d_model), BF16),
             pltpu.VMEM((TILES, tile, 3 * span), BF16),
+            pltpu.VMEM((TILES, tile, span), BF16),
             pltpu.VMEM((2, tile, d_model), BF16),
             pltpu.VMEM((2,) + table.shape[1:], F32),
             pltpu.VMEM((2, 2, heads, slots, head_dim), BF16),
@@ -708,7 +778,7 @@
             pltpu.VMEM((4, STAGES, tokens, d_model), BF16),
             pltpu.VMEM((3, STAGES, tokens, d_model), F32),
         ]
-        + [dma((SLICES,)), dma((SLICES,)), dma, dma((2,)), dma((2,)), dma((TILES,)), dma((TILES,)), dma((2, 2)), dma((heads,)),
+        + [dma((SLICES,)), dma((SLICES,)), dma, dma((2,)), dma((2,)), dma((TILES,)), dma((TILES,)), dma((2, 2)), dma((2, heads)),
            dma((2,)), dma((2, 2))]
         + [dma((2, TILES, 3))] * 2
         + [dma((HALVES,))] * 12
@@ -794,7 +864,7 @@
         heads, block_len, head_dim = k_block.shape[1:]
         table = rope_table(lengths, chunk_len, head_dim)
         norms = [p[None] for p in (ln1_gain, ln1_bias, ln2_gain, ln2_bias)]
-        small = jnp.concatenate([b_qkv.astype(F32), b_up.astype(F32), b_out.astype(F32) + b_down.astype(F32)])
+        small = jnp.concatenate([b_qkv, b_up, b_out, b_down]).astype(F32)
         out, pk, qb = run_layer(lengths, hidden_in, table, k_block, v_block, w_qkv, w_up, w_down, w_out, norms, small, tp_size)
         return tuple(finish(lax.axis_index("cp")[None], out, pk, qb, heads, head_dim))
 

time: 300 us -> 302 us (level)
  no operation moved by 1% of the time
where the time goes in v7:
time: 302 us
  Pallas kernels  295 us (98%)
  other arithmetic  3.49 us (1%)
    pallas_call x1, Pallas kernels, run_layer(): pl.pallas_call(functools.partial(layer_kernel, tp_size, heads), in_specs=...  276 us
    pallas_call x1, Pallas kernels, finish(): pl.pallas_call(functools.partial(finish_kernel, heads), in_specs=[pl.Bloc...  18.3 us

profile of v7, /device:TPU:0, one launch (start us, length us, event | category | flops | bytes accessed | tf_op | source)
XLA Modules:
  0.0 301.8 jit_solution(1788507560296258992)
XLA Ops:
  0.6 0.7 add_convert_fusion
  1.4 1.0 multiply_cosine_fusion
  2.4 1.1 pad_maximum_fusion.table
  3.5 0.7 concatenate.23
  4.2 0.7 concatenate.24
  4.9 0.7 concatenate.25
  5.6 0.7 concatenate.22
  6.3 0.6 maximum_convert_fusion.small
  6.9 276.5 %layer.1 = (bf16[4,1024,2048]{2,1,0:T(8,128)(2,1)}, f32[1024,2048]{1,0:T(8,128)}, f32[1024,2048]{1,0:T(8,128)}, f32[1024,2048]{1,0:T(8,128)}, bf16[2,1024,1536]{...) custom-call(s32[4]{0:T(128)} %lengths.1, bf16[4,1024,2048]{2,1,0:T(8,128)(2,1)} %hidden.1, ...), custom_call_target="tpu_custom_call" | custom-call | flops 99999997952 | bytes 33554432 | tf_op jit(solution)/shard_map/layer/pallas_call | solution.py:752
  283.4 18.3 %finish.1 = (bf16[4,1024,2048]{2,1,0:T(8,128)(2,1)}, bf16[4,4,1024,128]{3,2,1,0:T(8,128)(2,1)}, bf16[4,4,1024,128]{3,2,1,0:T(8,128)(2,1)}) custom-call(s32[1]{0:T(128)} %bitcast.meta, bf16[4,1024,2048]{2,1,0:T(8,128)(2,1)} %get-tuple-element.6.in_ref, bf16[2,1024,1536]{2,1,0:T(8,128)(2,1)} %get-tuple-element.7.pk, f32[2,1024,1536]{2,1,0:T(8,128)} %get-tuple-element.8.qb), custom_call_target="tpu_custom_call" | custom-call | tf_op jit(solution)/shard_map/finish/pallas_call | solution.py:843
  (1 shorter events, 0.0 us)

commit v8 on v6

--- a/solution.py
+++ b/solution.py
@@ -69,10 +69,18 @@
     return functools.reduce(jnp.maximum, [values[:, n:n + lanes] for n in range(0, values.shape[1], lanes)])
 
 
+def ahead(heads, scores):
+    coming = scores(0)
+    for h in range(heads):
+        now = coming
+        if h + 1 < heads:
+            coming = scores(h + 1)
+        yield h, now
+
+
 def first_step(heads, scale, q_of, k_of, v_of, m_scr, l_scr, o_scr, mask):
-    for h in range(heads):
-        lanes = o_scr.shape[2]
-        scores = scores_of(q_of(h), k_of(h), scale, mask)
+    lanes = o_scr.shape[2]
+    for h, scores in ahead(heads, lambda h: scores_of(q_of(h), k_of(h), scale, mask)):
         peak = jnp.maximum(jnp.max(lane_max(scores, lanes), axis=1, keepdims=True), EMPTY)
         peak = jnp.broadcast_to(peak, m_scr.shape[1:])
         probs = jnp.exp2(scores - wide(peak, scores.shape[1]))
@@ -82,9 +90,8 @@
 
 
 def block_step(heads, scale, q_of, k_of, v_of, m_scr, l_scr, o_scr, mask):
-    for h in range(heads):
-        lanes = o_scr.shape[2]
-        scores = scores_of(q_of(h), k_of(h), scale, mask)
+    lanes = o_scr.shape[2]
+    for h, scores in ahead(heads, lambda h: scores_of(q_of(h), k_of(h), scale, mask)):
         m_old = m_scr[h]
         m_new = jnp.maximum(m_old, jnp.max(lane_max(scores, lanes), axis=1, keepdims=True))
         probs = jnp.exp2(scores - wide(m_new, scores.shape[1]))
@@ -241,9 +248,8 @@
             other = jnp.where(lane < half_rot, pltpu.roll(long, head_dim - half_rot, 1), pltpu.roll(long, half_rot, 1))
             return (long * cos_tab + other * sin_tab).astype(BF16)
 
-        for p in range(3):
-            part = slice(p * span, (p + 1) * span)
-            some = (jnp.dot(normed, up[p], preferred_element_type=F32) + small[:, part]).astype(BF16)
+        for p, product in ahead(3, lambda p: jnp.dot(normed, up[p], preferred_element_type=F32)):
+            some = (product + small[:, p * span:(p + 1) * span]).astype(BF16)
             for g in range(heads):
                 group = p * heads + g
                 values = some[:, g * head_dim:(g + 1) * head_dim]
@@ -253,6 +259,15 @@
                 staged(t, p)[:, g * head_dim:(g + 1) * head_dim] = values.astype(F32)
         start(sent_tile(n, t))
 
+    def arrived_tiles(n):
+        for t in range(TILES):
+            for copy in sent_tile(n, t):
+                copy.wait_recv()
+
+    def query_copies(n):
+        return [pltpu.make_async_copy(qb.at[n, :, pl.ds(3 * h * head_dim, head_dim)],
+                                      acc.at[:, pl.ds(q_at + h * head_dim, head_dim)], q_sem.at[h]) for h in range(heads)]
+
     per_slice = width // tile
 
     def far_place(t):
@@ -273,21 +288,17 @@
 
     @pl.loop(0, TILES)
     def _(t):
+        @pl.when(t == TILES // 2)
+        def _():
+            arrived_tiles(0)
+            start(query_copies(0))
+
         project(1, t, mine.at[t])
         mine_out(t).start()
 
     for f in range(SLICES):
         weight_copies(f)[0].start()
 
-
-    def got_queries(n):
-        for t in range(TILES):
-            for copy in sent_tile(n, t):
-                copy.wait_recv()
-        copies = [pltpu.make_async_copy(qb.at[n, :, pl.ds(3 * h * head_dim, head_dim)],
-                                        acc.at[:, pl.ds(q_at + h * head_dim, head_dim)], q_sem.at[h]) for h in range(heads)]
-        start(copies)
-        return copies
 
     def attend(row, slot, query, e):
         valid = jnp.clip(lengths[row] - j * slots, 0, slots)
@@ -345,8 +356,9 @@
     def y_stats(e):
         return to_y(st.at[1, :, rows_of(e, half)], sbox.at[2, :, rows_of(e, half)], yss_sem.at[e], ysr_sem.at[e])
 
-    wait(got_queries(0))
+    wait(query_copies(0))
     wait(cache_copies(corner, 0))
+    wait(cache_copies(across, 1))
 
     @pl.loop(0, HALVES)
     def _(e):
@@ -356,12 +368,12 @@
         far_stats(e).start()
         far_piece(e).start()
 
-    start(cache_copies(mate, 0))
-    near_queries = got_queries(1)
-    wait(cache_copies(across, 1))
-
-    @pl.loop(0, HALVES)
-    def _(e):
+        @pl.when(e == HALVES - 1)
+        def _():
+            start(cache_copies(mate, 0))
+            arrived_tiles(1)
+            start(query_copies(1))
+
         attend(across, 1, held_far, e)
         keep(e, kept_at, 1)
 
@@ -386,28 +398,34 @@
     for e in range(HALVES):
         far_stats(e).wait_send()
         far_piece(e).wait_send()
-    wait(near_queries)
+    wait(query_copies(1))
     wait(cache_copies(mate, 0))
-    wait(cache_copies(j, 1))
-    proj_copy.wait()
 
 
     def near(e, phase):
-        @pl.when(phase == 2)
+        @pl.when(phase == 4)
         def _():
             attend(mate, 0, taken, e)
             keep(e, sent_at, 2)
             near_stats(e).start()
             near_piece(e).start()
 
-        @pl.when(phase == 4)
+            @pl.when(e == 0)
+            def _():
+                wait(cache_copies(j, 1))
+
+        @pl.when(phase == 5)
         def _():
             attend(j, 1, held_mine, e)
 
-        @pl.when(phase == 5)
+        @pl.when(phase == 6)
         def _():
             attend_own(e)
             keep(e, own_at, 3)
+
+            @pl.when(e == 0)
+            def _():
+                proj_copy.wait()
 
     def block_copies(b):
         rows = rows_of(b, block)
@@ -429,10 +447,6 @@
     def begin(b):
         slot = lax.rem(b, 2)
         rows = rows_of(b, block)
-
-        @pl.when(b + 1 < BLOCKS)
-        def _():
-            fetch(b + 1)
 
         wait(block_copies(b))
 
@@ -632,6 +646,7 @@
         def _():
             b, f = lax.div(s, SLICES), lax.rem(s, SLICES)
             when(f == 0, begin, b)
+            when(jnp.logical_and(f == SLICES // 2, b + 1 < BLOCKS), fetch, b + 1)
             slice_of(b, f)
 
             def push(send):

time: 300 us -> 290 us (0.967)
  Pallas kernels: 293 us -> 283 us
    pallas_call x1, Pallas kernels: 275 us -> 265 us  [run_layer(): pl.pallas_call(functools.partial(layer_kernel, tp_size, heads), in_specs=...]
where the time goes in v8:
time: 290 us
  Pallas kernels  283 us (98%)
  other arithmetic  4.94 us (2%)
    pallas_call x1, Pallas kernels, run_layer(): pl.pallas_call(functools.partial(layer_kernel, tp_size, heads), in_specs=...  265 us
    pallas_call x1, Pallas kernels, finish(): pl.pallas_call(functools.partial(finish_kernel, heads), in_specs=[pl.Bloc...  18.3 us

profile of v8, /device:TPU:0, one launch (start us, length us, event | category | flops | bytes accessed | tf_op | source)
XLA Modules:
  0.0 289.9 jit_solution(173375318088804295)
XLA Ops:
  0.6 0.7 add_convert_fusion
  1.4 1.0 multiply_cosine_fusion
  2.4 1.1 pad_maximum_fusion.table
  3.5 0.7 convert_add_fusion
  4.2 0.7 convert_element_type.20
  4.9 0.7 convert_element_type.21
  5.6 0.6 broadcast_in_dim.26.small
  6.2 265.2 %layer.1 = (bf16[4,1024,2048]{2,1,0:T(8,128)(2,1)}, f32[1024,2048]{1,0:T(8,128)}, f32[1024,2048]{1,0:T(8,128)}, f32[1024,2048]{1,0:T(8,128)}, bf16[2,1024,1536]{...) custom-call(s32[4]{0:T(128)} %lengths.1, bf16[4,1024,2048]{2,1,0:T(8,128)(2,1)} %hidden.1, ...), custom_call_target="tpu_custom_call" | custom-call | flops 99999997952 | bytes 33554432 | tf_op jit(solution)/shard_map/layer/pallas_call | solution.py:698
  271.4 18.3 %finish.1 = (bf16[4,1024,2048]{2,1,0:T(8,128)(2,1)}, bf16[4,4,1024,128]{3,2,1,0:T(8,128)(2,1)}, bf16[4,4,1024,128]{3,2,1,0:T(8,128)(2,1)}) custom-call(s32[1]{0:T(128)} %bitcast.meta, bf16[4,1024,2048]{2,1,0:T(8,128)(2,1)} %get-tuple-element.6.in_ref, bf16[2,1024,1536]{2,1,0:T(8,128)(2,1)} %get-tuple-element.7.pk, f32[2,1024,1536]{2,1,0:T(8,128)} %get-tuple-element.8.qb), custom_call_target="tpu_custom_call" | custom-call | tf_op jit(solution)/shard_map/finish/pallas_call | solution.py:788
  (2 shorter events, 0.0 us)

commit v9 on v8

--- a/solution.py
+++ b/solution.py
@@ -41,15 +41,13 @@
     return (centered * lax.rsqrt(variance + EPSILON) * gain_vec + bias_vec).astype(BF16)
 
 
-def rope_table(lengths, chunk_len, head_dim):
+def rope_tables(lengths, chunk_len, head_dim):
     rot_dim = head_dim // ROTARY_SHARE
-    half_rot = rot_dim // 2
-    positions = lengths[:, None] + jnp.arange(chunk_len, dtype=jnp.int32)[None, :]
-    inv_freq = ROPE_BASE ** (-2.0 * jnp.arange(half_rot, dtype=F32) / rot_dim)
-    angles = positions.astype(F32)[:, None, :] * inv_freq[:, None]
-    cos_tab = jnp.cos(angles)
-    sin_tab = jnp.sin(angles)
-    return jnp.concatenate([cos_tab, cos_tab, -sin_tab, sin_tab], axis=1)
+    shape = (lengths.shape[0], rot_dim // 2, chunk_len)
+    positions = lengths[:, None, None] + lax.broadcasted_iota(jnp.int32, shape, 2)
+    inv_freq = ROPE_BASE ** (-2.0 * jnp.arange(rot_dim // 2, dtype=F32) / rot_dim)
+    angles = positions.astype(F32) * inv_freq[:, None]
+    return jnp.cos(angles), jnp.sin(angles)
 
 
 def wide(column, lanes):
@@ -113,7 +111,7 @@
     return jnp.concatenate(parts + [jnp.zeros((head_dim - count, parts[0].shape[1]), F32)], axis=0).T
 
 
-def layer_kernel(tp_size, heads, lengths, hidden, table, k_cache, v_cache, w_qkv, w_up, w_down, w_out,
+def layer_kernel(tp_size, heads, lengths, hidden, cos_all, sin_all, k_cache, v_cache, w_qkv, w_up, w_down, w_out,
                  gain1, bias1, gain2, bias2, small,
                  out_ref, y_box, core_box, last_box, pk, qb, ob,
                  acc, from_left, from_right, up, down, proj, mine, x_big, tab_buf, kv, ob_far, m_scr, l_scr, o_scr, st, sbox,
@@ -175,7 +173,8 @@
             copy.wait()
 
     qkv_copies = [pltpu.make_async_copy(w_qkv.at[:, pl.ds(s * width, width)], up.at[s], up_sem.at[s]) for s in range(3)]
-    tab_copies = [pltpu.make_async_copy(table.at[row], tab_buf.at[n], tab_sem.at[n]) for n, row in enumerate((across, j))]
+    tab_copies = [pltpu.make_async_copy(ref.at[row], tab_buf.at[n, p], tab_sem.at[n, p])
+                  for n, row in enumerate((across, j)) for p, ref in enumerate((cos_all, sin_all))]
     proj_copy = pltpu.make_async_copy(w_out, proj, proj_sem)
     big_x(0).start()
     start(qkv_copies)
@@ -237,8 +236,8 @@
         if n == 1:
             sent_off(0, t)
         normed = layer_norm(x_big[lax.rem(i, 2)], gain1[...], bias1[...])
-        tab = tab_buf[n, :, rows_of(t, tile)]
-        tab = jnp.concatenate([tab] * (head_dim // tab.shape[0]), axis=0).T
+        cos_part, sin_part = tab_buf[n, 0, :, rows_of(t, tile)], tab_buf[n, 1, :, rows_of(t, tile)]
+        tab = jnp.concatenate([cos_part, cos_part, -sin_part, sin_part] * (head_dim // (4 * half_rot)), axis=0).T
         lane = lax.broadcasted_iota(jnp.int32, tab.shape, 1)
         cos_tab = jnp.where(lane < rot_dim, tab, 1.0)
         sin_tab = jnp.where(lane < rot_dim, pltpu.roll(tab, head_dim - rot_dim, 1), 0.0)
@@ -403,7 +402,7 @@
 
 
     def near(e, phase):
-        @pl.when(phase == 4)
+        @pl.when(phase == 5)
         def _():
             attend(mate, 0, taken, e)
             keep(e, sent_at, 2)
@@ -414,11 +413,11 @@
             def _():
                 wait(cache_copies(j, 1))
 
-        @pl.when(phase == 5)
+        @pl.when(phase == 6)
         def _():
             attend(j, 1, held_mine, e)
 
-        @pl.when(phase == 6)
+        @pl.when(phase == 7)
         def _():
             attend_own(e)
             keep(e, own_at, 3)
@@ -638,7 +637,7 @@
         def _():
             near(lax.div(step, waited), lax.rem(step, waited))
 
-        @pl.when(step == waited - 1)
+        @pl.when(step == waited - 2)
         def _():
             fetch(0)
 
@@ -646,7 +645,7 @@
         def _():
             b, f = lax.div(s, SLICES), lax.rem(s, SLICES)
             when(f == 0, begin, b)
-            when(jnp.logical_and(f == SLICES // 2, b + 1 < BLOCKS), fetch, b + 1)
+            when(jnp.logical_and(f == SLICES - 1, b + 1 < BLOCKS), fetch, b + 1)
             slice_of(b, f)
 
             def push(send):
@@ -681,7 +680,7 @@
             pltpu.make_async_copy(stage.at[stream, slot], at(out_ref.at[0], 0), stage_sem.at[stream, slot]).wait()
 
 
-def run_layer(lengths, hidden_in, table, k_block, v_block, w_qkv, w_up, w_down, w_out, norms, small, tp_size):
+def run_layer(lengths, hidden_in, tables, k_block, v_block, w_qkv, w_up, w_down, w_out, norms, small, tp_size):
     num_rows, chunk_len, d_model = hidden_in.shape
     heads, slots, head_dim = k_block.shape[1:]
     span = heads * head_dim
@@ -697,7 +696,7 @@
     vmem = pl.BlockSpec(memory_space=pltpu.VMEM)
     out, _, _, _, pk, qb, _ = pl.pallas_call(
         functools.partial(layer_kernel, tp_size, heads),
-        in_specs=[pl.BlockSpec(memory_space=pltpu.SMEM)] + [hbm] * 8 + [vmem] * 5,
+        in_specs=[pl.BlockSpec(memory_space=pltpu.SMEM)] + [hbm] * 9 + [vmem] * 5,
         out_specs=[hbm] * 7,
         out_shape=[
             jax.ShapeDtypeStruct((num_rows, chunk_len, d_model), BF16), box, box, box,
@@ -712,7 +711,7 @@
             pltpu.VMEM((span, d_model), BF16),
             pltpu.VMEM((TILES, tile, 3 * span), BF16),
             pltpu.VMEM((2, tile, d_model), BF16),
-            pltpu.VMEM((2,) + table.shape[1:], F32),
+            pltpu.VMEM((2, 2) + tables[0].shape[1:], F32),
             pltpu.VMEM((2, 2, heads, slots, head_dim), BF16),
             pltpu.VMEM((chunk_len, span), F32),
             pltpu.VMEM((heads, half, head_dim), F32),
@@ -723,7 +722,7 @@
             pltpu.VMEM((4, STAGES, tokens, d_model), BF16),
             pltpu.VMEM((3, STAGES, tokens, d_model), F32),
         ]
-        + [dma((SLICES,)), dma((SLICES,)), dma, dma((2,)), dma((2,)), dma((TILES,)), dma((TILES,)), dma((2, 2)), dma((heads,)),
+        + [dma((SLICES,)), dma((SLICES,)), dma, dma((2,)), dma((2, 2)), dma((TILES,)), dma((TILES,)), dma((2, 2)), dma((heads,)),
            dma((2,)), dma((2, 2))]
         + [dma((2, TILES, 3))] * 2
         + [dma((HALVES,))] * 12
@@ -732,7 +731,7 @@
         compiler_params=pltpu.CompilerParams(collective_id=0, has_side_effects=True, vmem_limit_bytes=LAYER_LIMIT),
         cost_estimate=pl.CostEstimate(flops=100_000_000_000, bytes_accessed=chunk_len * d_model * 16, transcendentals=0),
         name="layer",
-    )(lengths, hidden_in, table, k_block, v_block, w_qkv, w_up, w_down, w_out, *norms, small[None])
+    )(lengths, hidden_in, *tables, k_block, v_block, w_qkv, w_up, w_down, w_out, *norms, small[None])
     return out, pk, qb
 
 
@@ -807,10 +806,12 @@
     def local_layer(hidden_in, lengths, k_block, v_block, ln1_gain, ln1_bias, ln2_gain, ln2_bias, w_qkv, b_qkv, w_out, b_out, w_up, b_up, w_down, b_down):
         num_rows, chunk_len, d_model = hidden_in.shape
         heads, block_len, head_dim = k_block.shape[1:]
-        table = rope_table(lengths, chunk_len, head_dim)
+        tables = rope_tables(lengths, chunk_len, head_dim)
         norms = [p[None] for p in (ln1_gain, ln1_bias, ln2_gain, ln2_bias)]
-        small = jnp.concatenate([b_qkv.astype(F32), b_up.astype(F32), b_out.astype(F32) + b_down.astype(F32)])
-        out, pk, qb = run_layer(lengths, hidden_in, table, k_block, v_block, w_qkv, w_up, w_down, w_out, norms, small, tp_size)
+        parts = [(b_qkv, 0), (b_up, b_qkv.shape[0]), (b_out, b_qkv.shape[0] + b_up.shape[0]), (b_down, b_qkv.shape[0] + b_up.shape[0])]
+        total = b_qkv.shape[0] + b_up.shape[0] + d_model
+        small = functools.reduce(jnp.add, [jnp.pad(p.astype(F32), (at, total - at - p.shape[0])) for p, at in parts])
+        out, pk, qb = run_layer(lengths, hidden_in, tables, k_block, v_block, w_qkv, w_up, w_down, w_out, norms, small, tp_size)
         return tuple(finish(lax.axis_index("cp")[None], out, pk, qb, heads, head_dim))
 
     return jax.shard_map(local_layer, mesh=mesh, in_specs=in_specs, out_specs=out_specs, check_vma=False)

time: 290 us -> 289 us (level)
  no operation moved by 1% of the time
where the time goes in v9:
time: 289 us; the launch traced here: 288 us
  Pallas kernels  284 us (98%)
  other arithmetic  3.23 us (1%)
    pallas_call x1, Pallas kernels, run_layer(): pl.pallas_call(functools.partial(layer_kernel, tp_size, heads), in_specs=...  265 us
    pallas_call x1, Pallas kernels, finish(): pl.pallas_call(functools.partial(finish_kernel, heads), in_specs=[pl.Bloc...  18.3 us

profile of v9, /device:TPU:0, one launch (start us, length us, event | category | flops | bytes accessed | tf_op | source)
XLA Modules:
  0.0 288.2 jit_solution(7842680196128965905)
XLA Ops:
  0.6 2.5 fusion
  3.1 0.7 convert_add_fusion
  3.9 0.6 broadcast_in_dim.24.small
  4.5 265.2 %layer.1 = (bf16[4,1024,2048]{2,1,0:T(8,128)(2,1)}, f32[1024,2048]{1,0:T(8,128)}, f32[1024,2048]{1,0:T(8,128)}, f32[1024,2048]{1,0:T(8,128)}, bf16[2,1024,1536]{...) custom-call(s32[4]{0:T(128)} %lengths.1, bf16[4,1024,2048]{2,1,0:T(8,128)(2,1)} %hidden.1, ...), custom_call_target="tpu_custom_call" | custom-call | flops 99999997952 | bytes 33554432 | tf_op jit(solution)/shard_map/layer/pallas_call | solution.py:697
  269.7 18.3 %finish.1 = (bf16[4,1024,2048]{2,1,0:T(8,128)(2,1)}, bf16[4,4,1024,128]{3,2,1,0:T(8,128)(2,1)}, bf16[4,4,1024,128]{3,2,1,0:T(8,128)(2,1)}) custom-call(s32[1]{0:T(128)} %bitcast.meta, bf16[4,1024,2048]{2,1,0:T(8,128)(2,1)} %get-tuple-element.6.in_ref, bf16[2,1024,1536]{2,1,0:T(8,128)(2,1)} %get-tuple-element.7.pk, f32[2,1024,1536]{2,1,0:T(8,128)} %get-tuple-element.8.qb), custom_call_target="tpu_custom_call" | custom-call | tf_op jit(solution)/shard_map/finish/pallas_call | solution.py:787
  (1 shorter events, 0.0 us)

commit v10 on v9

--- a/solution.py
+++ b/solution.py
@@ -43,10 +43,9 @@
 
 def rope_tables(lengths, chunk_len, head_dim):
     rot_dim = head_dim // ROTARY_SHARE
-    shape = (lengths.shape[0], rot_dim // 2, chunk_len)
-    positions = lengths[:, None, None] + lax.broadcasted_iota(jnp.int32, shape, 2)
+    positions = lengths[:, None] + jnp.arange(chunk_len, dtype=jnp.int32)[None, :]
     inv_freq = ROPE_BASE ** (-2.0 * jnp.arange(rot_dim // 2, dtype=F32) / rot_dim)
-    angles = positions.astype(F32) * inv_freq[:, None]
+    angles = positions.astype(F32)[:, None, :] * inv_freq[:, None]
     return jnp.cos(angles), jnp.sin(angles)
 
 
@@ -648,13 +647,13 @@
             when(jnp.logical_and(f == SLICES - 1, b + 1 < BLOCKS), fetch, b + 1)
             slice_of(b, f)
 
-            def push(send):
+            def push(send, swapped):
                 @pl.loop(0, 2 * per_block)
                 def _(n):
-                    send(acc, b * 2 * per_block + n)
-
-            when(jnp.logical_and(f == SLICES - 1, z == 0), push, send_right)
-            when(jnp.logical_and(f == SLICES - 1, z == last), push, send_left)
+                    send(acc, b * 2 * per_block + (n + 1 - 2 * lax.rem(n, 2) if swapped else n))
+
+            when(jnp.logical_and(f == SLICES - 1, z == 0), push, send_right, True)
+            when(jnp.logical_and(f == SLICES - 1, z == last), push, send_left, False)
 
         i = s - lead
         when(z == 0, end, i, True)
@@ -731,7 +730,7 @@
         compiler_params=pltpu.CompilerParams(collective_id=0, has_side_effects=True, vmem_limit_bytes=LAYER_LIMIT),
         cost_estimate=pl.CostEstimate(flops=100_000_000_000, bytes_accessed=chunk_len * d_model * 16, transcendentals=0),
         name="layer",
-    )(lengths, hidden_in, *tables, k_block, v_block, w_qkv, w_up, w_down, w_out, *norms, small[None])
+    )(lengths, hidden_in, *tables, k_block, v_block, w_qkv, w_up, w_down, w_out, *norms, small)
     return out, pk, qb
 
 
@@ -810,7 +809,7 @@
         norms = [p[None] for p in (ln1_gain, ln1_bias, ln2_gain, ln2_bias)]
         parts = [(b_qkv, 0), (b_up, b_qkv.shape[0]), (b_out, b_qkv.shape[0] + b_up.shape[0]), (b_down, b_qkv.shape[0] + b_up.shape[0])]
         total = b_qkv.shape[0] + b_up.shape[0] + d_model
-        small = functools.reduce(jnp.add, [jnp.pad(p.astype(F32), (at, total - at - p.shape[0])) for p, at in parts])
+        small = functools.reduce(jnp.add, [jnp.pad(p[None].astype(F32), ((0, 0), (at, total - at - p.shape[0]))) for p, at in parts])
         out, pk, qb = run_layer(lengths, hidden_in, tables, k_block, v_block, w_qkv, w_up, w_down, w_out, norms, small, tp_size)
         return tuple(finish(lax.axis_index("cp")[None], out, pk, qb, heads, head_dim))
 

time: 289 us -> 291 us (level)
  no operation moved by 1% of the time
where the time goes in v10:
time: 291 us; the launch traced here: 290 us
  Pallas kernels  283 us (97%)
  other arithmetic  3.18 us (1%)
    pallas_call x1, Pallas kernels, run_layer(): pl.pallas_call(functools.partial(layer_kernel, tp_size, heads), in_specs=...  265 us
    pallas_call x1, Pallas kernels, finish(): pl.pallas_call(functools.partial(finish_kernel, heads), in_specs=[pl.Bloc...  18.3 us

profile of v10, /device:TPU:0, one launch (start us, length us, event | category | flops | bytes accessed | tf_op | source)
XLA Modules:
  0.0 290.2 jit_solution(11913587101417213683)
XLA Ops:
  0.6 0.7 add_convert_fusion
  1.4 1.8 multiply_sine_fusion
  3.2 0.7 convert_element_type.32
  3.9 0.7 convert_element_type.33
  4.6 0.7 convert_element_type.34
  5.2 0.7 convert_element_type.31
  5.9 0.6 convert_add_fusion.small
  6.6 265.2 %layer.1 = (bf16[4,1024,2048]{2,1,0:T(8,128)(2,1)}, f32[1024,2048]{1,0:T(8,128)}, f32[1024,2048]{1,0:T(8,128)}, f32[1024,2048]{1,0:T(8,128)}, bf16[2,1024,1536]{...) custom-call(s32[4]{0:T(128)} %lengths.1, bf16[4,1024,2048]{2,1,0:T(8,128)(2,1)} %hidden.1, ...), custom_call_target="tpu_custom_call" | custom-call | flops 99999997952 | bytes 33554432 | tf_op jit(solution)/shard_map/layer/pallas_call | solution.py:696
  271.8 18.3 %finish.1 = (bf16[4,1024,2048]{2,1,0:T(8,128)(2,1)}, bf16[4,4,1024,128]{3,2,1,0:T(8,128)(2,1)}, bf16[4,4,1024,128]{3,2,1,0:T(8,128)(2,1)}) custom-call(s32[1]{0:T(128)} %bitcast.meta, bf16[4,1024,2048]{2,1,0:T(8,128)(2,1)} %get-tuple-element.6.in_ref, bf16[2,1024,1536]{2,1,0:T(8,128)(2,1)} %get-tuple-element.7.pk, f32[2,1024,1536]{2,1,0:T(8,128)} %get-tuple-element.8.qb), custom_call_target="tpu_custom_call" | custom-call | tf_op jit(solution)/shard_map/finish/pallas_call | solution.py:786
  (1 shorter events, 0.0 us)

commit v11 on v9

--- a/solution.py
+++ b/solution.py
@@ -214,11 +214,11 @@
             src_ref=src, dst_ref=dst, send_sem=send, recv_sem=arrive, device_id={"cp": across}, device_id_type=MESH)
 
 
-    def staged(t, part):
-        return acc.at[rows_of(t, tile), pl.ds(part * span, span)]
+    def staged(n, t, part):
+        return acc.at[rows_of(t, tile), pl.ds((q_at if n == 1 and part == 2 else part * span), span)]
 
     def sent_tile(n, t):
-        return [to_core(staged(t, p), qb.at[n, rows_of(t, tile), pl.ds(p * span, span)], qs_sem.at[n, t, p], qr_sem.at[n, t, p])
+        return [to_core(staged(n, t, p), qb.at[n, rows_of(t, tile), pl.ds(p * span, span)], qs_sem.at[n, t, p], qr_sem.at[n, t, p])
                 for p in range(3)]
 
     def sent_off(n, t):
@@ -233,8 +233,6 @@
             big_x(i + 1).start()
 
         big_x(i).wait()
-        if n == 1:
-            sent_off(0, t)
         normed = layer_norm(x_big[lax.rem(i, 2)], gain1[...], bias1[...])
         cos_part, sin_part = tab_buf[n, 0, :, rows_of(t, tile)], tab_buf[n, 1, :, rows_of(t, tile)]
         tab = jnp.concatenate([cos_part, cos_part, -sin_part, sin_part] * (head_dim // (4 * half_rot)), axis=0).T
@@ -255,17 +253,18 @@
                 if group % 3 < 2:
                     values = rotate(values)
                 place[:, group * head_dim:(group + 1) * head_dim] = values
-                staged(t, p)[:, g * head_dim:(g + 1) * head_dim] = values.astype(F32)
+                staged(n, t, p)[:, g * head_dim:(g + 1) * head_dim] = values.astype(F32)
         start(sent_tile(n, t))
 
-    def arrived_tiles(n):
-        for t in range(TILES):
-            for copy in sent_tile(n, t):
-                copy.wait_recv()
-
-    def query_copies(n):
-        return [pltpu.make_async_copy(qb.at[n, :, pl.ds(3 * h * head_dim, head_dim)],
-                                      acc.at[:, pl.ds(q_at + h * head_dim, head_dim)], q_sem.at[h]) for h in range(heads)]
+    def query_copies(n, t):
+        rows = rows_of(t, tile)
+        return [pltpu.make_async_copy(qb.at[n, rows, pl.ds(3 * h * head_dim, head_dim)],
+                                      acc.at[rows, pl.ds(q_at + h * head_dim, head_dim)], q_sem.at[h]) for h in range(heads)]
+
+    def fetch_queries(n, t):
+        for copy in sent_tile(n, t):
+            copy.wait_recv()
+        start(query_copies(n, t))
 
     per_slice = width // tile
 
@@ -277,26 +276,6 @@
 
     wait(qkv_copies)
     wait(tab_copies)
-
-    @pl.loop(0, TILES)
-    def _(t):
-        project(0, t, far_place(t))
-
-    pack_copies = [pltpu.make_async_copy(far_place(t), pk.at[0, rows_of(t, tile), :], pk_sem.at[t]) for t in range(TILES)]
-    start(pack_copies)
-
-    @pl.loop(0, TILES)
-    def _(t):
-        @pl.when(t == TILES // 2)
-        def _():
-            arrived_tiles(0)
-            start(query_copies(0))
-
-        project(1, t, mine.at[t])
-        mine_out(t).start()
-
-    for f in range(SLICES):
-        weight_copies(f)[0].start()
 
 
     def attend(row, slot, query, e):
@@ -355,27 +334,18 @@
     def y_stats(e):
         return to_y(st.at[1, :, rows_of(e, half)], sbox.at[2, :, rows_of(e, half)], yss_sem.at[e], ysr_sem.at[e])
 
-    wait(query_copies(0))
-    wait(cache_copies(corner, 0))
-    wait(cache_copies(across, 1))
-
-    @pl.loop(0, HALVES)
-    def _(e):
-        sent_off(1, e)
+    def far_attend(e):
+        fetch_queries(0, e)
+        sent_off(0, e)
+        attend(across, 1, held_far, e)
+        keep(e, kept_at, 1)
+        wait(query_copies(0, e))
         attend(corner, 0, taken, e)
         keep(e, sent_at, 0)
         far_stats(e).start()
         far_piece(e).start()
 
-        @pl.when(e == HALVES - 1)
-        def _():
-            start(cache_copies(mate, 0))
-            arrived_tiles(1)
-            start(query_copies(1))
-
-        attend(across, 1, held_far, e)
-        keep(e, kept_at, 1)
-
+    def far_join(e):
         far_stats(e).wait_recv()
         far_piece(e).wait_recv()
         rows = rows_of(e, half)
@@ -390,20 +360,58 @@
         y_stats(e).start()
         y_piece(e).start()
 
+    @pl.loop(0, TILES + 2)
+    def _(t):
+        @pl.when(t < TILES)
+        def _():
+            project(0, t, far_place(t))
+
+        @pl.when(t == 1)
+        def _():
+            wait(cache_copies(corner, 0))
+            wait(cache_copies(across, 1))
+
+        @pl.when(t >= 2)
+        def _():
+            far_join(t - 2)
+
+        @pl.when(jnp.logical_and(t >= 1, t <= TILES))
+        def _():
+            far_attend(t - 1)
+
+    start(cache_copies(mate, 0))
     start(cache_copies(j, 1))
-    wait(pack_copies)
-    for f in range(SLICES):
-        weight_copies(f)[1].start()
+    pack_copies = [pltpu.make_async_copy(far_place(t), pk.at[0, rows_of(t, tile), :], pk_sem.at[t]) for t in range(TILES)]
+    start(pack_copies)
     for e in range(HALVES):
         far_stats(e).wait_send()
         far_piece(e).wait_send()
-    wait(query_copies(1))
+
+    @pl.loop(0, TILES)
+    def _(t):
+        @pl.when(t == 2)
+        def _():
+            sent_off(1, 0)
+            fetch_queries(1, 0)
+
+        project(1, t, mine.at[t])
+        mine_out(t).start()
+
+    wait(pack_copies)
+    for f in range(SLICES):
+        start(weight_copies(f))
     wait(cache_copies(mate, 0))
 
 
     def near(e, phase):
+        @pl.when(jnp.logical_and(phase == 4, e > 0))
+        def _():
+            sent_off(1, e)
+            fetch_queries(1, e)
+
         @pl.when(phase == 5)
         def _():
+            wait(query_copies(1, e))
             attend(mate, 0, taken, e)
             keep(e, sent_at, 2)
             near_stats(e).start()
@@ -648,13 +656,13 @@
             when(jnp.logical_and(f == SLICES - 1, b + 1 < BLOCKS), fetch, b + 1)
             slice_of(b, f)
 
-            def push(send):
+            def push(send, swapped):
                 @pl.loop(0, 2 * per_block)
                 def _(n):
-                    send(acc, b * 2 * per_block + n)
-
-            when(jnp.logical_and(f == SLICES - 1, z == 0), push, send_right)
-            when(jnp.logical_and(f == SLICES - 1, z == last), push, send_left)
+                    send(acc, b * 2 * per_block + (n + 1 - 2 * lax.rem(n, 2) if swapped else n))
+
+            when(jnp.logical_and(f == SLICES - 1, z == 0), push, send_right, True)
+            when(jnp.logical_and(f == SLICES - 1, z == last), push, send_left, False)
 
         i = s - lead
         when(z == 0, end, i, True)

time: 289 us -> 290 us (level)
  no operation moved by 1% of the time
where the time goes in v11:
time: 290 us; the launch traced here: 289 us
  Pallas kernels  285 us (98%)
  other arithmetic  3.23 us (1%)
    pallas_call x1, Pallas kernels, run_layer(): pl.pallas_call(functools.partial(layer_kernel, tp_size, heads), in_specs=...  266 us
    pallas_call x1, Pallas kernels, finish(): pl.pallas_call(functools.partial(finish_kernel, heads), in_specs=[pl.Bloc...  18.3 us

profile of v11, /device:TPU:0, one launch (start us, length us, event | category | flops | bytes accessed | tf_op | source)
XLA Modules:
  0.0 289.3 jit_solution(1065695533460649082)
XLA Ops:
  0.6 2.5 fusion
  3.1 0.7 convert_add_fusion
  3.9 0.6 broadcast_in_dim.24.small
  4.5 266.3 %layer.1 = (bf16[4,1024,2048]{2,1,0:T(8,128)(2,1)}, f32[1024,2048]{1,0:T(8,128)}, f32[1024,2048]{1,0:T(8,128)}, f32[1024,2048]{1,0:T(8,128)}, bf16[2,1024,1536]{...) custom-call(s32[4]{0:T(128)} %lengths.1, bf16[4,1024,2048]{2,1,0:T(8,128)(2,1)} %hidden.1, ...), custom_call_target="tpu_custom_call" | custom-call | flops 99999997952 | bytes 33554432 | tf_op jit(solution)/shard_map/layer/pallas_call | solution.py:705
  270.8 18.3 %finish.1 = (bf16[4,1024,2048]{2,1,0:T(8,128)(2,1)}, bf16[4,4,1024,128]{3,2,1,0:T(8,128)(2,1)}, bf16[4,4,1024,128]{3,2,1,0:T(8,128)(2,1)}) custom-call(s32[1]{0:T(128)} %bitcast.meta, bf16[4,1024,2048]{2,1,0:T(8,128)(2,1)} %get-tuple-element.6.in_ref, bf16[2,1024,1536]{2,1,0:T(8,128)(2,1)} %get-tuple-element.7.pk, f32[2,1024,1536]{2,1,0:T(8,128)} %get-tuple-element.8.qb), custom_call_target="tpu_custom_call" | custom-call | tf_op jit(solution)/shard_map/finish/pallas_call | solution.py:795
  (1 shorter events, 0.0 us)

commit v12 on v11

--- a/solution.py
+++ b/solution.py
@@ -28,9 +28,9 @@
 LAG_START = 2
 LAG_AHEAD = 1
 LAG_BACK = 1
-LAG_CORE = 2
-LAG_Y = 5
-LAG_LAST = 6
+LAG_CORE = 3
+LAG_Y = 9
+LAG_LAST = 11
 
 
 def layer_norm(values_in, gain_vec, bias_vec):

time: 290 us -> 295 us (1.017)
  Pallas kernels: 285 us -> 290 us
    pallas_call x1, Pallas kernels: 266 us -> 272 us  [run_layer(): pl.pallas_call(functools.partial(layer_kernel, tp_size, heads), in_specs=...]
where the time goes in v12:
time: 295 us
  Pallas kernels  290 us (98%)
  other arithmetic  3.23 us (1%)
    pallas_call x1, Pallas kernels, run_layer(): pl.pallas_call(functools.partial(layer_kernel, tp_size, heads), in_specs=...  272 us
    pallas_call x1, Pallas kernels, finish(): pl.pallas_call(functools.partial(finish_kernel, heads), in_specs=[pl.Bloc...  18.3 us

profile of v12, /device:TPU:0, one launch (start us, length us, event | category | flops | bytes accessed | tf_op | source)
XLA Modules:
  0.0 294.6 jit_solution(12723243374785056177)
XLA Ops:
  0.6 2.5 fusion
  3.1 0.7 convert_add_fusion
  3.9 0.6 broadcast_in_dim.24.small
  4.5 271.6 %layer.1 = (bf16[4,1024,2048]{2,1,0:T(8,128)(2,1)}, f32[1024,2048]{1,0:T(8,128)}, f32[1024,2048]{1,0:T(8,128)}, f32[1024,2048]{1,0:T(8,128)}, bf16[2,1024,1536]{...) custom-call(s32[4]{0:T(128)} %lengths.1, bf16[4,1024,2048]{2,1,0:T(8,128)(2,1)} %hidden.1, ...), custom_call_target="tpu_custom_call" | custom-call | flops 99999997952 | bytes 33554432 | tf_op jit(solution)/shard_map/layer/pallas_call | solution.py:705
  276.1 18.3 %finish.1 = (bf16[4,1024,2048]{2,1,0:T(8,128)(2,1)}, bf16[4,4,1024,128]{3,2,1,0:T(8,128)(2,1)}, bf16[4,4,1024,128]{3,2,1,0:T(8,128)(2,1)}) custom-call(s32[1]{0:T(128)} %bitcast.meta, bf16[4,1024,2048]{2,1,0:T(8,128)(2,1)} %get-tuple-element.6.in_ref, bf16[2,1024,1536]{2,1,0:T(8,128)(2,1)} %get-tuple-element.7.pk, f32[2,1024,1536]{2,1,0:T(8,128)} %get-tuple-element.8.qb), custom_call_target="tpu_custom_call" | custom-call | tf_op jit(solution)/shard_map/finish/pallas_call | solution.py:795
  (1 shorter events, 0.0 us)
